TPU v7x, 256 devices: a whole 4x4x8 slice. The times are simulated.
256 devices in a mesh: dom: 64 (over y, z, core), grp: 4 (over x).
Axes of the slice: x: 4, y: 4, z: 8, core: 2. Of those that a mesh axis runs over, the one named last changes fastest.
Arguments:
- nodes: bfloat16 [4, 32768, 128], P('grp', 'dom'), may hold values from -6 to 6
- edges: bfloat16 [4, 256, 128, 128], P('grp', 'dom'), may hold values from -6 to 6
- senders: int32 [4, 256, 128], P('grp', 'dom'), may hold values from 0 to 767
- receivers: int32 [4, 256, 128], P('grp', 'dom'), may hold values from 0 to 511
- block_count: int32 [4, 64], P('grp', 'dom'), may hold values from 1 to 4
- send_rows: int32 [4, 64, 2, 128], P('grp', 'dom'), may hold values from 0 to 511
- node_cot: bfloat16 [4, 32768, 128], P('grp', 'dom'), may hold values from -6 to 6
- edge_cot: bfloat16 [4, 256, 128, 128], P('grp', 'dom'), may hold values from -6 to 6
- edge_w1: bfloat16 [384, 128], replicated, may hold values from -0.3125 to 0.3125
- edge_b1: float32 [128], replicated, may hold values from -3 to 3
- edge_w2: bfloat16 [128, 128], replicated, may hold values from -0.5 to 0.5
- edge_b2: float32 [128], replicated, may hold values from -3 to 3
- edge_gain: float32 [128], replicated, may hold values from 0.5 to 1.5
- edge_shift: float32 [128], replicated, may hold values from -3 to 3
- node_w1: bfloat16 [256, 128], replicated, may hold values from -0.375 to 0.375
- node_b1: float32 [128], replicated, may hold values from -3 to 3
- node_w2: bfloat16 [128, 128], replicated, may hold values from -0.5 to 0.5
- node_b2: float32 [128], replicated, may hold values from -3 to 3
- node_gain: float32 [128], replicated, may hold values from 0.5 to 1.5
- node_shift: float32 [128], replicated, may hold values from -3 to 3
Outputs:
- node_out: bfloat16 [4, 32768, 128], P('grp', 'dom')
- edge_out: bfloat16 [4, 256, 128, 128], P('grp', 'dom')
- grad_node: bfloat16 [4, 32768, 128], P('grp', 'dom')
- grad_edge: bfloat16 [4, 256, 128, 128], P('grp', 'dom')
- weight_grads: float32 [115712], replicated
Inputs may be any that keep to these rules, and one draw needn't show every extreme that they name: `senders`: rows below 512 are the device's own nodes; row 512 + k holds the k-th row sent by the lower neighbouring partition, row 640 + k the k-th row sent by the upper one. `receivers`: receivers are own nodes of the device that holds the edge. `block_count`: A device's live blocks are its first ones; the rest are padding. send_rows[g, d, 0, :] are own rows of device d sent to device d - 1 of group g, send_rows[g, d, 1, :] those sent to device d + 1; they may repeat; lists toward no device are unused.
All inputs are finite; a program needn't handle non-finite values.
Results may differ from a plain program's by a relative error of at most 0.0054.
Values may be sent and summed in bfloat16 or wider, within the bound.
No kernel may reach another device: no remote copies, remote signals or barrier semaphores. Data moves between devices by JAX's collectives and lax.ppermute only.
A program may use at most 64 MiB of HBM per device.

v0:
```python
import math

import jax
import jax.numpy as jnp
from jax import lax
from jax.sharding import Mesh
from jax.sharding import PartitionSpec as P

DOM = ("dom_0", "dom_1", "dom_2")


EPSILON = 1e-05


def extended(value, sides, width):
    for axis, dim in sides:
        size, length = (lax.axis_size(axis), value.shape[dim])
        up = [(i, (i + 1) % size) for i in range(size - 1)]
        down = [(j, i) for i, j in up]
        last = lax.slice_in_dim(value, length - width, length, axis=dim)
        leading = lax.slice_in_dim(value, 0, width, axis=dim)
        before = lax.ppermute(last, axis, up)
        after = lax.ppermute(leading, axis, down)
        value = jnp.concatenate([before, value, after], axis=dim)
    return value


def padded_to(lines, length):
    spare = -len(lines) % length
    return jnp.pad(lines, [(0, spare)] + [(0, 0)] * (lines.ndim - 1))


def copy_for_each(value, axis):
    copies = jnp.broadcast_to(value, (lax.axis_size(axis), *value.shape))
    return lax.all_to_all(copies, axis, split_axis=0, concat_axis=0, tiled=True)


def in_order(tiles, dim):
    tiles = jnp.moveaxis(tiles, 0, dim)
    shape = tiles.shape
    return tiles.reshape(*shape[:dim], shape[dim] * shape[dim + 1], *shape[dim + 2 :])


def gather_axes(value, axes, dim):
    far, near = axes
    leading = copy_for_each(value, far)
    tiles = jnp.swapaxes(copy_for_each(leading, near), 0, 1)
    return in_order(tiles.reshape(-1, *value.shape), dim)


def cut_along(value, dim, length):
    shape = value.shape
    tiles = value.reshape(*shape[:dim], length, shape[dim] // length, *shape[dim + 1 :])
    return jnp.moveaxis(tiles, dim, 0)


def sent_and_summed(value, axis, dim):
    length = lax.axis_size(axis)
    tiles = lax.all_to_all(cut_along(value, dim, length), axis, 0, 0, tiled=True)
    return jnp.sum(tiles, axis=0)


def sum_by_axis(value, axes, dim):
    far, near = axes
    tiles = cut_along(value, dim, lax.axis_size(far))
    nearer = sent_and_summed(tiles, near, dim + 1)
    arrived = lax.all_to_all(nearer, far, split_axis=0, concat_axis=0, tiled=True)
    return arrived.sum(axis=0)


def nested_sum(value, axes):
    lines = value.reshape(-1)
    padded = padded_to(lines, lax.axis_size(axes[0]) * lax.axis_size(axes[1]))
    whole = gather_axes(sum_by_axis(padded, axes, 0), axes, 0)
    return lax.slice_in_dim(whole, 0, len(lines)).reshape(value.shape)


def norm_forward(pre_norm, norm_gain, norm_shift):
    average = jnp.mean(pre_norm, axis=-1, keepdims=True)
    centred = pre_norm - average
    variance = jnp.mean(centred * centred, axis=-1, keepdims=True)
    inverse = lax.rsqrt(variance + EPSILON)
    normed = centred * inverse
    return (normed * norm_gain + norm_shift, normed, inverse)


def norm_backward(grad_out, normed, inverse, norm_gain):
    scaled = grad_out * norm_gain
    return inverse * (
        scaled
        - jnp.mean(scaled, axis=-1, keepdims=True)
        - normed * jnp.mean(scaled * normed, axis=-1, keepdims=True)
    )


def silu_slope(pre_act):
    sigmoid = jax.nn.sigmoid(pre_act)
    return sigmoid * (1.0 + pre_act * (1.0 - sigmoid))


def row_product(left, right):
    return lax.dot_general(
        left, right, (((0,), (0,)), ((), ())), preferred_element_type=jnp.float32
    )


def mlp_forward(inputs, weights):
    w_first, b_first, w_second, b_second, norm_gain, norm_shift = weights
    first_pre = jnp.dot(inputs, w_first, preferred_element_type=jnp.float32) + b_first
    hidden = jax.nn.silu(first_pre).astype(jnp.bfloat16)
    second_pre = jnp.dot(hidden, w_second, preferred_element_type=jnp.float32) + b_second
    output, normed, inverse = norm_forward(second_pre, norm_gain, norm_shift)
    return (output, (first_pre, hidden, normed, inverse))


def mlp_backward(inputs, saved, grad_out, weights):
    w_first, b_first, w_second, b_second, norm_gain, norm_shift = weights
    first_pre, hidden, normed, inverse = saved
    grad_second = norm_backward(grad_out, normed, inverse, norm_gain)
    second_low = grad_second.astype(jnp.bfloat16)
    grad_hidden = jnp.dot(second_low, w_second.T, preferred_element_type=jnp.float32)
    grad_first = grad_hidden * silu_slope(first_pre)
    first_low = grad_first.astype(jnp.bfloat16)
    grad_inputs = jnp.dot(first_low, w_first.T, preferred_element_type=jnp.float32)
    grads = (
        row_product(inputs, first_low),
        jnp.sum(grad_first, axis=0),
        row_product(hidden, second_low),
        jnp.sum(grad_second, axis=0),
        jnp.sum(grad_out * normed, axis=0),
        jnp.sum(grad_out, axis=0),
    )
    return (grad_inputs, grads)


def shards(
    nodes,
    edges,
    senders,
    receivers,
    block_count,
    send_rows,
    node_cot,
    edge_cot,
    edge_w1,
    edge_b1,
    edge_w2,
    edge_b2,
    edge_gain,
    edge_shift,
    node_w1,
    node_b1,
    node_w2,
    node_b2,
    node_gain,
    node_shift,
):
    edge_weights = (edge_w1, edge_b1, edge_w2, edge_b2, edge_gain, edge_shift)
    node_weights = (node_w1, node_b1, node_w2, node_b2, node_gain, node_shift)
    own_nodes = nodes[0]
    node_rows, width = own_nodes.shape
    hidden_width = edge_w1.shape[1]
    block_total = senders.shape[1]
    block_rows = senders.shape[2]
    edge_rows = block_total * block_rows
    flat_edges = edges[0].reshape(edge_rows, width)
    flat_send = senders[0].reshape(edge_rows)
    flat_recv = receivers[0].reshape(edge_rows)
    flat_cot = edge_cot[0].reshape(edge_rows, width)
    live_blocks = block_count[0, 0]
    row_lists = send_rows[0, 0]
    slot_count = row_lists.shape[1]
    outgoing = own_nodes[row_lists.reshape(-1)].reshape(2, slot_count, width)
    padded = extended(outgoing, ((DOM, 0),), 1)
    from_lower, from_upper = (padded[0], padded[3])
    node_table = jnp.concatenate([own_nodes, from_lower, from_upper], axis=0)
    group_blocks = 4
    span = group_blocks * block_rows
    step_total = (live_blocks + group_blocks - 1) // group_blocks

    def edge_indices(offset):
        positions = offset + jnp.arange(span, dtype=jnp.int32)
        live_mask = (positions // block_rows < live_blocks).astype(jnp.float32)[:, None]
        return (flat_send, flat_recv, live_mask)

    def edge_inputs(send_part, recv_part):
        return jnp.concatenate([flat_edges, node_table[send_part], own_nodes[recv_part]], axis=1)

    stores = (
        jnp.zeros((edge_rows, 3 * width), jnp.bfloat16),
        jnp.zeros((edge_rows, hidden_width), jnp.float32),
        jnp.zeros((edge_rows, hidden_width), jnp.bfloat16),
        jnp.zeros((edge_rows, width), jnp.float32),
        jnp.zeros((edge_rows, 1), jnp.float32),
    )

    def forward_step(step_index, state_tuple):
        aggregate, edge_out, kept = state_tuple
        offset = step_index * span
        send_part, recv_part, live_mask = edge_indices(offset)
        inputs = edge_inputs(send_part, recv_part)
        message, saved = mlp_forward(inputs, edge_weights)
        live_message = message * live_mask
        aggregate = aggregate.at[recv_part].add(live_message)
        updated = (inputs[:, :width].astype(jnp.float32) + live_message).astype(jnp.bfloat16)
        edge_out = updated
        kept = tuple((piece for piece in (inputs,) + saved))
        return (aggregate, edge_out, kept)

    aggregate, edge_out, kept = lax.fori_loop(
        0,
        step_total,
        forward_step,
        (jnp.zeros((node_rows, width), jnp.float32), flat_edges, stores),
    )
    node_inputs = jnp.concatenate([own_nodes, aggregate.astype(jnp.bfloat16)], axis=1)
    update, node_saved = mlp_forward(node_inputs, node_weights)
    node_out = (own_nodes.astype(jnp.float32) + update).astype(jnp.bfloat16)
    node_grad = node_cot[0].astype(jnp.float32)
    grad_node_inputs, node_grads = mlp_backward(node_inputs, node_saved, node_grad, node_weights)
    grad_aggregate = grad_node_inputs[:, width:]

    def backward_step(step_index, state_tuple):
        table_grad, grad_edge, totals = state_tuple
        offset = step_index * span
        send_part, recv_part, live_mask = edge_indices(offset)
        inputs = kept[0]
        saved = tuple((buffer for buffer in kept[1:]))
        cot_part = flat_cot.astype(jnp.float32)
        grad_message = live_mask * (cot_part + grad_aggregate[recv_part])
        grad_inputs, step_grads = mlp_backward(inputs, saved, grad_message, edge_weights)
        new_grad = (cot_part + grad_inputs[:, :width]).astype(jnp.bfloat16)
        grad_edge = new_grad
        table_grad = table_grad.at[send_part].add(grad_inputs[:, width : 2 * width])
        table_grad = table_grad.at[recv_part].add(grad_inputs[:, 2 * width :])
        totals = tuple((total + piece for total, piece in zip(totals, step_grads)))
        return (table_grad, grad_edge, totals)

    zero_grads = tuple((jnp.zeros(piece.shape, jnp.float32) for piece in edge_weights))
    table_grad, grad_edge, edge_grads = lax.fori_loop(
        0,
        step_total,
        backward_step,
        (jnp.zeros((node_table.shape[0], width), jnp.float32), flat_cot, zero_grads),
    )
    halo_grad = table_grad[node_rows:].reshape(2, slot_count, width)
    padded_grad = extended(halo_grad.astype(jnp.bfloat16), ((DOM, 0),), 1).astype(halo_grad.dtype)
    back_lower, back_upper = (padded_grad[0], padded_grad[3])
    returned = jnp.concatenate([back_lower, back_upper], axis=0)
    local_grad = node_grad + grad_node_inputs[:, :width] + table_grad[:node_rows]
    local_grad = local_grad.at[row_lists.reshape(-1)].add(returned)
    grad_node = local_grad.astype(jnp.bfloat16)
    flat_grads = jnp.concatenate([piece.reshape(-1) for piece in edge_grads + node_grads])
    summed = nested_sum(flat_grads, (("dom_0", "dom_1"), ("dom_2", "grp")))
    scale = 1.0 / math.sqrt(lax.axis_size(DOM) * lax.axis_size("grp") * edge_rows)
    weight_grads = summed * scale
    return (
        node_out[None],
        edge_out.reshape(1, block_total, block_rows, width),
        grad_node[None],
        grad_edge.reshape(1, block_total, block_rows, width),
        weight_grads,
    )


def solution(mesh):
    finer = Mesh(
        mesh.devices.reshape(4, 8, 2, mesh.shape["grp"]), ("dom_0", "dom_1", "dom_2", "grp")
    )
    in_specs = (
        P("grp", DOM, None),
        P("grp", DOM, None, None),
        P("grp", DOM, None),
        P("grp", DOM, None),
        P("grp", DOM),
        P("grp", DOM, None, None),
        P("grp", DOM, None),
        P("grp", DOM, None, None),
        P(),
        P(),
        P(),
        P(),
        P(),
        P(),
        P(),
        P(),
        P(),
        P(),
        P(),
        P(),
    )
    out_specs = (
        P("grp", DOM, None),
        P("grp", DOM, None, None),
        P("grp", DOM, None),
        P("grp", DOM, None, None),
        P(),
    )
    return jax.shard_map(
        shards, mesh=finer, in_specs=in_specs, out_specs=out_specs, check_vma=False
    )
```

profile of v0, /device:TPU:1, one launch (start us, length us, event | category | flops | bytes accessed | tf_op | source)
XLA Modules:
  0.0 130.5 jit_solution(15611981314673636786)
XLA Ops:
  0.7 0.7 copy-done.21
  1.4 1.7 %gather_fusion.1 = bf16[256,128]{1,0:T(8,128)(2,1)S(1)} fusion(bf16[512,128]{1,0:T(8,128)(2,1)} %bitcast.152, s32[1024]{0:T(1024)S(1)} %pad_clamp_fusion.3), kind=kCustom, calls=%fused_computation.1 | custom fusion | bytes 132096 | tf_op jit(solution)/shard_map/gather | solution.py:173
  3.2 5.1 %collective-permute-start.1 = (bf16[1,128,128]{1,2,0:T(8,128)(2,1)S(1)}, bf16[1,128,128]{1,2,0:T(8,128)(2,1)S(1)}, u32[]{:S(2)}, u32[]{:S(2)}) collective-permute-start(bf16[1,128,128]{1,2,0:T(8,128)(2,1)S(1)} %bitcast.183), channel_id=1, source_target_pairs={{4,0},{8,4},{12,8},{16,12},{20,16},{24,20},{28,24},{32,28},{36,32}... | collective-permute-start | bytes 98312 | tf_op jit(solution)/shard_map/ppermute | solution.py:23
  8.4 2.1 %collective-permute-start = (bf16[1,128,128]{1,2,0:T(8,128)(2,1)S(1)}, bf16[1,128,128]{1,2,0:T(8,128)(2,1)S(1)}, u32[]{:S(2)}, u32[]{:S(2)}) collective-permute-start(bf16[1,128,128]{1,2,0:T(8,128)(2,1)S(1)} %bitcast.184), channel_id=1, source_target_pairs={{0,4},{4,8},{8,12},{12,16},{16,20},{20,24},{24,28},{28,32},{32,36}... | collective-permute-start | bytes 98312 | tf_op jit(solution)/shard_map/ppermute | solution.py:22
  10.5 0.6 copy-done.16
  11.3 0.7 convert_reduce_fusion
  12.8 1.3 %gather_fusion.3 = bf16[512,128]{1,0:T(8,128)(2,1)S(1)} fusion(bf16[512,128]{1,0:T(8,128)(2,1)S(1)} %bitcast.153, s32[1024]{0:T(1024)S(1)} %pad_clamp_fusion.1), kind=kCustom, calls=%fused_computation.3 | custom fusion | bytes 264192 | tf_op jit(solution)/shard_map/while/body/gather | solution.py:187
  14.2 0.7 copy.107
  15.1 0.7 copy.131
  16.0 1.3 %gather_fusion.2 = bf16[512,128]{1,0:T(8,128)(2,1)S(1)} fusion(bf16[768,128]{1,0:T(8,128)(2,1)S(1)} %copy.79, s32[1024]{0:T(1024)S(1)} %pad_clamp_fusion.2), kind=kCustom, calls=%fused_computation.2 | custom fusion | bytes 264192 | tf_op jit(solution)/shard_map/while/body/gather | solution.py:187
  18.0 1.0 add_reduce_fusion
  19.3 0.6 broadcast_in_dim.32
  19.9 0.7 broadcast_in_dim.31
  20.6 0.7 broadcast.453.clone.1
  21.3 0.7 broadcast.453.clone
  22.1 0.8 broadcast_in_dim.30
  22.8 7.5 %while.52 = (s32[]{:T(128)}, f32[512,128]{1,0:T(8,128)S(1)}, bf16[512,128]{1,0:T(8,128)(2,1)}, bf16[512,384]{1,0:T(8,128)(2,1)}, f32[512,128]{1,0:T(8,128)}, /*i...) while((s32[]{:T(128)}, f32[512,128]{1,0:T(8,128)S(1)}, ...), condition=%wide.region_4.5_spmd, body=%wide.region_2.4_spmd.sunk | while | flops 2438147 | bytes 4105505 | solution.py:210
  22.8 0.7 fusion.103
  23.6 1.3 %gather_fusion = bf16[512,128]{1,0:T(8,128)(2,1)S(1)} fusion(bf16[512,128]{1,0:T(8,128)(2,1)S(1)} %get-tuple-element.1407, s32[1024]{0:T(1024)S(1)} %pad_clamp_fusion.5), kind=kCustom, calls=%fused_computation.clone.1 | custom fusion | bytes 264192 | tf_op jit(solution)/shard_map/while/body/gather | solution.py:187
  24.9 0.8 pad_maximum_fusion.8
  25.7 1.0 multiply_convert_fusion.7
  26.8 3.5 %scatter_custom_fusion.15 = f32[512,128]{1,0:T(8,128)S(1)} fusion(f32[512,128]{1,0:T(8,128)S(1)} %get-tuple-element.1366, s32[512]{0:T(512)S(1)} %bitcast.173, f32[512,128]{1,0:T(8,128)S(1)} %get-tuple-element.1395, f32[512]{0:T(512)S(1)} %fusion.103, f32[128]{0:T(128)S(1)} %get-tuple-element.1404, f32[128]{0:T(128)S(1)} %get-tuple-element.1403), kind=kCustom, calls=%fused_computation.14.clone.1 | custom fusion | flops 262144 | bytes 527360 | tf_op jit(solution)/shard_map/while/body/scatter-add | solution.py:204
  30.5 0.5 copy-done.24
  32.1 0.6 copy-done.20
  33.2 0.9 fusion.68
  34.5 1.7 %negate_exponential_fusion = f32[512,128]{1,0:T(8,128)} fusion(f32[512,128]{1,0:T(8,128)} %get-tuple-element.1432), kind=kLoop, calls=%fused_computation.97 | loop fusion | flops 65536 | bytes 524288 | tf_op jit(solution)/shard_map/while/body/exp | solution.py:97
  36.2 0.7 fusion.65
  36.9 1.0 gather_fusion.4
  38.0 0.5 broadcast.461.clone.2
  38.5 0.6 broadcast.461.clone.1
  39.1 0.6 broadcast.461.clone
  40.2 0.9 copy-done.3
  41.1 15.7 %while.53 = (s32[]{:T(128)}, f32[768,128]{1,0:T(8,128)S(1)}, bf16[512,128]{1,0:T(8,128)(2,1)}, f32[384,128]{0,1:T(8,128)S(1)}, f32[128]{0:T(128)}, /*index=5*/f3...) while((s32[]{:T(128)}, f32[768,128]{1,0:T(8,128)S(1)}, ...), condition=%wide.region_18.19_spmd, body=%wide.region_9.18_spmd.sunk | while | flops 136327168 | bytes 6593785 | solution.py:240
  41.1 0.7 fusion.114
  42.4 1.2 add.550
  43.6 1.2 add.551
  44.9 1.2 add.552
  46.3 1.3 fusion.116
  47.5 1.1 add.549
  49.2 0.7 fusion.118
  49.8 3.5 %scatter_custom_fusion.18 = f32[768,128]{1,0:T(8,128)S(1)} fusion(f32[768,128]{1,0:T(8,128)S(1)} %get-tuple-element.1440, s32[512]{0:T(512)S(1)} %bitcast.180, f32[512,384]{1,0:T(8,128)S(1)} %fusion.117), kind=kCustom, calls=%fused_computation.45.clone.1 | custom fusion | flops 65536 | bytes 655360 | tf_op jit(solution)/shard_map/while/body/scatter-add | solution.py:234
  53.3 3.5 %scatter_custom_fusion.19 = f32[768,128]{1,0:T(8,128)S(1)} fusion(f32[768,128]{1,0:T(8,128)S(1)} %scatter_custom_fusion.18, s32[512]{0:T(512)S(1)} %bitcast.179, f32[512,384]{1,0:T(8,128)S(1)} %fusion.117), kind=kCustom, calls=%fused_computation.43.clone.1 | custom fusion | flops 65536 | bytes 655360 | tf_op jit(solution)/shard_map/while/body/scatter-add | solution.py:235
  57.2 0.8 copy-done.9
  58.2 0.6 constant_dynamic-update-slice_fusion.9
  58.8 0.7 constant_dynamic-update-slice_fusion.8
  59.5 0.7 constant_dynamic-update-slice_fusion.7
  60.1 0.6 constant_dynamic-update-slice_fusion.6
  60.8 0.6 copy-done.27
  61.5 0.6 copy-done.22
  62.4 0.7 copy-done.23
  63.8 13.4 %all_to_all.28 = f32[8,32,452]{2,1,0:T(8,128)S(1)} all-to-all(f32[8,32,452]{2,1,0:T(8,128)S(1)} %copy.90), channel_id=1, replica_groups=mesh['dom_0'=4,'dom_1'=8,'dom_2'=2,'grp'=4] {'dom_2','grp'}, dimensions={0} | all-to-all | bytes 925696 | tf_op jit(solution)/shard_map/all_to_all | solution.py:59
  77.3 20.2 %all_to_all.29 = f32[32,1,452]{2,1,0:T(1,128)S(1)} all-to-all(f32[32,1,452]{2,1,0:T(1,128)S(1)} %all_to_all.19), channel_id=1, replica_groups=mesh['dom_0'=4,'dom_1'=8,'dom_2'=2,'grp'=4] {'dom_0','dom_1'}, dimensions={0} | all-to-all | bytes 115712 | tf_op jit(solution)/shard_map/all_to_all | solution.py:67
  97.5 0.7 broadcast_in_dim.38
  98.2 3.9 %all-to-all-start.2 = ((f32[32,1,452]{2,1,0:T(1,128)}), f32[32,1,452]{2,1,0:T(1,128)S(1)}, u32[]{:S(2)}, u32[]{:S(2)}) async-start(f32[32,1,452]{2,1,0:T(1,128)} %broadcast_in_dim.38), calls=%async_computation.2 | async-start | bytes 131072 | tf_op jit(solution)/shard_map/all_to_all | solution.py:35
  102.1 8.8 %all-to-all-done.2 = f32[32,1,452]{2,1,0:T(1,128)S(1)} async-done(((f32[32,1,452]{2,1,0:T(1,128)}), f32[32,1,452]{2,1,0:T(1,128)S(1)}, u32[]{:S(2)}, u32[]{:S(2)}) %all-to-all-start.2) | async-done | bytes 57888 | tf_op jit(solution)/shard_map/all_to_all | solution.py:35
  111.0 0.8 broadcast_in_dim.39
  111.8 6.3 %all-to-all-start.3 = ((f32[8,32,452]{2,1,0:T(8,128)}), f32[8,32,452]{2,1,0:T(8,128)S(1)}, u32[]{:S(2)}, u32[]{:S(2)}) async-start(f32[8,32,452]{2,1,0:T(8,128)} %broadcast_in_dim.39), calls=%async_computation.3 | async-start | bytes 1048576 | tf_op jit(solution)/shard_map/all_to_all | solution.py:35
  118.1 2.4 %collective-permute-start.2 = (bf16[1,128,128]{2,1,0:T(8,128)(2,1)S(1)}, bf16[1,128,128]{2,1,0:T(8,128)(2,1)S(1)}, u32[]{:S(2)}, u32[]{:S(2)}) collective-permute-start(bf16[1,128,128]{2,1,0:T(8,128)(2,1)S(1)} %get-tuple-element.1024), channel_id=1, source_target_pairs={{0,4},{4,8},{8,12},{12,16},{16,20},{20,24},{24,28},{28,32},{32,36}... | collective-permute-start | bytes 98312 | tf_op jit(solution)/shard_map/ppermute | solution.py:22
  120.6 1.9 %collective-permute-start.3 = (bf16[1,128,128]{2,1,0:T(8,128)(2,1)S(1)}, bf16[1,128,128]{2,1,0:T(8,128)(2,1)S(1)}, u32[]{:S(2)}, u32[]{:S(2)}) collective-permute-start(bf16[1,128,128]{2,1,0:T(8,128)(2,1)S(1)} %get-tuple-element.1025), channel_id=1, source_target_pairs={{4,0},{8,4},{12,8},{16,12},{20,16},{24,20},{28,24},{32,28},{36,32}... | collective-permute-start | bytes 98312 | tf_op jit(solution)/shard_map/ppermute | solution.py:23
  122.5 0.8 copy.92
  123.4 2.7 %collective-permute-done.3 = bf16[1,128,128]{2,1,0:T(8,128)(2,1)S(1)} collective-permute-done((bf16[1,128,128]{2,1,0:T(8,128)(2,1)S(1)}, bf16[1,128,128]{2,1,0:T(8,128)(2,1)S(1)}, u32[]{:S(2)}, u32[]{:S(2)}) %collective-permute-start.3) | collective-permute-done | bytes 32800 | tf_op jit(solution)/shard_map/ppermute | solution.py:23
  126.1 2.1 %scatter_custom_fusion.3 = f32[512,128]{1,0:T(8,128)S(1)} fusion(f32[512,128]{1,0:T(8,128)S(1)} %copy.87, s32[256]{0:T(256)S(1)} %bitcast.188, f32[128,128]{1,0:T(8,128)S(1)} %get-tuple-element.1028, f32[]{:T(128)} %constant.233, f32[128,128]{1,0:T(8,128)S(1)} %get-tuple-element.1027), kind=kCustom, calls=%fused_computation.109 | custom fusion | flops 65536 | bytes 393220 | tf_op jit(solution)/shard_map/scatter-add | solution.py:251
  128.2 0.7 convert_bitcast_fusion.1
  129.2 1.2 mul.282
  (123 shorter events, 8.2 us)
Async XLA Ops:
  0.6 29.8 %copy-start = (bf16[256,128]{1,0:T(8,128)(2,1)S(1)}, bf16[256,128]{1,0:T(8,128)(2,1)}, u32[]{:S(2)}) copy-start(bf16[256,128]{1,0:T(8,128)(2,1)} %param.38) | copy-start | bytes 196612
  0.6 0.7 copy-start.21
  3.0 8.1 %copy-start.15 = (bf16[1,512,128]{2,1,0:T(8,128)(2,1)S(1)}, bf16[1,512,128]{2,1,0:T(8,128)(2,1)}, u32[]{:S(2)}) copy-start(bf16[1,512,128]{2,1,0:T(8,128)(2,1)} %param.30) | copy-start | bytes 393220
  3.2 12.6 %collective-permute-start.1 = (bf16[1,128,128]{1,2,0:T(8,128)(2,1)S(1)}, bf16[1,128,128]{1,2,0:T(8,128)(2,1)S(1)}, u32[]{:S(2)}, u32[]{:S(2)}) collective-permute-start(bf16[1,128,128]{1,2,0:T(8,128)(2,1)S(1)} %bitcast.183), channel_id=1, source_target_pairs={{4,0},{8,4},{12,8},{16,12},{20,16},{24,20},{28,24},{32,28},{36,32}... | collective-permute-start | bytes 98312 | tf_op jit(solution)/shard_map/ppermute | solution.py:23
  8.4 2.1 %copy-start.11 = (s32[1,4,128]{2,1,0:T(4,128)S(1)}, s32[1,4,128]{2,1,0:T(4,128)}, u32[]{:S(2)}) copy-start(s32[1,4,128]{2,1,0:T(4,128)} %param.27) | copy-start | bytes 6148
  8.4 7.4 %collective-permute-start = (bf16[1,128,128]{1,2,0:T(8,128)(2,1)S(1)}, bf16[1,128,128]{1,2,0:T(8,128)(2,1)S(1)}, u32[]{:S(2)}, u32[]{:S(2)}) collective-permute-start(bf16[1,128,128]{1,2,0:T(8,128)(2,1)S(1)} %bitcast.184), channel_id=1, source_target_pairs={{0,4},{4,8},{8,12},{12,16},{16,20},{20,24},{24,28},{28,32},{32,36}... | collective-permute-start | bytes 98312 | tf_op jit(solution)/shard_map/ppermute | solution.py:22
  10.5 0.7 copy-start.16
  11.3 1.4 %copy-start.1 = (bf16[1,512,128]{2,1,0:T(8,128)(2,1)S(1)}, bf16[1,512,128]{2,1,0:T(8,128)(2,1)}, u32[]{:S(2)}) copy-start(bf16[1,512,128]{2,1,0:T(8,128)(2,1)} %param.24) | copy-start | bytes 393220
  12.8 1.4 %copy-start.5 = (bf16[1,4,128,128]{3,2,1,0:T(8,128)(2,1)S(1)}, bf16[1,4,128,128]{3,2,1,0:T(8,128)(2,1)}, u32[]{:S(2)}) copy-start(bf16[1,4,128,128]{3,2,1,0:T(8,128)(2,1)} %param.25) | copy-start | bytes 393220
  14.2 1.0 copy-start.4
  16.0 1.4 %copy-start.8 = (bf16[384,128]{1,0:T(8,128)(2,1)S(1)}, bf16[384,128]{1,0:T(8,128)(2,1)}, u32[]{:S(2)}) copy-start(bf16[384,128]{1,0:T(8,128)(2,1)} %param.32) | copy-start | bytes 294916
  17.4 0.7 copy-start.18
  17.4 0.7 copy-start.19
  22.0 0.8 copy-start.14
  22.0 0.8 copy-start.17
  23.5 2.2 %copy-start.12 = (f32[512]{0:T(512)}, f32[512]{0:T(512)S(1)}, u32[]{:S(2)}) copy-start(f32[512]{0:T(512)S(1)} %add_rsqrt_fusion.3) | copy-start | bytes 6148 | tf_op jit(solution)/shard_map/while
  26.8 3.5 %copy-start.2 = (f32[512,128]{1,0:T(8,128)}, f32[512,128]{1,0:T(8,128)S(1)}, u32[]{:S(2)}) copy-start(f32[512,128]{1,0:T(8,128)S(1)} %get-tuple-element.1395) | copy-start | bytes 786436 | tf_op jit(solution)/shard_map/while
  30.3 0.7 copy-start.24
  31.0 0.8 copy-start.25
  31.0 0.8 copy-start.26
  32.1 0.7 copy-start.20
  36.9 3.3 %copy-start.7 = (bf16[512,128]{1,0:T(8,128)(2,1)S(1)}, bf16[512,128]{1,0:T(8,128)(2,1)}, u32[]{:S(2)}) copy-start(bf16[512,128]{1,0:T(8,128)(2,1)} %get-tuple-element.1436) | copy-start | bytes 393220
  37.9 2.3 %copy-start.6 = (bf16[512,384]{1,0:T(8,128)(2,1)S(1)}, bf16[512,384]{1,0:T(8,128)(2,1)}, u32[]{:S(2)}) copy-start(bf16[512,384]{1,0:T(8,128)(2,1)} %get-tuple-element.1435) | copy-start | bytes 1179652
  40.1 0.9 copy-start.3
  40.2 0.9 copy-start.13
  57.1 1.0 copy-start.9
  60.8 0.6 copy-start.27
  61.4 0.7 copy-start.22
  62.3 0.7 copy-start.23
  98.2 12.7 %all-to-all-start.2 = ((f32[32,1,452]{2,1,0:T(1,128)}), f32[32,1,452]{2,1,0:T(1,128)S(1)}, u32[]{:S(2)}, u32[]{:S(2)}) async-start(f32[32,1,452]{2,1,0:T(1,128)} %broadcast_in_dim.38), calls=%async_computation.2 | async-start | bytes 131072 | tf_op jit(solution)/shard_map/all_to_all | solution.py:35
  102.1 20.4 %copy-start.10 = (bf16[768,128]{1,0:T(8,128)(2,1)}, bf16[768,128]{1,0:T(8,128)(2,1)S(1)}, u32[]{:S(2)}) copy-start(bf16[768,128]{1,0:T(8,128)(2,1)S(1)} %convert.3) | copy-start | bytes 589828
  111.8 17.1 %all-to-all-start.3 = ((f32[8,32,452]{2,1,0:T(8,128)}), f32[8,32,452]{2,1,0:T(8,128)S(1)}, u32[]{:S(2)}, u32[]{:S(2)}) async-start(f32[8,32,452]{2,1,0:T(8,128)} %broadcast_in_dim.39), calls=%async_computation.3 | async-start | bytes 1048576 | tf_op jit(solution)/shard_map/all_to_all | solution.py:35
  118.1 5.3 %collective-permute-start.2 = (bf16[1,128,128]{2,1,0:T(8,128)(2,1)S(1)}, bf16[1,128,128]{2,1,0:T(8,128)(2,1)S(1)}, u32[]{:S(2)}, u32[]{:S(2)}) collective-permute-start(bf16[1,128,128]{2,1,0:T(8,128)(2,1)S(1)} %get-tuple-element.1024), channel_id=1, source_target_pairs={{0,4},{4,8},{8,12},{12,16},{16,20},{20,24},{24,28},{28,32},{32,36}... | collective-permute-start | bytes 98312 | tf_op jit(solution)/shard_map/ppermute | solution.py:22
  120.6 5.5 %collective-permute-start.3 = (bf16[1,128,128]{2,1,0:T(8,128)(2,1)S(1)}, bf16[1,128,128]{2,1,0:T(8,128)(2,1)S(1)}, u32[]{:S(2)}, u32[]{:S(2)}) collective-permute-start(bf16[1,128,128]{2,1,0:T(8,128)(2,1)S(1)} %get-tuple-element.1025), channel_id=1, source_target_pairs={{4,0},{8,4},{12,8},{16,12},{20,16},{24,20},{28,24},{32,28},{36,32}... | collective-permute-start | bytes 98312 | tf_op jit(solution)/shard_map/ppermute | solution.py:23
  123.3 2.8 %slice-start = ((bf16[768,128]{1,0:T(8,128)(2,1)}), bf16[256,128]{1,0:T(8,128)(2,1)S(1)}, s32[]{:S(2)}) async-start(bf16[768,128]{1,0:T(8,128)(2,1)} %copy-done.10), calls=%async_computation.4 | async-start | bytes 131072 | tf_op jit(solution)/shard_map/slice | solution.py:246
where the time goes:
time: 131 us; the launch traced here: 130 us
  blocking collectives  33.6 us (26%)
  local copies, waits for them, and re-layouts  30.6 us (23%)
  other arithmetic  25.6 us (20%)
  starting transfers between devices  21.7 us (17%)
  waiting for transfers between devices  11.5 us (9%)
  matrix products  5.45 us (4%)
  between operations  1.92 us (1%)
    all_to_all x1, blocking collectives, sum_by_axis(): lax.all_to_all(nearer, far, split_axis=0, concat_axis=0, tiled=True)  20.2 us
    all_to_all x1, blocking collectives, sent_and_summed(): lax.all_to_all(cut_along(value, dim, length), axis, 0, 0, tiled=True)  13.4 us
    unnamed x72, local copies, waits for them, and re-layouts  12.7 us
    all_to_all x2, starting transfers between devices, copy_for_each(): return lax.all_to_all(copies, axis, split_axis=0, concat_axis=0, tiled=True)  10.2 us
    all_to_all x2, waiting for transfers between devices, copy_for_each(): return lax.all_to_all(copies, axis, split_axis=0, concat_axis=0, tiled=True)  8.82 us
    ppermute x2, starting transfers between devices, extended(): after = lax.ppermute(leading, axis, down)  7.03 us
    add x4, other arithmetic, backward_step(): totals = tuple((total + piece for total, piece in zip(totals, step_grads)))  4.7 us
    ppermute x2, starting transfers between devices, extended(): before = lax.ppermute(last, axis, up)  4.48 us
  transfers between devices with their start and end apart: 6, of which 2 were waited for; matrix products, arithmetic and copies ran while one was open for 6% of the time, Pallas kernels for 0%

commit v1 on v0

v1 whole, which is shorter than its diff:
```python
import math

import jax
import jax.numpy as jnp
from jax import lax
from jax.experimental import pallas as pl
from jax.experimental.pallas import tpu as pltpu
from jax.sharding import Mesh
from jax.sharding import PartitionSpec as P

DOM = ("y", "z", "c")
PLANE = ("z", "x")
EPSILON = 1e-05
F32 = jnp.float32
BF16 = jnp.bfloat16
ROWS = 1024
HALF = 512
LIVE_ROWS = 904
VMEM = pl.BlockSpec(memory_space=pltpu.VMEM)
SMEM = pl.BlockSpec(memory_space=pltpu.SMEM)


def dot(left, right):
    return jnp.dot(left, right, preferred_element_type=F32)


def dot_nt(left, right):
    return lax.dot_general(left, right, (((1,), (1,)), ((), ())), preferred_element_type=F32)


def dot_tn(left, right):
    return lax.dot_general(left, right, (((0,), (0,)), ((), ())), preferred_element_type=F32)


def as_bf16(mask):
    return jnp.where(mask, 1.0, 0.0).astype(BF16)


def pick_rows(row, count):
    column = jnp.transpose(jnp.broadcast_to(row, (128, 128)))
    lanes = lax.broadcasted_iota(jnp.int32, (128, 128), 1)
    tiles = [as_bf16(column == lanes + 128 * j) for j in range(count // 128)]
    return jnp.concatenate(tiles, axis=1)


def place_rows(row, count):
    lines = lax.broadcasted_iota(jnp.int32, (count, 128), 0)
    return as_bf16(lines == row)


def split(value):
    high = value.astype(BF16)
    low = (value - high.astype(F32)).astype(BF16)
    return jnp.concatenate([high, low], axis=1)


def joined(value):
    return value[:, :128] + value[:, 128:]


def pack_kernel(nodes, lists, near, far):
    core = lax.axis_index("c")
    near[...] = dot(pick_rows(lists[pl.ds(1 - core, 1), :], 512), nodes[...]).astype(BF16)
    far[...] = dot(pick_rows(lists[pl.ds(core, 1), :], 512), nodes[...]).astype(BF16)


def norm_forward(second):
    average = jnp.mean(second, axis=-1, keepdims=True)
    centred = second - average
    variance = jnp.mean(centred * centred, axis=-1, keepdims=True)
    inverse = lax.rsqrt(variance + EPSILON)
    return centred * inverse, inverse


def norm_backward(cot, normed, inverse, gain):
    scaled = cot * gain
    return inverse * (
        scaled
        - jnp.mean(scaled, axis=-1, keepdims=True)
        - normed * jnp.mean(scaled * normed, axis=-1, keepdims=True)
    )


def partial_sum(value):
    return jnp.sum(value.reshape(-1, 8, 128), axis=0)


def total(value):
    return jnp.sum(value, axis=0, keepdims=True)


def main_kernel(
    count, nodes, near, far, edges, senders, receivers, node_cot, edge_cot,
    ew1, eb1, ew2, eb2, egain, eshift, nw1, nb1, nw2, nb2, ngain, nshift,
    node_out, edge_out, grad_edge, local_grad, near_grad, far_grad, keep, send,
    table, pick_recv, place_recv, place_send, messages, inputs, hidden, slope, normed, inverse,
    spread, dxs, dxr, first_low, second_low, node_inputs, node_hidden, node_first, node_second, grads,
):
    core = lax.axis_index("c")
    live_blocks = count[0, 0]
    table[pl.ds(0, 512), :] = nodes[...]
    table[pl.ds(pl.multiple_of(640 - 128 * core, 128), 128), :] = near[...]
    table[pl.ds(pl.multiple_of(512 + 128 * core, 128), 128), :] = far[...]

    for b in range(4):
        rows = pl.ds(b * 128, 128)
        live = jnp.where(b < live_blocks, 1.0, 0.0).astype(F32)
        send_row, recv_row = senders[pl.ds(b, 1), :], receivers[pl.ds(b, 1), :]
        pick = pick_rows(recv_row, 512)
        pick_recv[rows, :] = pick
        place_recv[:, rows] = place_rows(recv_row, 512)
        place_send[:, rows] = place_rows(send_row, 768)
        own = edges[rows, :]
        sender = dot(pick_rows(send_row, 768), table[...]).astype(BF16)
        receiver = dot(pick, nodes[...]).astype(BF16)
        gathered = jnp.concatenate([own, sender, receiver], axis=1)
        inputs[rows, :] = gathered
        first = dot(gathered, ew1[...]) + eb1[...]
        sigmoid = jax.nn.sigmoid(first)
        low = (first * sigmoid).astype(BF16)
        hidden[rows, :] = low
        slope[rows, :] = sigmoid * (1.0 + first * (1.0 - sigmoid))
        n, inv = norm_forward(dot(low, ew2[...]) + eb2[...])
        normed[rows, :] = n
        inverse[rows, :] = inv
        message = (n * egain[...] + eshift[...]) * live
        edge_out[rows, :] = (own.astype(F32) + message).astype(BF16)
        messages[rows, :] = split(message)

    sums = [jnp.zeros((8, 128), F32) for _ in range(8)]
    for b in range(4):
        rows = pl.ds(b * 128, 128)
        aggregate = joined(dot(place_recv[rows, :], messages[...])).astype(BF16)
        own = nodes[rows, :]
        gathered = jnp.concatenate([own, aggregate], axis=1)
        node_inputs[rows, :] = gathered
        first = dot(gathered, nw1[...]) + nb1[...]
        sigmoid = jax.nn.sigmoid(first)
        low = (first * sigmoid).astype(BF16)
        node_hidden[rows, :] = low
        n, inv = norm_forward(dot(low, nw2[...]) + nb2[...])
        node_out[rows, :] = (own.astype(F32) + (n * ngain[...] + nshift[...])).astype(BF16)
        cot = node_cot[rows, :].astype(F32)
        g2 = norm_backward(cot, n, inv, ngain[...])
        g2_low = g2.astype(BF16)
        g1 = dot_nt(g2_low, nw2[...]) * (sigmoid * (1.0 + first * (1.0 - sigmoid)))
        g1_low = g1.astype(BF16)
        node_first[rows, :] = g1_low
        node_second[rows, :] = g2_low
        back = dot_nt(g1_low, nw1[...])
        local_grad[rows, :] = cot + back[:, :128]
        spread[rows, :] = split(back[:, 128:])
        for k, piece in enumerate((g1, g2, cot * n, cot)):
            sums[4 + k] += partial_sum(piece)

    for b in range(4):
        rows = pl.ds(b * 128, 128)
        live = jnp.where(b < live_blocks, 1.0, 0.0).astype(F32)
        edge_grad = edge_cot[rows, :].astype(F32)
        cot = live * (edge_grad + joined(dot(pick_recv[rows, :], spread[...])))
        n = normed[rows, :]
        g2 = norm_backward(cot, n, inverse[rows, :], egain[...])
        g2_low = g2.astype(BF16)
        g1 = dot_nt(g2_low, ew2[...]) * slope[rows, :]
        g1_low = g1.astype(BF16)
        first_low[rows, :] = g1_low
        second_low[rows, :] = g2_low
        back = dot_nt(g1_low, ew1[...])
        grad_edge[rows, :] = (edge_grad + back[:, :128]).astype(BF16)
        dxs[rows, :] = split(back[:, 128:256])
        dxr[rows, :] = split(back[:, 256:])
        for k, piece in enumerate((g1, g2, cot * n, cot)):
            sums[k] += partial_sum(piece)

    lower = joined(dot(place_send[512:640, :], dxs[...])).astype(BF16)
    upper = joined(dot(place_send[640:768, :], dxs[...])).astype(BF16)
    is_first = core == 0
    near_grad[...] = jnp.where(is_first, upper, lower)
    far_grad[...] = jnp.where(is_first, lower, upper)

    grads[0:384, :] = dot_tn(inputs[...], first_low[...])
    grads[384:385, :] = total(sums[0])
    grads[385:513, :] = dot_tn(hidden[...], second_low[...])
    grads[513:514, :] = total(sums[1])
    grads[514:515, :] = total(sums[2])
    grads[515:516, :] = total(sums[3])
    grads[516:772, :] = dot_tn(node_inputs[...], node_first[...])
    grads[772:773, :] = total(sums[4])
    grads[773:901, :] = dot_tn(node_hidden[...], node_second[...])
    grads[901:902, :] = total(sums[5])
    grads[902:903, :] = total(sums[6])
    grads[903:904, :] = total(sums[7])
    grads[904:1024, :] = jnp.zeros((120, 128), F32)
    keep[...] = grads[pl.ds(pl.multiple_of(core * HALF, HALF), HALF), :]
    send[...] = grads[pl.ds(pl.multiple_of((1 - core) * HALF, HALF), HALF), :].astype(BF16)

    for b in range(4):
        rows = pl.ds(b * 128, 128)
        both = dot(place_send[rows, :], dxs[...]) + dot(place_recv[rows, :], dxr[...])
        local_grad[rows, :] += joined(both)


def finish_kernel(local_grad, near, far, lists, out):
    core = lax.axis_index("c")
    added = dot(place_rows(lists[pl.ds(1 - core, 1), :], 512), near[...])
    added += dot(place_rows(lists[pl.ds(core, 1), :], 512), far[...])
    out[...] = (local_grad[...] + added).astype(BF16)


def call(body, name, out_shape, operands, scratch=(), flops=1000000, smem_first=False, vmem=None):
    specs = [VMEM] * len(operands)
    if smem_first:
        specs[0] = SMEM
    return pl.pallas_call(
        body,
        name=name,
        out_shape=out_shape,
        in_specs=specs,
        out_specs=jax.tree.map(lambda _: VMEM, out_shape),
        scratch_shapes=scratch,
        compiler_params=pltpu.CompilerParams(vmem_limit_bytes=vmem),
        cost_estimate=pl.CostEstimate(flops=flops, bytes_accessed=1000000, transcendentals=0),
    )(*operands)


def shape(rows, width, kind):
    return jax.ShapeDtypeStruct((rows, width), kind)


def exchange(value, axis, size, flip):
    return lax.ppermute(value, axis, [(j, j ^ flip) for j in range(size)])


def shards(
    nodes, edges, senders, receivers, block_count, send_rows, node_cot, edge_cot,
    edge_w1, edge_b1, edge_w2, edge_b2, edge_gain, edge_shift,
    node_w1, node_b1, node_w2, node_b2, node_gain, node_shift,
):
    own_nodes = nodes[0]
    lists = send_rows[0, 0]
    line = lambda vector: vector.reshape(1, 128)
    near_pairs = [(j, j ^ 1) for j in range(64)]
    far_pairs = [(j, j + 1) for j in range(1, 63, 2)] + [(j + 1, j) for j in range(1, 63, 2)]

    near, far = call(pack_kernel, "pack", (shape(128, 128, BF16),) * 2, (own_nodes, lists))
    far = lax.ppermute(far, DOM, far_pairs)
    near = lax.ppermute(near, DOM, near_pairs)

    operands = (
        block_count, own_nodes, near, far, edges[0].reshape(512, 128), senders[0], receivers[0],
        node_cot[0], edge_cot[0].reshape(512, 128),
        edge_w1, line(edge_b1), edge_w2, line(edge_b2), line(edge_gain), line(edge_shift),
        node_w1, line(node_b1), node_w2, line(node_b2), line(node_gain), line(node_shift),
    )
    outs = (
        shape(512, 128, BF16), shape(512, 128, BF16), shape(512, 128, BF16), shape(512, 128, F32),
        shape(128, 128, BF16), shape(128, 128, BF16), shape(HALF, 128, F32), shape(HALF, 128, BF16),
    )
    scratch = [
        pltpu.VMEM(dims, kind)
        for dims, kind in (
            ((768, 128), BF16), ((512, 512), BF16), ((512, 512), BF16), ((768, 512), BF16),
            ((512, 256), BF16), ((512, 384), BF16), ((512, 128), BF16), ((512, 128), F32),
            ((512, 128), F32), ((512, 1), F32), ((512, 256), BF16), ((512, 256), BF16), ((512, 256), BF16),
            ((512, 128), BF16), ((512, 128), BF16), ((512, 256), BF16), ((512, 128), BF16),
            ((512, 128), BF16), ((512, 128), BF16), ((ROWS, 128), F32),
        )
    ]
    node_out, edge_out, grad_edge, local_grad, near_grad, far_grad, keep, send = call(
        main_kernel, "main", outs, operands, scratch, flops=2000000000, smem_first=True, vmem=24 << 20
    )

    arrived = exchange(send, "c", 2, 1)
    pair = (keep + arrived.astype(F32)).astype(BF16).reshape(32, 16, 128)
    far_back = lax.ppermute(far_grad, DOM, far_pairs)
    near_back = lax.ppermute(near_grad, DOM, near_pairs)
    tiles = lax.all_to_all(pair, PLANE, 0, 0, tiled=True)
    piece = jnp.sum(tiles.astype(F32), axis=0)
    piece = piece + exchange(piece, "y", 4, 1)
    piece = piece + exchange(piece, "y", 4, 3)
    scale = 1.0 / math.sqrt(lax.axis_size(DOM) * lax.axis_size("x") * 512)
    piece = (piece * scale).astype(BF16)
    copies = jnp.broadcast_to(piece, (32, 16, 128))
    half = lax.all_to_all(copies, PLANE, 0, 0, tiled=True).reshape(HALF, 128)
    whole = lax.all_gather(half, "c", axis=0, tiled=True)
    weight_grads = whole[:LIVE_ROWS].astype(F32).reshape(LIVE_ROWS * 128)

    grad_node = call(
        finish_kernel, "finish", shape(512, 128, BF16), (local_grad, near_back, far_back, lists)
    )
    return (
        node_out[None],
        edge_out.reshape(1, 4, 128, 128),
        grad_node[None],
        grad_edge.reshape(1, 4, 128, 128),
        weight_grads,
    )


def solution(mesh):
    finer = Mesh(mesh.devices.reshape(4, 8, 2, mesh.shape["grp"]), ("y", "z", "c", "x"))
    by_row = P("x", DOM)
    return jax.shard_map(
        shards,
        mesh=finer,
        in_specs=(by_row,) * 8 + (P(),) * 12,
        out_specs=(by_row,) * 4 + (P(),),
        check_vma=False,
    )
```

time: 131 us -> 78.8 us (0.60)
  other arithmetic: 25.6 us -> 0.88 us
  local copies, waits for them, and re-layouts: 30.6 us -> 11.8 us
  Pallas kernels: 0 us -> 11.3 us
  blocking collectives: 33.6 us -> 23.3 us
  matrix products: 5.45 us -> 0 us
  waiting for transfers between devices: 11.5 us -> 8.87 us
    all_to_all x2 -> x1, blocking collectives: 33.6 us -> 19.3 us  [shards(): tiles = lax.all_to_all(pair, PLANE, 0, 0, tiled=True)]
    scatter-add x4 -> x0, other arithmetic: 12.5 us -> none  [the longest x1 3.53 us: forward_step(): aggregate = aggregate.at[recv_part].add(live_message)]
    pallas_call x0 -> x3, Pallas kernels: none -> 11.3 us  [call(): pl.pallas_call(body, name=name, out_shape=out_shape, in_specs=specs, out_...]
    all_to_all x2 -> x1, waiting for transfers between devices: 8.82 us -> 0.01 us  [shards(): half = lax.all_to_all(copies, PLANE, 0, 0, tiled=True).reshape(HALF, 128)]
    gather x5 -> x0, local copies, waits for them, and re-layouts: 6.7 us -> none  [the longest x2 2.68 us: edge_inputs(): own_nodes[recv_part]]
    all_to_all x2 -> x1, starting transfers between devices: 10.2 us -> 3.89 us  [shards(): half = lax.all_to_all(copies, PLANE, 0, 0, tiled=True).reshape(HALF, 128)]
    ppermute x4 -> x7, waiting for transfers between devices: 2.7 us -> 8.87 us  [the longest x3 3.59 us: exchange(): return lax.ppermute(value, axis, [(j, j ^ flip) for j in range(size)])]
    dot_general x12 -> x0, matrix products: 5.45 us -> none  [the longest x2 2.18 us: mlp_backward(): jnp.dot(second_low, w_second.T, preferred_element_type=jnp.float32)]
  transfers between devices with their start and end apart: 6 -> 8, of which waited for: 2 -> 5; matrix products, arithmetic and copies ran while one was open for 6% -> 0% of each run, Pallas kernels for 0% -> 2%
where the time goes in v1:
time: 78.8 us; the launch traced here: 78.2 us
  blocking collectives  23.3 us (30%)
  starting transfers between devices  20.7 us (26%)
  local copies, waits for them, and re-layouts  11.8 us (15%)
  Pallas kernels  11.3 us (14%)
  waiting for transfers between devices  8.87 us (11%)
  between operations  1.4 us (2%)
  other arithmetic  0.88 us (1%)
    all_to_all x1, blocking collectives, shards(): tiles = lax.all_to_all(pair, PLANE, 0, 0, tiled=True)  19.3 us
    pallas_call x3, Pallas kernels, call(): pl.pallas_call(body, name=name, out_shape=out_shape, in_specs=specs, out_...  11.3 us
    unnamed x42, local copies, waits for them, and re-layouts  11.1 us
    ppermute x1, starting transfers between devices, shards(): near_back = lax.ppermute(near_grad, DOM, near_pairs)  4.38 us
    ppermute x3, starting transfers between devices, exchange(): return lax.ppermute(value, axis, [(j, j ^ flip) for j in range(size)])  4.12 us
    all_gather x1, blocking collectives, shards(): whole = lax.all_gather(half, 'c', axis=0, tiled=True)  3.94 us
    all_to_all x1, starting transfers between devices, shards(): half = lax.all_to_all(copies, PLANE, 0, 0, tiled=True).reshape(HALF, 128)  3.89 us
    ppermute x3, waiting for transfers between devices, exchange(): return lax.ppermute(value, axis, [(j, j ^ flip) for j in range(size)])  3.59 us
  transfers between devices with their start and end apart: 8, of which 5 were waited for; matrix products, arithmetic and copies ran while one was open for 0% of the time, Pallas kernels for 2%

profile of v1, /device:TPU:1, one launch (start us, length us, event | category | flops | bytes accessed | tf_op | source)
XLA Modules:
  0.0 78.2 jit_solution(10506277480384598992)
XLA Ops:
  0.6 0.0 copy-start.1
  0.6 0.0 copy-start.7
  0.7 1.9 %pack.1 = (bf16[128,128]{1,0:T(8,128)(2,1)}, bf16[128,128]{1,0:T(8,128)(2,1)}) custom-call(bf16[512,128]{1,0:T(8,128)(2,1)} %bitcast.26, s32[2,128]{1,0:T(2,128)} %bitcast.44), custom_call_target="tpu_custom_call" | custom-call | flops 1000000 | bytes 1000000 | tf_op jit(solution)/shard_map/pack/pallas_call | solution.py:214
  2.5 3.2 %collective-permute-start = (bf16[128,128]{1,0:T(8,128)(2,1)}, bf16[128,128]{1,0:T(8,128)(2,1)S(1)}, u32[]{:S(2)}, u32[]{:S(2)}) collective-permute-start(bf16[128,128]{1,0:T(8,128)(2,1)} %get-tuple-element.15), channel_id=1, source_target_pairs={{0,4},{4,0},{8,12},{12,8},{16,20},{20,16},{24,28},{28,24},{32,36},... | collective-permute-start | bytes 98312 | tf_op jit(solution)/shard_map/ppermute | solution.py:247
  5.7 1.9 %collective-permute-start.1 = (bf16[128,128]{1,0:T(8,128)(2,1)}, bf16[128,128]{1,0:T(8,128)(2,1)S(1)}, u32[]{:S(2)}, u32[]{:S(2)}) collective-permute-start(bf16[128,128]{1,0:T(8,128)(2,1)} %get-tuple-element.16), channel_id=1, source_target_pairs={{4,8},{12,16},{20,24},{28,32},{36,40},{44,48},{52,56},{60,64},{68,... | collective-permute-start | bytes 98312 | tf_op jit(solution)/shard_map/ppermute | solution.py:246
  8.3 0.0 collective-permute-done.near
  8.3 2.9 %collective-permute-done.1.far = bf16[128,128]{1,0:T(8,128)(2,1)S(1)} collective-permute-done((bf16[128,128]{1,0:T(8,128)(2,1)}, bf16[128,128]{1,0:T(8,128)(2,1)S(1)}, u32[]{:S(2)}, u32[]{:S(2)}) %collective-permute-start.1) | collective-permute-done | bytes 32800 | tf_op jit(solution)/shard_map/ppermute | solution.py:246
  11.1 0.0 copy-start.9
  11.1 0.0 copy-start.11
  11.2 0.0 copy-start.12
  11.2 0.0 copy-done.1
  11.2 0.0 copy-done.7
  11.2 0.7 copy-done.9
  11.8 0.0 copy-done.11
  11.8 0.0 copy-done.12
  11.8 0.0 copy-start.2
  11.8 0.9 %copy-done.2 = bf16[1,4,128,128]{3,2,1,0:T(8,128)(2,1)S(1)} copy-done((bf16[1,4,128,128]{3,2,1,0:T(8,128)(2,1)S(1)}, bf16[1,4,128,128]{3,2,1,0:T(8,128)(2,1)}, u32[]{:S(2)}) %copy-start.2) | copy-done | bytes 131096
  12.7 0.0 copy-start.3
  12.7 0.9 %copy-done.3 = bf16[1,512,128]{2,1,0:T(8,128)(2,1)S(1)} copy-done((bf16[1,512,128]{2,1,0:T(8,128)(2,1)S(1)}, bf16[1,512,128]{2,1,0:T(8,128)(2,1)}, u32[]{:S(2)}) %copy-start.3) | copy-done | bytes 131096
  13.6 0.0 copy-start.4
  13.6 0.9 %copy-done.4 = bf16[1,4,128,128]{3,2,1,0:T(8,128)(2,1)S(1)} copy-done((bf16[1,4,128,128]{3,2,1,0:T(8,128)(2,1)S(1)}, bf16[1,4,128,128]{3,2,1,0:T(8,128)(2,1)}, u32[]{:S(2)}) %copy-start.4) | copy-done | bytes 131096
  14.6 0.0 copy-start.5
  14.6 0.9 %copy-done.5 = bf16[384,128]{1,0:T(8,128)(2,1)S(1)} copy-done((bf16[384,128]{1,0:T(8,128)(2,1)S(1)}, bf16[384,128]{1,0:T(8,128)(2,1)}, u32[]{:S(2)}) %copy-start.5) | copy-done | bytes 98328
  15.4 0.0 copy-start.6
  15.4 0.8 %copy-done.6 = bf16[256,128]{1,0:T(8,128)(2,1)S(1)} copy-done((bf16[256,128]{1,0:T(8,128)(2,1)S(1)}, bf16[256,128]{1,0:T(8,128)(2,1)}, u32[]{:S(2)}) %copy-start.6) | copy-done | bytes 65560
  16.3 0.0 copy-start.8
  16.3 0.8 copy-done.8
  17.0 0.0 copy-start.10
  17.0 0.7 copy-done.10
  17.7 0.0 copy-start.13
  17.7 0.7 copy-done.13
  18.4 0.0 copy-start.14
  18.4 0.7 copy-done.14
  19.0 0.0 copy-start.15
  19.0 0.7 copy-done.15
  19.7 0.0 copy-start.16
  19.7 0.7 copy-done.16
  20.3 0.7 copy-done.17
  21.0 0.0 copy-start.18
  21.0 0.7 copy-done.18
  21.7 7.6 %main.1 = (bf16[512,128]{1,0:T(8,128)(2,1)}, bf16[512,128]{1,0:T(8,128)(2,1)}, bf16[512,128]{1,0:T(8,128)(2,1)}, f32[512,128]{1,0:T(8,128)S(1)}, bf16[128,128]{1...) custom-call(s32[1,1]{1,0:T(1,128)S(6)} %copy.25.count, ...), custom_call_target="tpu_custom_call" | custom-call | flops 2000000000 | bytes 1000000 | tf_op jit(solution)/shard_map/main/pallas_call | solution.py:214
  29.2 0.0 copy-start
  29.2 0.0 collective-permute-start.4
  29.2 1.3 %collective-permute-done.4 = bf16[512,128]{1,0:T(8,128)(2,1)S(1)} collective-permute-done((bf16[512,128]{1,0:T(8,128)(2,1)S(1)}, bf16[512,128]{1,0:T(8,128)(2,1)S(1)}, u32[]{:S(2)}, u32[]{:S(2)}) %collective-permute-start.4) | collective-permute-done | bytes 131104 | tf_op jit(solution)/shard_map/ppermute | solution.py:231
  30.6 0.0 copy-done
  30.6 19.3 %all_to_all.10 = bf16[32,16,128]{2,1,0:T(8,128)(2,1)S(1)} all-to-all(bf16[32,16,128]{2,1,0:T(8,128)(2,1)S(1)} %bitcast.42), channel_id=1, replica_groups=mesh['y'=4,'z'=8,'c'=2,'x'=4] {'z','x'}, dimensions={0} | all-to-all | bytes 262144 | tf_op jit(solution)/shard_map/all_to_all | solution.py:277
  50.0 1.4 %collective-permute-start.5 = (f32[16,128]{1,0:T(8,128)S(1)}, f32[16,128]{1,0:T(8,128)S(1)}, u32[]{:S(2)}, u32[]{:S(2)}) collective-permute-start(f32[16,128]{1,0:T(8,128)S(1)} %convert_reduce_fusion), channel_id=1, source_target_pairs={{0,64},{64,0},{128,192},{192,128},{1,65},{65,1},{129,193},{193,129... | collective-permute-start | bytes 24584 | tf_op jit(solution)/shard_map/ppermute | solution.py:231
  51.4 1.2 %collective-permute-done.5 = f32[16,128]{1,0:T(8,128)S(1)} collective-permute-done((f32[16,128]{1,0:T(8,128)S(1)}, f32[16,128]{1,0:T(8,128)S(1)}, u32[]{:S(2)}, u32[]{:S(2)}) %collective-permute-start.5) | collective-permute-done | bytes 8224 | tf_op jit(solution)/shard_map/ppermute | solution.py:231
  52.6 2.7 %collective-permute-start.6 = (f32[16,128]{1,0:T(8,128)S(1)}, f32[16,128]{1,0:T(8,128)S(1)}, u32[]{:S(2)}, u32[]{:S(2)}) collective-permute-start(f32[16,128]{1,0:T(8,128)S(1)} %add.10), channel_id=1, source_target_pairs={{0,192},{64,128},{128,64},{192,0},{1,193},{65,129},{129,65},{193,1... | collective-permute-start | bytes 24584 | tf_op jit(solution)/shard_map/ppermute | solution.py:231
  55.3 1.0 %collective-permute-done.6 = f32[16,128]{1,0:T(8,128)S(1)} collective-permute-done((f32[16,128]{1,0:T(8,128)S(1)}, f32[16,128]{1,0:T(8,128)S(1)}, u32[]{:S(2)}, u32[]{:S(2)}) %collective-permute-start.6) | collective-permute-done | bytes 8224 | tf_op jit(solution)/shard_map/ppermute | solution.py:231
  56.4 0.7 broadcast_in_dim.11
  57.1 3.9 %all-to-all-start.1 = ((bf16[32,16,128]{2,1,0:T(8,128)(2,1)}), bf16[32,16,128]{2,1,0:T(8,128)(2,1)S(1)}, u32[]{:S(2)}, u32[]{:S(2)}) async-start(bf16[32,16,128]{2,1,0:T(8,128)(2,1)} %broadcast_in_dim.11), calls=%async_computation.1 | async-start | bytes 262144 | tf_op jit(solution)/shard_map/all_to_all | solution.py:284
  60.9 4.4 %collective-permute-start.2 = (bf16[128,128]{1,0:T(8,128)(2,1)S(1)}, bf16[128,128]{1,0:T(8,128)(2,1)S(1)}, u32[]{:S(2)}, u32[]{:S(2)}) collective-permute-start(bf16[128,128]{1,0:T(8,128)(2,1)S(1)} %get-tuple-element.20), channel_id=1, source_target_pairs={{0,4},{4,0},{8,12},{12,8},{16,20},{20,16},{24,28},{28,24},{32,36},... | collective-permute-start | bytes 98312 | tf_op jit(solution)/shard_map/ppermute | solution.py:276
  65.3 3.2 %collective-permute-start.3 = (bf16[128,128]{1,0:T(8,128)(2,1)S(1)}, bf16[128,128]{1,0:T(8,128)(2,1)S(1)}, u32[]{:S(2)}, u32[]{:S(2)}) collective-permute-start(bf16[128,128]{1,0:T(8,128)(2,1)S(1)} %get-tuple-element.21), channel_id=1, source_target_pairs={{4,8},{12,16},{20,24},{28,32},{36,40},{44,48},{52,56},{60,64},{68,... | collective-permute-start | bytes 98312 | tf_op jit(solution)/shard_map/ppermute | solution.py:275
  68.6 0.0 collective-permute-done.2.near
  68.6 0.0 copy-start.19
  68.6 2.4 %collective-permute-done.3.far = bf16[128,128]{1,0:T(8,128)(2,1)S(1)} collective-permute-done((bf16[128,128]{1,0:T(8,128)(2,1)S(1)}, bf16[128,128]{1,0:T(8,128)(2,1)S(1)}, u32[]{:S(2)}, u32[]{:S(2)}) %collective-permute-start.3) | collective-permute-done | bytes 32800 | tf_op jit(solution)/shard_map/ppermute | solution.py:275
  71.0 0.0 copy-start.20
  71.0 0.0 copy-done.19
  71.0 0.6 copy-done.20
  71.6 1.9 %finish.1 = bf16[512,128]{1,0:T(8,128)(2,1)} custom-call(f32[512,128]{1,0:T(8,128)} %copy-done, bf16[128,128]{1,0:T(8,128)(2,1)} %copy-done.19, bf16[128,128]{1,0:T(8,128)(2,1)} %copy-done.20, s32[2,128]{1,0:T(2,128)} %bitcast.45), custom_call_target="tpu_custom_call" | custom-call | flops 1000000 | bytes 1000000 | tf_op jit(solution)/shard_map/finish/pallas_call | solution.py:214
  73.5 0.0 all-to-all-done.1
  73.5 3.9 %all_gather.3 = bf16[1024,128]{1,0:T(8,128)(2,1)S(1)} all-gather(bf16[512,128]{1,0:T(8,128)(2,1)S(1)} %bitcast.41), channel_id=1, replica_groups=mesh['y'=4,'z'=8,'c'=2,'x'=4] {'c'}, dimensions={0}, use_global_device_ids=true | all-gather | bytes 393216 | tf_op jit(solution)/shard_map/all_gather | solution.py:285
  77.4 0.8 %fusion = f32[115712]{0:T(1024)} fusion(bf16[1024,128]{1,0:T(8,128)(2,1)S(1)} %all_gather.3), kind=kLoop, calls=%fused_computation.3 | loop fusion | flops 115712 | bytes 694272 | tf_op jit(solution)/shard_map/reshape | solution.py:286
  (5 shorter events, 0.1 us)
Async XLA Ops:
  0.6 10.5 %copy-start.1 = (bf16[1,512,128]{2,1,0:T(8,128)(2,1)S(1)}, bf16[1,512,128]{2,1,0:T(8,128)(2,1)}, u32[]{:S(2)}) copy-start(bf16[1,512,128]{2,1,0:T(8,128)(2,1)} %param.20) | copy-start | bytes 393220
  0.6 10.5 %copy-start.7 = (bf16[128,128]{1,0:T(8,128)(2,1)S(1)}, bf16[128,128]{1,0:T(8,128)(2,1)}, u32[]{:S(2)}) copy-start(bf16[128,128]{1,0:T(8,128)(2,1)} %ew2.1) | copy-start | bytes 98308
  2.5 5.8 %collective-permute-start = (bf16[128,128]{1,0:T(8,128)(2,1)}, bf16[128,128]{1,0:T(8,128)(2,1)S(1)}, u32[]{:S(2)}, u32[]{:S(2)}) collective-permute-start(bf16[128,128]{1,0:T(8,128)(2,1)} %get-tuple-element.15), channel_id=1, source_target_pairs={{0,4},{4,0},{8,12},{12,8},{16,20},{20,16},{24,28},{28,24},{32,36},... | collective-permute-start | bytes 98312 | tf_op jit(solution)/shard_map/ppermute | solution.py:247
  5.7 5.4 %collective-permute-start.1 = (bf16[128,128]{1,0:T(8,128)(2,1)}, bf16[128,128]{1,0:T(8,128)(2,1)S(1)}, u32[]{:S(2)}, u32[]{:S(2)}) collective-permute-start(bf16[128,128]{1,0:T(8,128)(2,1)} %get-tuple-element.16), channel_id=1, source_target_pairs={{4,8},{12,16},{20,24},{28,32},{36,40},{44,48},{52,56},{60,64},{68,... | collective-permute-start | bytes 98312 | tf_op jit(solution)/shard_map/ppermute | solution.py:246
  11.1 0.7 copy-start.9
  11.1 0.7 copy-start.11
  11.2 0.7 copy-start.12
  11.8 0.9 %copy-start.2 = (bf16[1,4,128,128]{3,2,1,0:T(8,128)(2,1)S(1)}, bf16[1,4,128,128]{3,2,1,0:T(8,128)(2,1)}, u32[]{:S(2)}) copy-start(bf16[1,4,128,128]{3,2,1,0:T(8,128)(2,1)} %param.21) | copy-start | bytes 393220
  12.7 0.9 %copy-start.3 = (bf16[1,512,128]{2,1,0:T(8,128)(2,1)S(1)}, bf16[1,512,128]{2,1,0:T(8,128)(2,1)}, u32[]{:S(2)}) copy-start(bf16[1,512,128]{2,1,0:T(8,128)(2,1)} %param.26) | copy-start | bytes 393220
  13.6 0.9 %copy-start.4 = (bf16[1,4,128,128]{3,2,1,0:T(8,128)(2,1)S(1)}, bf16[1,4,128,128]{3,2,1,0:T(8,128)(2,1)}, u32[]{:S(2)}) copy-start(bf16[1,4,128,128]{3,2,1,0:T(8,128)(2,1)} %param.27) | copy-start | bytes 393220
  14.6 0.9 %copy-start.5 = (bf16[384,128]{1,0:T(8,128)(2,1)S(1)}, bf16[384,128]{1,0:T(8,128)(2,1)}, u32[]{:S(2)}) copy-start(bf16[384,128]{1,0:T(8,128)(2,1)} %ew1.1) | copy-start | bytes 294916
  15.4 0.8 %copy-start.6 = (bf16[256,128]{1,0:T(8,128)(2,1)S(1)}, bf16[256,128]{1,0:T(8,128)(2,1)}, u32[]{:S(2)}) copy-start(bf16[256,128]{1,0:T(8,128)(2,1)} %nw1.1) | copy-start | bytes 196612
  16.3 0.8 copy-start.8
  17.0 0.7 copy-start.10
  17.7 0.7 copy-start.13
  18.4 0.7 copy-start.14
  19.0 0.7 copy-start.15
  19.7 0.7 copy-start.16
  20.3 0.7 copy-start.17
  21.0 0.7 copy-start.18
  29.2 1.4 %copy-start = (f32[512,128]{1,0:T(8,128)}, f32[512,128]{1,0:T(8,128)S(1)}, u32[]{:S(2)}) copy-start(f32[512,128]{1,0:T(8,128)S(1)} %get-tuple-element.19.local_grad) | copy-start | bytes 786436
  29.2 1.3 %collective-permute-start.4 = (bf16[512,128]{1,0:T(8,128)(2,1)S(1)}, bf16[512,128]{1,0:T(8,128)(2,1)S(1)}, u32[]{:S(2)}, u32[]{:S(2)}) collective-permute-start(bf16[512,128]{1,0:T(8,128)(2,1)S(1)} %get-tuple-element.24), channel_id=1, source_target_pairs={{0,4},{4,0},{1,5},{5,1},{2,6},{6,2},{3,7},{7,3},{8,12},{12,8},{9,1... | collective-permute-start | bytes 393224 | tf_op jit(solution)/shard_map/ppermute | solution.py:231
  50.0 2.6 %collective-permute-start.5 = (f32[16,128]{1,0:T(8,128)S(1)}, f32[16,128]{1,0:T(8,128)S(1)}, u32[]{:S(2)}, u32[]{:S(2)}) collective-permute-start(f32[16,128]{1,0:T(8,128)S(1)} %convert_reduce_fusion), channel_id=1, source_target_pairs={{0,64},{64,0},{128,192},{192,128},{1,65},{65,1},{129,193},{193,129... | collective-permute-start | bytes 24584 | tf_op jit(solution)/shard_map/ppermute | solution.py:231
  52.6 3.8 %collective-permute-start.6 = (f32[16,128]{1,0:T(8,128)S(1)}, f32[16,128]{1,0:T(8,128)S(1)}, u32[]{:S(2)}, u32[]{:S(2)}) collective-permute-start(f32[16,128]{1,0:T(8,128)S(1)} %add.10), channel_id=1, source_target_pairs={{0,192},{64,128},{128,64},{192,0},{1,193},{65,129},{129,65},{193,1... | collective-permute-start | bytes 24584 | tf_op jit(solution)/shard_map/ppermute | solution.py:231
  57.1 16.4 %all-to-all-start.1 = ((bf16[32,16,128]{2,1,0:T(8,128)(2,1)}), bf16[32,16,128]{2,1,0:T(8,128)(2,1)S(1)}, u32[]{:S(2)}, u32[]{:S(2)}) async-start(bf16[32,16,128]{2,1,0:T(8,128)(2,1)} %broadcast_in_dim.11), calls=%async_computation.1 | async-start | bytes 262144 | tf_op jit(solution)/shard_map/all_to_all | solution.py:284
  60.9 7.6 %collective-permute-start.2 = (bf16[128,128]{1,0:T(8,128)(2,1)S(1)}, bf16[128,128]{1,0:T(8,128)(2,1)S(1)}, u32[]{:S(2)}, u32[]{:S(2)}) collective-permute-start(bf16[128,128]{1,0:T(8,128)(2,1)S(1)} %get-tuple-element.20), channel_id=1, source_target_pairs={{0,4},{4,0},{8,12},{12,8},{16,20},{20,16},{24,28},{28,24},{32,36},... | collective-permute-start | bytes 98312 | tf_op jit(solution)/shard_map/ppermute | solution.py:276
  65.3 5.7 %collective-permute-start.3 = (bf16[128,128]{1,0:T(8,128)(2,1)S(1)}, bf16[128,128]{1,0:T(8,128)(2,1)S(1)}, u32[]{:S(2)}, u32[]{:S(2)}) collective-permute-start(bf16[128,128]{1,0:T(8,128)(2,1)S(1)} %get-tuple-element.21), channel_id=1, source_target_pairs={{4,8},{12,16},{20,24},{28,32},{36,40},{44,48},{52,56},{60,64},{68,... | collective-permute-start | bytes 98312 | tf_op jit(solution)/shard_map/ppermute | solution.py:275
  68.6 2.4 %copy-start.19 = (bf16[128,128]{1,0:T(8,128)(2,1)}, bf16[128,128]{1,0:T(8,128)(2,1)S(1)}, u32[]{:S(2)}) copy-start(bf16[128,128]{1,0:T(8,128)(2,1)S(1)} %collective-permute-done.2.near) | copy-start | bytes 98308
  71.0 0.6 copy-start.20

commit v2 on v1

--- a/solution.py
+++ b/solution.py
@@ -1,3 +1,4 @@
+import functools
 import math
 
 import jax
@@ -9,15 +10,17 @@
 from jax.sharding import PartitionSpec as P
 
 DOM = ("y", "z", "c")
-PLANE = ("z", "x")
+COLUMN = ("z", "c")
+PLANE = ("y", "x")
 EPSILON = 1e-05
 F32 = jnp.float32
 BF16 = jnp.bfloat16
 ROWS = 1024
-HALF = 512
 LIVE_ROWS = 904
+SMALL = 8 << 20
 VMEM = pl.BlockSpec(memory_space=pltpu.VMEM)
 SMEM = pl.BlockSpec(memory_space=pltpu.SMEM)
+HBM = pl.BlockSpec(memory_space=pltpu.HBM)
 
 
 def dot(left, right):
@@ -58,7 +61,15 @@
     return value[:, :128] + value[:, 128:]
 
 
-def pack_kernel(nodes, lists, near, far):
+def pack_kernel(nodes_in, lists_in, near, far, nodes, lists, arrive):
+    loads = [
+        pltpu.make_async_copy(nodes_in, nodes, arrive.at[0]),
+        pltpu.make_async_copy(lists_in, lists, arrive.at[1]),
+    ]
+    for load in loads:
+        load.start()
+    for load in loads[::-1]:
+        load.wait()
     core = lax.axis_index("c")
     near[...] = dot(pick_rows(lists[pl.ds(1 - core, 1), :], 512), nodes[...]).astype(BF16)
     far[...] = dot(pick_rows(lists[pl.ds(core, 1), :], 512), nodes[...]).astype(BF16)
@@ -89,15 +100,32 @@
     return jnp.sum(value, axis=0, keepdims=True)
 
 
-def main_kernel(
-    count, nodes, near, far, edges, senders, receivers, node_cot, edge_cot,
-    ew1, eb1, ew2, eb2, egain, eshift, nw1, nb1, nw2, nb2, ngain, nshift,
-    node_out, edge_out, grad_edge, local_grad, near_grad, far_grad, keep, send,
-    table, pick_recv, place_recv, place_send, messages, inputs, hidden, slope, normed, inverse,
-    spread, dxs, dxr, first_low, second_low, node_inputs, node_hidden, node_first, node_second, grads,
-):
+def main_kernel(count, near, far, *refs):
+    sources, refs = refs[:18], refs[18:]
+    (node_out, edge_out, grad_edge, local_grad, near_grad, far_grad, send), refs = refs[:7], refs[7:]
+    landed, refs = refs[:18], refs[18:]
+    left, refs = refs[:3], refs[3:]
+    (
+        table, pick_recv, place_recv, place_send, messages, inputs, hidden, slope, normed, inverse,
+        spread, dxs, dxr, first_low, second_low, node_inputs, node_hidden, node_first, node_second, grads,
+        arrive, leave,
+    ) = refs
+    loads = [pltpu.make_async_copy(a, b, arrive.at[k]) for k, (a, b) in enumerate(zip(sources, landed))]
+    stores = [
+        pltpu.make_async_copy(a, b, leave.at[k])
+        for k, (a, b) in enumerate(zip(left, (edge_out, node_out, grad_edge)))
+    ]
+    for load in loads:
+        load.start()
+    (
+        nodes, senders, receivers, edges, ew1, eb1, ew2, eb2, egain, eshift,
+        nw1, nb1, nw2, nb2, ngain, nshift, node_cot, edge_cot,
+    ) = landed
+    edge_left, node_left, grad_left = left
     core = lax.axis_index("c")
     live_blocks = count[0, 0]
+    for load in loads[:10]:
+        load.wait()
     table[pl.ds(0, 512), :] = nodes[...]
     table[pl.ds(pl.multiple_of(640 - 128 * core, 128), 128), :] = near[...]
     table[pl.ds(pl.multiple_of(512 + 128 * core, 128), 128), :] = far[...]
@@ -124,9 +152,12 @@
         normed[rows, :] = n
         inverse[rows, :] = inv
         message = (n * egain[...] + eshift[...]) * live
-        edge_out[rows, :] = (own.astype(F32) + message).astype(BF16)
+        edge_left[rows, :] = (own.astype(F32) + message).astype(BF16)
         messages[rows, :] = split(message)
 
+    stores[0].start()
+    for load in loads[10:]:
+        load.wait()
     sums = [jnp.zeros((8, 128), F32) for _ in range(8)]
     for b in range(4):
         rows = pl.ds(b * 128, 128)
@@ -139,7 +170,7 @@
         low = (first * sigmoid).astype(BF16)
         node_hidden[rows, :] = low
         n, inv = norm_forward(dot(low, nw2[...]) + nb2[...])
-        node_out[rows, :] = (own.astype(F32) + (n * ngain[...] + nshift[...])).astype(BF16)
+        node_left[rows, :] = (own.astype(F32) + (n * ngain[...] + nshift[...])).astype(BF16)
         cot = node_cot[rows, :].astype(F32)
         g2 = norm_backward(cot, n, inv, ngain[...])
         g2_low = g2.astype(BF16)
@@ -152,6 +183,7 @@
         spread[rows, :] = split(back[:, 128:])
         for k, piece in enumerate((g1, g2, cot * n, cot)):
             sums[4 + k] += partial_sum(piece)
+    stores[1].start()
 
     for b in range(4):
         rows = pl.ds(b * 128, 128)
@@ -166,11 +198,12 @@
         first_low[rows, :] = g1_low
         second_low[rows, :] = g2_low
         back = dot_nt(g1_low, ew1[...])
-        grad_edge[rows, :] = (edge_grad + back[:, :128]).astype(BF16)
+        grad_left[rows, :] = (edge_grad + back[:, :128]).astype(BF16)
         dxs[rows, :] = split(back[:, 128:256])
         dxr[rows, :] = split(back[:, 256:])
         for k, piece in enumerate((g1, g2, cot * n, cot)):
             sums[k] += partial_sum(piece)
+    stores[2].start()
 
     lower = joined(dot(place_send[512:640, :], dxs[...])).astype(BF16)
     upper = joined(dot(place_send[640:768, :], dxs[...])).astype(BF16)
@@ -191,13 +224,23 @@
     grads[902:903, :] = total(sums[6])
     grads[903:904, :] = total(sums[7])
     grads[904:1024, :] = jnp.zeros((120, 128), F32)
-    keep[...] = grads[pl.ds(pl.multiple_of(core * HALF, HALF), HALF), :]
-    send[...] = grads[pl.ds(pl.multiple_of((1 - core) * HALF, HALF), HALF), :].astype(BF16)
+    send[...] = grads[...].astype(BF16)
 
     for b in range(4):
         rows = pl.ds(b * 128, 128)
         both = dot(place_send[rows, :], dxs[...]) + dot(place_recv[rows, :], dxr[...])
         local_grad[rows, :] += joined(both)
+    for store in stores:
+        store.wait()
+
+
+def fold_kernel(scale, tiles, copies):
+    summed = tiles[0].astype(F32)
+    for k in range(1, 16):
+        summed += tiles[k].astype(F32)
+    low = (summed * scale).astype(BF16)
+    for k in range(16):
+        copies[k] = low
 
 
 def finish_kernel(local_grad, near, far, lists, out):
@@ -207,31 +250,27 @@
     out[...] = (local_grad[...] + added).astype(BF16)
 
 
-def call(body, name, out_shape, operands, scratch=(), flops=1000000, smem_first=False, vmem=None):
-    specs = [VMEM] * len(operands)
-    if smem_first:
-        specs[0] = SMEM
+def call(body, out_shape, operands, in_specs=None, out_specs=None, scratch=(), flops=1000000, vmem=None):
     return pl.pallas_call(
         body,
-        name=name,
         out_shape=out_shape,
-        in_specs=specs,
-        out_specs=jax.tree.map(lambda _: VMEM, out_shape),
+        in_specs=in_specs or [VMEM] * len(operands),
+        out_specs=out_specs or jax.tree.map(lambda _: VMEM, out_shape),
         scratch_shapes=scratch,
         compiler_params=pltpu.CompilerParams(vmem_limit_bytes=vmem),
         cost_estimate=pl.CostEstimate(flops=flops, bytes_accessed=1000000, transcendentals=0),
     )(*operands)
 
 
+def in_hbm(value):
+    return pltpu.with_memory_space_constraint(value, pltpu.HBM)
+
+
 def shape(rows, width, kind):
     return jax.ShapeDtypeStruct((rows, width), kind)
 
 
-def exchange(value, axis, size, flip):
-    return lax.ppermute(value, axis, [(j, j ^ flip) for j in range(size)])
-
-
-def shards(
+def layer(
     nodes, edges, senders, receivers, block_count, send_rows, node_cot, edge_cot,
     edge_w1, edge_b1, edge_w2, edge_b2, edge_gain, edge_shift,
     node_w1, node_b1, node_w2, node_b2, node_gain, node_shift,
@@ -242,52 +281,56 @@
     near_pairs = [(j, j ^ 1) for j in range(64)]
     far_pairs = [(j, j + 1) for j in range(1, 63, 2)] + [(j + 1, j) for j in range(1, 63, 2)]
 
-    near, far = call(pack_kernel, "pack", (shape(128, 128, BF16),) * 2, (own_nodes, lists))
+    near, far = call(
+        pack_kernel, (shape(128, 128, BF16),) * 2, (in_hbm(own_nodes), in_hbm(lists)), [HBM] * 2,
+        scratch=[
+            pltpu.VMEM((512, 128), BF16), pltpu.VMEM((2, 128), jnp.int32), pltpu.SemaphoreType.DMA((2,))
+        ],
+        vmem=SMALL,
+    )
     far = lax.ppermute(far, DOM, far_pairs)
     near = lax.ppermute(near, DOM, near_pairs)
 
-    operands = (
-        block_count, own_nodes, near, far, edges[0].reshape(512, 128), senders[0], receivers[0],
-        node_cot[0], edge_cot[0].reshape(512, 128),
+    sources = (
+        own_nodes, senders[0], receivers[0], edges[0].reshape(512, 128),
         edge_w1, line(edge_b1), edge_w2, line(edge_b2), line(edge_gain), line(edge_shift),
         node_w1, line(node_b1), node_w2, line(node_b2), line(node_gain), line(node_shift),
+        node_cot[0], edge_cot[0].reshape(512, 128),
     )
     outs = (
         shape(512, 128, BF16), shape(512, 128, BF16), shape(512, 128, BF16), shape(512, 128, F32),
-        shape(128, 128, BF16), shape(128, 128, BF16), shape(HALF, 128, F32), shape(HALF, 128, BF16),
-    )
-    scratch = [
+        shape(128, 128, BF16), shape(128, 128, BF16), shape(ROWS, 128, BF16),
+    )
+    scratch = [pltpu.VMEM(source.shape, source.dtype) for source in sources]
+    scratch += [
         pltpu.VMEM(dims, kind)
         for dims, kind in (
+            ((512, 128), BF16), ((512, 128), BF16), ((512, 128), BF16),
             ((768, 128), BF16), ((512, 512), BF16), ((512, 512), BF16), ((768, 512), BF16),
             ((512, 256), BF16), ((512, 384), BF16), ((512, 128), BF16), ((512, 128), F32),
             ((512, 128), F32), ((512, 1), F32), ((512, 256), BF16), ((512, 256), BF16), ((512, 256), BF16),
             ((512, 128), BF16), ((512, 128), BF16), ((512, 256), BF16), ((512, 128), BF16),
             ((512, 128), BF16), ((512, 128), BF16), ((ROWS, 128), F32),
         )
-    ]
-    node_out, edge_out, grad_edge, local_grad, near_grad, far_grad, keep, send = call(
-        main_kernel, "main", outs, operands, scratch, flops=2000000000, smem_first=True, vmem=24 << 20
-    )
-
-    arrived = exchange(send, "c", 2, 1)
-    pair = (keep + arrived.astype(F32)).astype(BF16).reshape(32, 16, 128)
+    ] + [pltpu.SemaphoreType.DMA((18,)), pltpu.SemaphoreType.DMA((3,))]
+    node_out, edge_out, grad_edge, local_grad, near_grad, far_grad, send = call(
+        main_kernel, outs, (block_count, near, far)
+        + tuple(in_hbm(source) for source in sources),
+        [SMEM, VMEM, VMEM] + [HBM] * 18, (HBM,) * 3 + (VMEM,) * 4, scratch, 2000000000, 24 << 20,
+    )
+
     far_back = lax.ppermute(far_grad, DOM, far_pairs)
     near_back = lax.ppermute(near_grad, DOM, near_pairs)
-    tiles = lax.all_to_all(pair, PLANE, 0, 0, tiled=True)
-    piece = jnp.sum(tiles.astype(F32), axis=0)
-    piece = piece + exchange(piece, "y", 4, 1)
-    piece = piece + exchange(piece, "y", 4, 3)
     scale = 1.0 / math.sqrt(lax.axis_size(DOM) * lax.axis_size("x") * 512)
-    piece = (piece * scale).astype(BF16)
-    copies = jnp.broadcast_to(piece, (32, 16, 128))
-    half = lax.all_to_all(copies, PLANE, 0, 0, tiled=True).reshape(HALF, 128)
-    whole = lax.all_gather(half, "c", axis=0, tiled=True)
+    stack = jax.ShapeDtypeStruct((16, 64, 128), BF16)
+    tiles = lax.all_to_all(send.reshape(16, 64, 128), COLUMN, 0, 0, tiled=True)
+    copies = call(functools.partial(fold_kernel, 1.0), stack, (tiles,), vmem=SMALL)
+    tiles = lax.all_to_all(copies, PLANE, 0, 0, tiled=True)
+    copies = call(functools.partial(fold_kernel, scale), stack, (tiles,), vmem=SMALL)
+    whole = lax.all_to_all(copies, COLUMN, 0, 0, tiled=True).reshape(ROWS, 128)
     weight_grads = whole[:LIVE_ROWS].astype(F32).reshape(LIVE_ROWS * 128)
 
-    grad_node = call(
-        finish_kernel, "finish", shape(512, 128, BF16), (local_grad, near_back, far_back, lists)
-    )
+    grad_node = call(finish_kernel, shape(512, 128, BF16), (local_grad, near_back, far_back, lists), vmem=SMALL)
     return (
         node_out[None],
         edge_out.reshape(1, 4, 128, 128),
@@ -301,7 +344,7 @@
     finer = Mesh(mesh.devices.reshape(4, 8, 2, mesh.shape["grp"]), ("y", "z", "c", "x"))
     by_row = P("x", DOM)
     return jax.shard_map(
-        shards,
+        layer,
         mesh=finer,
         in_specs=(by_row,) * 8 + (P(),) * 12,
         out_specs=(by_row,) * 4 + (P(),),

time: 78.8 us -> 72.1 us (0.915)
  local copies, waits for them, and re-layouts: 11.8 us -> 0.01 us
  blocking collectives: 23.3 us -> 34.5 us
  starting transfers between devices: 20.7 us -> 13.4 us
  waiting for transfers between devices: 8.87 us -> 9.98 us
    all_to_all x1 -> x2, blocking collectives: 19.3 us -> 34.5 us  [the longest x1 19.4 us: layer(): tiles = lax.all_to_all(send.reshape(16, 64, 128), COLUMN, 0, 0, tiled=True)]
    unnamed x42 -> x2, local copies, waits for them, and re-layouts: 11.1 us -> 0.01 us
    ppermute x7 -> x4, starting transfers between devices: 16.8 us -> 8.98 us  [the longest x1 3.48 us: layer(): far_back = lax.ppermute(far_grad, DOM, far_pairs)]
    all_gather x1 -> x0, blocking collectives: 3.94 us -> none  [shards(): whole = lax.all_gather(half, 'c', axis=0, tiled=True)]
    all_to_all x1, waiting for transfers between devices: 0.01 us -> 2.36 us  [layer(): whole = lax.all_to_all(copies, COLUMN, 0, 0, tiled=True).reshape(ROWS, 128)]
    ppermute x7 -> x4, waiting for transfers between devices: 8.87 us -> 7.62 us  [the longest x1 4.97 us: layer(): far_back = lax.ppermute(far_grad, DOM, far_pairs)]
    pallas_call x3 -> x5, Pallas kernels: 11.3 us -> 11.7 us  [call(): pl.pallas_call(body, out_shape=out_shape, in_specs=in_specs or [VMEM] * l...]
  transfers between devices with their start and end apart: 8 -> 5, of which waited for: 5 -> 3; matrix products, arithmetic and copies ran while one was open for 0% -> 0% of each run, Pallas kernels for 2% -> 1%
where the time goes in v2:
time: 72.1 us; the launch traced here: 71.7 us
  blocking collectives  34.5 us (48%)
  starting transfers between devices  13.4 us (19%)
  Pallas kernels  11.7 us (16%)
  waiting for transfers between devices  9.98 us (14%)
  between operations  1.34 us (2%)
  other arithmetic  0.8 us (1%)
    all_to_all x1, blocking collectives, layer(): tiles = lax.all_to_all(send.reshape(16, 64, 128), COLUMN, 0, 0, tiled=True)  19.4 us
    all_to_all x1, blocking collectives, layer(): tiles = lax.all_to_all(copies, PLANE, 0, 0, tiled=True)  15.1 us
    pallas_call x5, Pallas kernels, call(): pl.pallas_call(body, out_shape=out_shape, in_specs=in_specs or [VMEM] * l...  11.7 us
    ppermute x1, waiting for transfers between devices, layer(): far_back = lax.ppermute(far_grad, DOM, far_pairs)  4.97 us
    all_to_all x1, starting transfers between devices, layer(): whole = lax.all_to_all(copies, COLUMN, 0, 0, tiled=True).reshape(ROWS, 128)  4.41 us
    ppermute x1, starting transfers between devices, layer(): far_back = lax.ppermute(far_grad, DOM, far_pairs)  3.48 us
    ppermute x1, starting transfers between devices, layer(): near = lax.ppermute(near, DOM, near_pairs)  3.29 us
    ppermute x1, waiting for transfers between devices, layer(): far = lax.ppermute(far, DOM, far_pairs)  2.65 us
  transfers between devices with their start and end apart: 5, of which 3 were waited for; matrix products, arithmetic and copies ran while one was open for 0% of the time, Pallas kernels for 1%

profile of v2, /device:TPU:1, one launch (start us, length us, event | category | flops | bytes accessed | tf_op | source)
XLA Modules:
  0.0 71.7 jit_solution(2466020763136926959)
XLA Ops:
  0.6 1.2 %shard_map.227 = (bf16[128,128]{1,0:T(8,128)(2,1)S(1)}, bf16[128,128]{1,0:T(8,128)(2,1)S(1)}) custom-call(bf16[512,128]{1,0:T(8,128)(2,1)} %bitcast.31, s32[2,128]{1,0:T(2,128)} %bitcast.27), custom_call_target="tpu_custom_call" | custom-call | flops 1000000 | bytes 1000000 | tf_op jit(solution)/shard_map/pallas_call | solution.py:254
  1.9 3.3 %collective-permute-start = (bf16[128,128]{1,0:T(8,128)(2,1)S(1)}, bf16[128,128]{1,0:T(8,128)(2,1)S(1)}, u32[]{:S(2)}, u32[]{:S(2)}) collective-permute-start(bf16[128,128]{1,0:T(8,128)(2,1)S(1)} %get-tuple-element.14), channel_id=1, source_target_pairs={{0,4},{4,0},{8,12},{12,8},{16,20},{20,16},{24,28},{28,24},{32,36},... | collective-permute-start | bytes 98312 | tf_op jit(solution)/shard_map/ppermute | solution.py:292
  5.1 1.9 %collective-permute-start.1 = (bf16[128,128]{1,0:T(8,128)(2,1)S(1)}, bf16[128,128]{1,0:T(8,128)(2,1)S(1)}, u32[]{:S(2)}, u32[]{:S(2)}) collective-permute-start(bf16[128,128]{1,0:T(8,128)(2,1)S(1)} %get-tuple-element.15), channel_id=1, source_target_pairs={{4,8},{12,16},{20,24},{28,32},{36,40},{44,48},{52,56},{60,64},{68,... | collective-permute-start | bytes 98312 | tf_op jit(solution)/shard_map/ppermute | solution.py:291
  7.7 0.0 collective-permute-done.near
  7.7 2.6 %collective-permute-done.1.far = bf16[128,128]{1,0:T(8,128)(2,1)S(1)} collective-permute-done((bf16[128,128]{1,0:T(8,128)(2,1)S(1)}, bf16[128,128]{1,0:T(8,128)(2,1)S(1)}, u32[]{:S(2)}, u32[]{:S(2)}) %collective-permute-start.1) | collective-permute-done | bytes 32800 | tf_op jit(solution)/shard_map/ppermute | solution.py:291
  10.4 8.8 %shard_map.228 = (bf16[512,128]{1,0:T(8,128)(2,1)}, bf16[512,128]{1,0:T(8,128)(2,1)}, bf16[512,128]{1,0:T(8,128)(2,1)}, f32[512,128]{1,0:T(8,128)S(1)}, bf16[128...) custom-call(s32[1,1]{1,0:T(1,128)S(6)} %copy.25.count, ...), custom_call_target="tpu_custom_call" | custom-call | flops 2000000000 | bytes 1000000 | tf_op jit(solution)/shard_map/pallas_call | solution.py:254
  19.2 19.4 %all_to_all.15.tiles = bf16[16,64,128]{2,1,0:T(8,128)(2,1)S(1)} all-to-all(bf16[16,64,128]{2,1,0:T(8,128)(2,1)S(1)} %bitcast.26), channel_id=1, replica_groups=mesh['y'=4,'z'=8,'c'=2,'x'=4] {'z','c'}, dimensions={0} | all-to-all | bytes 524288 | tf_op jit(solution)/shard_map/all_to_all | solution.py:326
  38.6 15.1 %all_to_all.16.tiles = bf16[16,64,128]{2,1,0:T(8,128)(2,1)S(1)} all-to-all(bf16[16,64,128]{2,1,0:T(8,128)(2,1)S(1)} %shard_map.230), channel_id=1, replica_groups=mesh['y'=4,'z'=8,'c'=2,'x'=4] {'y','x'}, dimensions={0} | all-to-all | bytes 524288 | tf_op jit(solution)/shard_map/all_to_all | solution.py:328
  53.7 0.8 %shard_map.231 = bf16[16,64,128]{2,1,0:T(8,128)(2,1)} custom-call(bf16[16,64,128]{2,1,0:T(8,128)(2,1)S(1)} %all_to_all.16.tiles), custom_call_target="tpu_custom_call" | custom-call | flops 1000000 | bytes 1000000 | tf_op jit(solution)/shard_map/pallas_call | solution.py:254
  54.5 4.4 %all-to-all-start.2 = ((bf16[16,64,128]{2,1,0:T(8,128)(2,1)}), bf16[16,64,128]{2,1,0:T(8,128)(2,1)S(1)}, u32[]{:S(2)}, u32[]{:S(2)}) async-start(bf16[16,64,128]{2,1,0:T(8,128)(2,1)} %shard_map.231), calls=%async_computation.2 | async-start | bytes 524288 | tf_op jit(solution)/shard_map/all_to_all | solution.py:330
  58.9 0.3 collective-permute-start.2
  59.2 0.0 copy-start
  59.2 3.5 %collective-permute-start.3 = (bf16[128,128]{1,0:T(8,128)(2,1)S(1)}, bf16[128,128]{1,0:T(8,128)(2,1)S(1)}, u32[]{:S(2)}, u32[]{:S(2)}) collective-permute-start(bf16[128,128]{1,0:T(8,128)(2,1)S(1)} %get-tuple-element.20), channel_id=1, source_target_pairs={{4,8},{12,16},{20,24},{28,32},{36,40},{44,48},{52,56},{60,64},{68,... | collective-permute-start | bytes 98312 | tf_op jit(solution)/shard_map/ppermute | solution.py:322
  62.7 0.0 collective-permute-done.2.near
  62.7 5.0 %collective-permute-done.3.far = bf16[128,128]{1,0:T(8,128)(2,1)S(1)} collective-permute-done((bf16[128,128]{1,0:T(8,128)(2,1)S(1)}, bf16[128,128]{1,0:T(8,128)(2,1)S(1)}, u32[]{:S(2)}, u32[]{:S(2)}) %collective-permute-start.3) | collective-permute-done | bytes 32800 | tf_op jit(solution)/shard_map/ppermute | solution.py:322
  67.7 0.0 copy-done
  67.7 0.9 %shard_map.229 = bf16[512,128]{1,0:T(8,128)(2,1)} custom-call(f32[512,128]{1,0:T(8,128)S(1)} %get-tuple-element.18.local_grad, bf16[128,128]{1,0:T(8,128)(2,1)S(1)} %collective-permute-done.2.near, bf16[128,128]{1,0:T(8,128)(2,1)S(1)} %collective-permute-done.3.far, s32[2,128]{1,0:T(2,128)S(1)} %bitcast.28), custom_call_target="tpu_custom_call" | custom-call | flops 1000000 | bytes 1000000 | tf_op jit(solution)/shard_map/pallas_call | solution.py:254
  68.6 2.4 %all-to-all-done.2 = bf16[16,64,128]{2,1,0:T(8,128)(2,1)S(1)} async-done(((bf16[16,64,128]{2,1,0:T(8,128)(2,1)}), bf16[16,64,128]{2,1,0:T(8,128)(2,1)S(1)}, u32[]{:S(2)}, u32[]{:S(2)}) %all-to-all-start.2) | async-done | bytes 262176 | tf_op jit(solution)/shard_map/all_to_all | solution.py:330
  70.9 0.8 %fusion = f32[115712]{0:T(1024)} fusion(bf16[1024,128]{1,0:T(8,128)(2,1)S(1)} %bitcast.29), kind=kLoop, calls=%fused_computation.1 | loop fusion | flops 115712 | bytes 694272 | tf_op jit(solution)/shard_map/reshape | solution.py:331
  (1 shorter events, 0.0 us)
Async XLA Ops:
  1.9 5.9 %collective-permute-start = (bf16[128,128]{1,0:T(8,128)(2,1)S(1)}, bf16[128,128]{1,0:T(8,128)(2,1)S(1)}, u32[]{:S(2)}, u32[]{:S(2)}) collective-permute-start(bf16[128,128]{1,0:T(8,128)(2,1)S(1)} %get-tuple-element.14), channel_id=1, source_target_pairs={{0,4},{4,0},{8,12},{12,8},{16,20},{20,16},{24,28},{28,24},{32,36},... | collective-permute-start | bytes 98312 | tf_op jit(solution)/shard_map/ppermute | solution.py:292
  5.1 5.2 %collective-permute-start.1 = (bf16[128,128]{1,0:T(8,128)(2,1)S(1)}, bf16[128,128]{1,0:T(8,128)(2,1)S(1)}, u32[]{:S(2)}, u32[]{:S(2)}) collective-permute-start(bf16[128,128]{1,0:T(8,128)(2,1)S(1)} %get-tuple-element.15), channel_id=1, source_target_pairs={{4,8},{12,16},{20,24},{28,32},{36,40},{44,48},{52,56},{60,64},{68,... | collective-permute-start | bytes 98312 | tf_op jit(solution)/shard_map/ppermute | solution.py:291
  54.5 16.4 %all-to-all-start.2 = ((bf16[16,64,128]{2,1,0:T(8,128)(2,1)}), bf16[16,64,128]{2,1,0:T(8,128)(2,1)S(1)}, u32[]{:S(2)}, u32[]{:S(2)}) async-start(bf16[16,64,128]{2,1,0:T(8,128)(2,1)} %shard_map.231), calls=%async_computation.2 | async-start | bytes 524288 | tf_op jit(solution)/shard_map/all_to_all | solution.py:330
  58.9 3.8 %collective-permute-start.2 = (bf16[128,128]{1,0:T(8,128)(2,1)S(1)}, bf16[128,128]{1,0:T(8,128)(2,1)S(1)}, u32[]{:S(2)}, u32[]{:S(2)}) collective-permute-start(bf16[128,128]{1,0:T(8,128)(2,1)S(1)} %get-tuple-element.19), channel_id=1, source_target_pairs={{0,4},{4,0},{8,12},{12,8},{16,20},{20,16},{24,28},{28,24},{32,36},... | collective-permute-start | bytes 98312 | tf_op jit(solution)/shard_map/ppermute | solution.py:323
  59.2 8.5 %copy-start = (s32[1,1,2,128]{3,2,1,0:T(2,128)S(1)}, s32[1,1,2,128]{3,2,1,0:T(2,128)}, u32[]{:S(2)}) copy-start(s32[1,1,2,128]{3,2,1,0:T(2,128)} %param.25) | copy-start | bytes 3076
  59.2 8.5 %collective-permute-start.3 = (bf16[128,128]{1,0:T(8,128)(2,1)S(1)}, bf16[128,128]{1,0:T(8,128)(2,1)S(1)}, u32[]{:S(2)}, u32[]{:S(2)}) collective-permute-start(bf16[128,128]{1,0:T(8,128)(2,1)S(1)} %get-tuple-element.20), channel_id=1, source_target_pairs={{4,8},{12,16},{20,24},{28,32},{36,40},{44,48},{52,56},{60,64},{68,... | collective-permute-start | bytes 98312 | tf_op jit(solution)/shard_map/ppermute | solution.py:322

commit v3 on v2

--- a/solution.py
+++ b/solution.py
@@ -10,8 +10,8 @@
 from jax.sharding import PartitionSpec as P
 
 DOM = ("y", "z", "c")
-COLUMN = ("z", "c")
-PLANE = ("y", "x")
+PLANE = ("c", "y", "x")
+COLUMN = ("z",)
 EPSILON = 1e-05
 F32 = jnp.float32
 BF16 = jnp.bfloat16
@@ -236,10 +236,10 @@
 
 def fold_kernel(scale, tiles, copies):
     summed = tiles[0].astype(F32)
-    for k in range(1, 16):
+    for k in range(1, tiles.shape[0]):
         summed += tiles[k].astype(F32)
     low = (summed * scale).astype(BF16)
-    for k in range(16):
+    for k in range(copies.shape[0]):
         copies[k] = low
 
 
@@ -250,9 +250,10 @@
     out[...] = (local_grad[...] + added).astype(BF16)
 
 
-def call(body, out_shape, operands, in_specs=None, out_specs=None, scratch=(), flops=1000000, vmem=None):
+def call(body, name, out_shape, operands, in_specs=None, out_specs=None, scratch=(), flops=1000000, vmem=None):
     return pl.pallas_call(
         body,
+        name=name,
         out_shape=out_shape,
         in_specs=in_specs or [VMEM] * len(operands),
         out_specs=out_specs or jax.tree.map(lambda _: VMEM, out_shape),
@@ -262,6 +263,11 @@
     )(*operands)
 
 
+def fold(tiles, count, scale, name):
+    out = jax.ShapeDtypeStruct((count, *tiles.shape[1:]), BF16)
+    return call(functools.partial(fold_kernel, scale), name, out, (tiles,), vmem=SMALL)
+
+
 def in_hbm(value):
     return pltpu.with_memory_space_constraint(value, pltpu.HBM)
 
@@ -270,7 +276,7 @@
     return jax.ShapeDtypeStruct((rows, width), kind)
 
 
-def layer(
+def shards(
     nodes, edges, senders, receivers, block_count, send_rows, node_cot, edge_cot,
     edge_w1, edge_b1, edge_w2, edge_b2, edge_gain, edge_shift,
     node_w1, node_b1, node_w2, node_b2, node_gain, node_shift,
@@ -282,7 +288,7 @@
     far_pairs = [(j, j + 1) for j in range(1, 63, 2)] + [(j + 1, j) for j in range(1, 63, 2)]
 
     near, far = call(
-        pack_kernel, (shape(128, 128, BF16),) * 2, (in_hbm(own_nodes), in_hbm(lists)), [HBM] * 2,
+        pack_kernel, "pack", (shape(128, 128, BF16),) * 2, (in_hbm(own_nodes), in_hbm(lists)), [HBM] * 2,
         scratch=[
             pltpu.VMEM((512, 128), BF16), pltpu.VMEM((2, 128), jnp.int32), pltpu.SemaphoreType.DMA((2,))
         ],
@@ -314,7 +320,7 @@
         )
     ] + [pltpu.SemaphoreType.DMA((18,)), pltpu.SemaphoreType.DMA((3,))]
     node_out, edge_out, grad_edge, local_grad, near_grad, far_grad, send = call(
-        main_kernel, outs, (block_count, near, far)
+        main_kernel, "main", outs, (block_count, near, far)
         + tuple(in_hbm(source) for source in sources),
         [SMEM, VMEM, VMEM] + [HBM] * 18, (HBM,) * 3 + (VMEM,) * 4, scratch, 2000000000, 24 << 20,
     )
@@ -322,15 +328,18 @@
     far_back = lax.ppermute(far_grad, DOM, far_pairs)
     near_back = lax.ppermute(near_grad, DOM, near_pairs)
     scale = 1.0 / math.sqrt(lax.axis_size(DOM) * lax.axis_size("x") * 512)
-    stack = jax.ShapeDtypeStruct((16, 64, 128), BF16)
-    tiles = lax.all_to_all(send.reshape(16, 64, 128), COLUMN, 0, 0, tiled=True)
-    copies = call(functools.partial(fold_kernel, 1.0), stack, (tiles,), vmem=SMALL)
-    tiles = lax.all_to_all(copies, PLANE, 0, 0, tiled=True)
-    copies = call(functools.partial(fold_kernel, scale), stack, (tiles,), vmem=SMALL)
-    whole = lax.all_to_all(copies, COLUMN, 0, 0, tiled=True).reshape(ROWS, 128)
+    planes, columns = lax.axis_size(PLANE), lax.axis_size(COLUMN)
+    rows = ROWS // planes
+    tiles = lax.all_to_all(send.reshape(planes, rows, 128), PLANE, 0, 0, tiled=True)
+    copies = fold(tiles, columns, 1.0, "fold_plane")
+    tiles = lax.all_to_all(copies, COLUMN, 0, 0, tiled=True)
+    copies = fold(tiles, planes, scale, "fold_column")
+    whole = lax.all_to_all(copies, PLANE, 0, 0, tiled=True).reshape(ROWS, 128)
     weight_grads = whole[:LIVE_ROWS].astype(F32).reshape(LIVE_ROWS * 128)
 
-    grad_node = call(finish_kernel, shape(512, 128, BF16), (local_grad, near_back, far_back, lists), vmem=SMALL)
+    grad_node = call(
+        finish_kernel, "finish", shape(512, 128, BF16), (local_grad, near_back, far_back, lists), vmem=SMALL
+    )
     return (
         node_out[None],
         edge_out.reshape(1, 4, 128, 128),
@@ -344,7 +353,7 @@
     finer = Mesh(mesh.devices.reshape(4, 8, 2, mesh.shape["grp"]), ("y", "z", "c", "x"))
     by_row = P("x", DOM)
     return jax.shard_map(
-        layer,
+        shards,
         mesh=finer,
         in_specs=(by_row,) * 8 + (P(),) * 12,
         out_specs=(by_row,) * 4 + (P(),),

time: 72.1 us -> 65.5 us (0.908)
  blocking collectives: 34.5 us -> 30 us
  waiting for transfers between devices: 9.98 us -> 7.27 us
    all_to_all x2, blocking collectives: 34.5 us -> 30 us  [the longest x1 17.8 us: shards(): lax.all_to_all(send.reshape(planes, rows, 128), PLANE, 0, 0, tiled=True)]
    ppermute x4, waiting for transfers between devices: 7.62 us -> 5.82 us  [the longest x1 3.17 us: shards(): far_back = lax.ppermute(far_grad, DOM, far_pairs)]
    all_to_all x1, starting transfers between devices: 4.41 us -> 6.06 us  [shards(): whole = lax.all_to_all(copies, PLANE, 0, 0, tiled=True).reshape(ROWS, 128)]
    ppermute x4, starting transfers between devices: 8.98 us -> 7.99 us  [the longest x1 3.29 us: shards(): near = lax.ppermute(near, DOM, near_pairs)]
    all_to_all x1, waiting for transfers between devices: 2.36 us -> 1.45 us  [shards(): whole = lax.all_to_all(copies, PLANE, 0, 0, tiled=True).reshape(ROWS, 128)]
where the time goes in v3:
time: 65.5 us; the launch traced here: 65.1 us
  blocking collectives  30 us (46%)
  starting transfers between devices  14 us (21%)
  Pallas kernels  11.7 us (18%)
  waiting for transfers between devices  7.27 us (11%)
  between operations  1.34 us (2%)
  other arithmetic  0.8 us (1%)
    all_to_all x1, blocking collectives, shards(): lax.all_to_all(send.reshape(planes, rows, 128), PLANE, 0, 0, tiled=True)  17.8 us
    all_to_all x1, blocking collectives, shards(): tiles = lax.all_to_all(copies, COLUMN, 0, 0, tiled=True)  12.2 us
    pallas_call x5, Pallas kernels, call(): pl.pallas_call(body, name=name, out_shape=out_shape, in_specs=in_specs or...  11.7 us
    all_to_all x1, starting transfers between devices, shards(): whole = lax.all_to_all(copies, PLANE, 0, 0, tiled=True).reshape(ROWS, 128)  6.06 us
    ppermute x1, starting transfers between devices, shards(): near = lax.ppermute(near, DOM, near_pairs)  3.29 us
    ppermute x1, waiting for transfers between devices, shards(): far_back = lax.ppermute(far_grad, DOM, far_pairs)  3.17 us
    ppermute x1, waiting for transfers between devices, shards(): far = lax.ppermute(far, DOM, far_pairs)  2.65 us
    ppermute x1, starting transfers between devices, shards(): far_back = lax.ppermute(far_grad, DOM, far_pairs)  2.46 us
  transfers between devices with their start and end apart: 5, of which 3 were waited for; matrix products, arithmetic and copies ran while one was open for 0% of the time, Pallas kernels for 1%

profile of v3, /device:TPU:1, one launch (start us, length us, event | category | flops | bytes accessed | tf_op | source)
XLA Modules:
  0.0 65.1 jit_solution(41886681175067959)
XLA Ops:
  0.6 1.2 %pack.1 = (bf16[128,128]{1,0:T(8,128)(2,1)S(1)}, bf16[128,128]{1,0:T(8,128)(2,1)S(1)}) custom-call(bf16[512,128]{1,0:T(8,128)(2,1)} %bitcast.31, s32[2,128]{1,0:T(2,128)} %bitcast.27), custom_call_target="tpu_custom_call" | custom-call | flops 1000000 | bytes 1000000 | tf_op jit(solution)/shard_map/pack/pallas_call | solution.py:254
  1.9 3.3 %collective-permute-start = (bf16[128,128]{1,0:T(8,128)(2,1)S(1)}, bf16[128,128]{1,0:T(8,128)(2,1)S(1)}, u32[]{:S(2)}, u32[]{:S(2)}) collective-permute-start(bf16[128,128]{1,0:T(8,128)(2,1)S(1)} %get-tuple-element.14), channel_id=1, source_target_pairs={{0,4},{4,0},{8,12},{12,8},{16,20},{20,16},{24,28},{28,24},{32,36},... | collective-permute-start | bytes 98312 | tf_op jit(solution)/shard_map/ppermute | solution.py:298
  5.1 1.9 %collective-permute-start.1 = (bf16[128,128]{1,0:T(8,128)(2,1)S(1)}, bf16[128,128]{1,0:T(8,128)(2,1)S(1)}, u32[]{:S(2)}, u32[]{:S(2)}) collective-permute-start(bf16[128,128]{1,0:T(8,128)(2,1)S(1)} %get-tuple-element.15), channel_id=1, source_target_pairs={{4,8},{12,16},{20,24},{28,32},{36,40},{44,48},{52,56},{60,64},{68,... | collective-permute-start | bytes 98312 | tf_op jit(solution)/shard_map/ppermute | solution.py:297
  7.7 0.0 collective-permute-done.near
  7.7 2.6 %collective-permute-done.1.far = bf16[128,128]{1,0:T(8,128)(2,1)S(1)} collective-permute-done((bf16[128,128]{1,0:T(8,128)(2,1)S(1)}, bf16[128,128]{1,0:T(8,128)(2,1)S(1)}, u32[]{:S(2)}, u32[]{:S(2)}) %collective-permute-start.1) | collective-permute-done | bytes 32800 | tf_op jit(solution)/shard_map/ppermute | solution.py:297
  10.4 8.8 %main.1 = (bf16[512,128]{1,0:T(8,128)(2,1)}, bf16[512,128]{1,0:T(8,128)(2,1)}, bf16[512,128]{1,0:T(8,128)(2,1)}, f32[512,128]{1,0:T(8,128)S(1)}, bf16[128,128]{1...) custom-call(s32[1,1]{1,0:T(1,128)S(6)} %copy.25.count, ...), custom_call_target="tpu_custom_call" | custom-call | flops 2000000000 | bytes 1000000 | tf_op jit(solution)/shard_map/main/pallas_call | solution.py:254
  19.2 17.8 %all_to_all.15.tiles = bf16[32,32,128]{2,1,0:T(8,128)(2,1)S(1)} all-to-all(bf16[32,32,128]{2,1,0:T(8,128)(2,1)S(1)} %bitcast.26), channel_id=1, replica_groups=mesh['y'=4,'z'=8,'c'=2,'x'=4] {'c','y','x'}, dimensions={0} | all-to-all | bytes 524288 | tf_op jit(solution)/shard_map/all_to_all | solution.py:333
  37.0 12.2 %all_to_all.16.tiles = bf16[8,32,128]{2,1,0:T(8,128)(2,1)S(1)} all-to-all(bf16[8,32,128]{2,1,0:T(8,128)(2,1)S(1)} %fold_plane.1), channel_id=1, replica_groups=mesh['y'=4,'z'=8,'c'=2,'x'=4] {'z'}, dimensions={0} | all-to-all | bytes 131072 | tf_op jit(solution)/shard_map/all_to_all | solution.py:335
  49.2 0.7 %fold_column.1 = bf16[32,32,128]{2,1,0:T(8,128)(2,1)} custom-call(bf16[8,32,128]{2,1,0:T(8,128)(2,1)S(1)} %all_to_all.16.tiles), custom_call_target="tpu_custom_call" | custom-call | flops 1000000 | bytes 1000000 | tf_op jit(solution)/shard_map/fold_column/pallas_call | solution.py:254
  49.9 6.1 %all-to-all-start.2 = ((bf16[32,32,128]{2,1,0:T(8,128)(2,1)}), bf16[32,32,128]{2,1,0:T(8,128)(2,1)S(1)}, u32[]{:S(2)}, u32[]{:S(2)}) async-start(bf16[32,32,128]{2,1,0:T(8,128)(2,1)} %fold_column.1), calls=%async_computation.2 | async-start | bytes 524288 | tf_op jit(solution)/shard_map/all_to_all | solution.py:337
  56.0 0.3 collective-permute-start.2
  56.3 0.0 copy-start
  56.3 2.5 %collective-permute-start.3 = (bf16[128,128]{1,0:T(8,128)(2,1)S(1)}, bf16[128,128]{1,0:T(8,128)(2,1)S(1)}, u32[]{:S(2)}, u32[]{:S(2)}) collective-permute-start(bf16[128,128]{1,0:T(8,128)(2,1)S(1)} %get-tuple-element.20), channel_id=1, source_target_pairs={{4,8},{12,16},{20,24},{28,32},{36,40},{44,48},{52,56},{60,64},{68,... | collective-permute-start | bytes 98312 | tf_op jit(solution)/shard_map/ppermute | solution.py:328
  58.8 0.0 collective-permute-done.2.near
  58.8 3.2 %collective-permute-done.3.far = bf16[128,128]{1,0:T(8,128)(2,1)S(1)} collective-permute-done((bf16[128,128]{1,0:T(8,128)(2,1)S(1)}, bf16[128,128]{1,0:T(8,128)(2,1)S(1)}, u32[]{:S(2)}, u32[]{:S(2)}) %collective-permute-start.3) | collective-permute-done | bytes 32800 | tf_op jit(solution)/shard_map/ppermute | solution.py:328
  62.0 0.0 copy-done
  62.0 0.9 %finish.1 = bf16[512,128]{1,0:T(8,128)(2,1)} custom-call(f32[512,128]{1,0:T(8,128)S(1)} %get-tuple-element.18.local_grad, bf16[128,128]{1,0:T(8,128)(2,1)S(1)} %collective-permute-done.2.near, bf16[128,128]{1,0:T(8,128)(2,1)S(1)} %collective-permute-done.3.far, s32[2,128]{1,0:T(2,128)S(1)} %bitcast.28), custom_call_target="tpu_custom_call" | custom-call | flops 1000000 | bytes 1000000 | tf_op jit(solution)/shard_map/finish/pallas_call | solution.py:254
  62.9 1.4 %all-to-all-done.2 = bf16[32,32,128]{2,1,0:T(8,128)(2,1)S(1)} async-done(((bf16[32,32,128]{2,1,0:T(8,128)(2,1)}), bf16[32,32,128]{2,1,0:T(8,128)(2,1)S(1)}, u32[]{:S(2)}, u32[]{:S(2)}) %all-to-all-start.2) | async-done | bytes 262176 | tf_op jit(solution)/shard_map/all_to_all | solution.py:337
  64.3 0.8 %fusion = f32[115712]{0:T(1024)} fusion(bf16[1024,128]{1,0:T(8,128)(2,1)S(1)} %bitcast.29), kind=kLoop, calls=%fused_computation.1 | loop fusion | flops 115712 | bytes 694272 | tf_op jit(solution)/shard_map/reshape | solution.py:338
  (1 shorter events, 0.0 us)
Async XLA Ops:
  1.9 5.9 %collective-permute-start = (bf16[128,128]{1,0:T(8,128)(2,1)S(1)}, bf16[128,128]{1,0:T(8,128)(2,1)S(1)}, u32[]{:S(2)}, u32[]{:S(2)}) collective-permute-start(bf16[128,128]{1,0:T(8,128)(2,1)S(1)} %get-tuple-element.14), channel_id=1, source_target_pairs={{0,4},{4,0},{8,12},{12,8},{16,20},{20,16},{24,28},{28,24},{32,36},... | collective-permute-start | bytes 98312 | tf_op jit(solution)/shard_map/ppermute | solution.py:298
  5.1 5.2 %collective-permute-start.1 = (bf16[128,128]{1,0:T(8,128)(2,1)S(1)}, bf16[128,128]{1,0:T(8,128)(2,1)S(1)}, u32[]{:S(2)}, u32[]{:S(2)}) collective-permute-start(bf16[128,128]{1,0:T(8,128)(2,1)S(1)} %get-tuple-element.15), channel_id=1, source_target_pairs={{4,8},{12,16},{20,24},{28,32},{36,40},{44,48},{52,56},{60,64},{68,... | collective-permute-start | bytes 98312 | tf_op jit(solution)/shard_map/ppermute | solution.py:297
  49.9 14.4 %all-to-all-start.2 = ((bf16[32,32,128]{2,1,0:T(8,128)(2,1)}), bf16[32,32,128]{2,1,0:T(8,128)(2,1)S(1)}, u32[]{:S(2)}, u32[]{:S(2)}) async-start(bf16[32,32,128]{2,1,0:T(8,128)(2,1)} %fold_column.1), calls=%async_computation.2 | async-start | bytes 524288 | tf_op jit(solution)/shard_map/all_to_all | solution.py:337
  56.0 2.8 %collective-permute-start.2 = (bf16[128,128]{1,0:T(8,128)(2,1)S(1)}, bf16[128,128]{1,0:T(8,128)(2,1)S(1)}, u32[]{:S(2)}, u32[]{:S(2)}) collective-permute-start(bf16[128,128]{1,0:T(8,128)(2,1)S(1)} %get-tuple-element.19), channel_id=1, source_target_pairs={{0,4},{4,0},{8,12},{12,8},{16,20},{20,16},{24,28},{28,24},{32,36},... | collective-permute-start | bytes 98312 | tf_op jit(solution)/shard_map/ppermute | solution.py:329
  56.3 5.7 %copy-start = (s32[1,1,2,128]{3,2,1,0:T(2,128)S(1)}, s32[1,1,2,128]{3,2,1,0:T(2,128)}, u32[]{:S(2)}) copy-start(s32[1,1,2,128]{3,2,1,0:T(2,128)} %param.25) | copy-start | bytes 3076
  56.3 5.6 %collective-permute-start.3 = (bf16[128,128]{1,0:T(8,128)(2,1)S(1)}, bf16[128,128]{1,0:T(8,128)(2,1)S(1)}, u32[]{:S(2)}, u32[]{:S(2)}) collective-permute-start(bf16[128,128]{1,0:T(8,128)(2,1)S(1)} %get-tuple-element.20), channel_id=1, source_target_pairs={{4,8},{12,16},{20,24},{28,32},{36,40},{44,48},{52,56},{60,64},{68,... | collective-permute-start | bytes 98312 | tf_op jit(solution)/shard_map/ppermute | solution.py:328

commit v4 on v3

--- a/solution.py
+++ b/solution.py
@@ -59,6 +59,11 @@
 
 def joined(value):
     return value[:, :128] + value[:, 128:]
+
+
+def is_live(blocks):
+    line = lax.broadcasted_iota(jnp.int32, (512, 128), 0)
+    return jnp.where(line < blocks * 128, 1.0, 0.0).astype(F32)
 
 
 def pack_kernel(nodes_in, lists_in, near, far, nodes, lists, arrive):
@@ -118,91 +123,87 @@
     for load in loads:
         load.start()
     (
-        nodes, senders, receivers, edges, ew1, eb1, ew2, eb2, egain, eshift,
+        senders, receivers, nodes, edges, ew1, eb1, ew2, eb2, egain, eshift,
         nw1, nb1, nw2, nb2, ngain, nshift, node_cot, edge_cot,
     ) = landed
     edge_left, node_left, grad_left = left
     core = lax.axis_index("c")
     live_blocks = count[0, 0]
+    table[pl.ds(pl.multiple_of(640 - 128 * core, 128), 128), :] = near[...]
+    table[pl.ds(pl.multiple_of(512 + 128 * core, 128), 128), :] = far[...]
     for load in loads[:10]:
         load.wait()
-    table[pl.ds(0, 512), :] = nodes[...]
-    table[pl.ds(pl.multiple_of(640 - 128 * core, 128), 128), :] = near[...]
-    table[pl.ds(pl.multiple_of(512 + 128 * core, 128), 128), :] = far[...]
-
     for b in range(4):
         rows = pl.ds(b * 128, 128)
-        live = jnp.where(b < live_blocks, 1.0, 0.0).astype(F32)
         send_row, recv_row = senders[pl.ds(b, 1), :], receivers[pl.ds(b, 1), :]
-        pick = pick_rows(recv_row, 512)
-        pick_recv[rows, :] = pick
+        pick_recv[rows, :] = pick_rows(recv_row, 512)
         place_recv[:, rows] = place_rows(recv_row, 512)
         place_send[:, rows] = place_rows(send_row, 768)
-        own = edges[rows, :]
-        sender = dot(pick_rows(send_row, 768), table[...]).astype(BF16)
-        receiver = dot(pick, nodes[...]).astype(BF16)
-        gathered = jnp.concatenate([own, sender, receiver], axis=1)
-        inputs[rows, :] = gathered
-        first = dot(gathered, ew1[...]) + eb1[...]
-        sigmoid = jax.nn.sigmoid(first)
-        low = (first * sigmoid).astype(BF16)
-        hidden[rows, :] = low
-        slope[rows, :] = sigmoid * (1.0 + first * (1.0 - sigmoid))
-        n, inv = norm_forward(dot(low, ew2[...]) + eb2[...])
-        normed[rows, :] = n
-        inverse[rows, :] = inv
-        message = (n * egain[...] + eshift[...]) * live
-        edge_left[rows, :] = (own.astype(F32) + message).astype(BF16)
-        messages[rows, :] = split(message)
+
+    table[pl.ds(0, 512), :] = nodes[...]
+    live = is_live(live_blocks)
+    own = edges[...]
+    picks = jnp.concatenate([pick_rows(senders[pl.ds(k, 1), :], 768) for k in range(4)], axis=0)
+    sender = dot(picks, table[...]).astype(BF16)
+    receiver = dot(pick_recv[...], nodes[...]).astype(BF16)
+    gathered = jnp.concatenate([own, sender, receiver], axis=1)
+    inputs[...] = gathered
+    first = dot(gathered, ew1[...]) + eb1[...]
+    sigmoid = jax.nn.sigmoid(first)
+    low = (first * sigmoid).astype(BF16)
+    hidden[...] = low
+    slope[...] = sigmoid * (1.0 + first * (1.0 - sigmoid))
+    n, inv = norm_forward(dot(low, ew2[...]) + eb2[...])
+    normed[...] = n
+    inverse[...] = inv
+    message = (n * egain[...] + eshift[...]) * live
+    edge_left[...] = (own.astype(F32) + message).astype(BF16)
+    messages[...] = split(message)
 
     stores[0].start()
     for load in loads[10:]:
         load.wait()
     sums = [jnp.zeros((8, 128), F32) for _ in range(8)]
-    for b in range(4):
-        rows = pl.ds(b * 128, 128)
-        aggregate = joined(dot(place_recv[rows, :], messages[...])).astype(BF16)
-        own = nodes[rows, :]
-        gathered = jnp.concatenate([own, aggregate], axis=1)
-        node_inputs[rows, :] = gathered
-        first = dot(gathered, nw1[...]) + nb1[...]
-        sigmoid = jax.nn.sigmoid(first)
-        low = (first * sigmoid).astype(BF16)
-        node_hidden[rows, :] = low
-        n, inv = norm_forward(dot(low, nw2[...]) + nb2[...])
-        node_left[rows, :] = (own.astype(F32) + (n * ngain[...] + nshift[...])).astype(BF16)
-        cot = node_cot[rows, :].astype(F32)
-        g2 = norm_backward(cot, n, inv, ngain[...])
-        g2_low = g2.astype(BF16)
-        g1 = dot_nt(g2_low, nw2[...]) * (sigmoid * (1.0 + first * (1.0 - sigmoid)))
-        g1_low = g1.astype(BF16)
-        node_first[rows, :] = g1_low
-        node_second[rows, :] = g2_low
-        back = dot_nt(g1_low, nw1[...])
-        local_grad[rows, :] = cot + back[:, :128]
-        spread[rows, :] = split(back[:, 128:])
-        for k, piece in enumerate((g1, g2, cot * n, cot)):
-            sums[4 + k] += partial_sum(piece)
+    aggregate = joined(dot(place_recv[...], messages[...])).astype(BF16)
+    own = nodes[...]
+    gathered = jnp.concatenate([own, aggregate], axis=1)
+    node_inputs[...] = gathered
+    first = dot(gathered, nw1[...]) + nb1[...]
+    sigmoid = jax.nn.sigmoid(first)
+    low = (first * sigmoid).astype(BF16)
+    node_hidden[...] = low
+    n, inv = norm_forward(dot(low, nw2[...]) + nb2[...])
+    node_left[...] = (own.astype(F32) + (n * ngain[...] + nshift[...])).astype(BF16)
+    cot = node_cot[...].astype(F32)
+    g2 = norm_backward(cot, n, inv, ngain[...])
+    g2_low = g2.astype(BF16)
+    g1 = dot_nt(g2_low, nw2[...]) * (sigmoid * (1.0 + first * (1.0 - sigmoid)))
+    g1_low = g1.astype(BF16)
+    node_first[...] = g1_low
+    node_second[...] = g2_low
+    back = dot_nt(g1_low, nw1[...])
+    local_grad[...] = cot + back[:, :128]
+    spread[...] = split(back[:, 128:])
+    for k, piece in enumerate((g1, g2, cot * n, cot)):
+        sums[4 + k] += partial_sum(piece)
     stores[1].start()
 
-    for b in range(4):
-        rows = pl.ds(b * 128, 128)
-        live = jnp.where(b < live_blocks, 1.0, 0.0).astype(F32)
-        edge_grad = edge_cot[rows, :].astype(F32)
-        cot = live * (edge_grad + joined(dot(pick_recv[rows, :], spread[...])))
-        n = normed[rows, :]
-        g2 = norm_backward(cot, n, inverse[rows, :], egain[...])
-        g2_low = g2.astype(BF16)
-        g1 = dot_nt(g2_low, ew2[...]) * slope[rows, :]
-        g1_low = g1.astype(BF16)
-        first_low[rows, :] = g1_low
-        second_low[rows, :] = g2_low
-        back = dot_nt(g1_low, ew1[...])
-        grad_left[rows, :] = (edge_grad + back[:, :128]).astype(BF16)
-        dxs[rows, :] = split(back[:, 128:256])
-        dxr[rows, :] = split(back[:, 256:])
-        for k, piece in enumerate((g1, g2, cot * n, cot)):
-            sums[k] += partial_sum(piece)
+    live = is_live(live_blocks)
+    edge_grad = edge_cot[...].astype(F32)
+    cot = live * (edge_grad + joined(dot(pick_recv[...], spread[...])))
+    n = normed[...]
+    g2 = norm_backward(cot, n, inverse[...], egain[...])
+    g2_low = g2.astype(BF16)
+    g1 = dot_nt(g2_low, ew2[...]) * slope[...]
+    g1_low = g1.astype(BF16)
+    first_low[...] = g1_low
+    second_low[...] = g2_low
+    back = dot_nt(g1_low, ew1[...])
+    grad_left[...] = (edge_grad + back[:, :128]).astype(BF16)
+    dxs[...] = split(back[:, 128:256])
+    dxr[...] = split(back[:, 256:])
+    for k, piece in enumerate((g1, g2, cot * n, cot)):
+        sums[k] += partial_sum(piece)
     stores[2].start()
 
     lower = joined(dot(place_send[512:640, :], dxs[...])).astype(BF16)
@@ -250,10 +251,9 @@
     out[...] = (local_grad[...] + added).astype(BF16)
 
 
-def call(body, name, out_shape, operands, in_specs=None, out_specs=None, scratch=(), flops=1000000, vmem=None):
+def call(body, out_shape, operands, in_specs=None, out_specs=None, scratch=(), flops=1000000, vmem=None):
     return pl.pallas_call(
         body,
-        name=name,
         out_shape=out_shape,
         in_specs=in_specs or [VMEM] * len(operands),
         out_specs=out_specs or jax.tree.map(lambda _: VMEM, out_shape),
@@ -263,9 +263,9 @@
     )(*operands)
 
 
-def fold(tiles, count, scale, name):
+def fold(tiles, count, scale):
     out = jax.ShapeDtypeStruct((count, *tiles.shape[1:]), BF16)
-    return call(functools.partial(fold_kernel, scale), name, out, (tiles,), vmem=SMALL)
+    return call(functools.partial(fold_kernel, scale), out, (tiles,), vmem=SMALL)
 
 
 def in_hbm(value):
@@ -276,7 +276,7 @@
     return jax.ShapeDtypeStruct((rows, width), kind)
 
 
-def shards(
+def layer(
     nodes, edges, senders, receivers, block_count, send_rows, node_cot, edge_cot,
     edge_w1, edge_b1, edge_w2, edge_b2, edge_gain, edge_shift,
     node_w1, node_b1, node_w2, node_b2, node_gain, node_shift,
@@ -288,7 +288,7 @@
     far_pairs = [(j, j + 1) for j in range(1, 63, 2)] + [(j + 1, j) for j in range(1, 63, 2)]
 
     near, far = call(
-        pack_kernel, "pack", (shape(128, 128, BF16),) * 2, (in_hbm(own_nodes), in_hbm(lists)), [HBM] * 2,
+        pack_kernel, (shape(128, 128, BF16),) * 2, (in_hbm(own_nodes), in_hbm(lists)), [HBM] * 2,
         scratch=[
             pltpu.VMEM((512, 128), BF16), pltpu.VMEM((2, 128), jnp.int32), pltpu.SemaphoreType.DMA((2,))
         ],
@@ -298,7 +298,7 @@
     near = lax.ppermute(near, DOM, near_pairs)
 
     sources = (
-        own_nodes, senders[0], receivers[0], edges[0].reshape(512, 128),
+        senders[0], receivers[0], own_nodes, edges[0].reshape(512, 128),
         edge_w1, line(edge_b1), edge_w2, line(edge_b2), line(edge_gain), line(edge_shift),
         node_w1, line(node_b1), node_w2, line(node_b2), line(node_gain), line(node_shift),
         node_cot[0], edge_cot[0].reshape(512, 128),
@@ -320,7 +320,7 @@
         )
     ] + [pltpu.SemaphoreType.DMA((18,)), pltpu.SemaphoreType.DMA((3,))]
     node_out, edge_out, grad_edge, local_grad, near_grad, far_grad, send = call(
-        main_kernel, "main", outs, (block_count, near, far)
+        main_kernel, outs, (block_count, near, far)
         + tuple(in_hbm(source) for source in sources),
         [SMEM, VMEM, VMEM] + [HBM] * 18, (HBM,) * 3 + (VMEM,) * 4, scratch, 2000000000, 24 << 20,
     )
@@ -331,15 +331,13 @@
     planes, columns = lax.axis_size(PLANE), lax.axis_size(COLUMN)
     rows = ROWS // planes
     tiles = lax.all_to_all(send.reshape(planes, rows, 128), PLANE, 0, 0, tiled=True)
-    copies = fold(tiles, columns, 1.0, "fold_plane")
+    copies = fold(tiles, columns, 1.0)
     tiles = lax.all_to_all(copies, COLUMN, 0, 0, tiled=True)
-    copies = fold(tiles, planes, scale, "fold_column")
+    copies = fold(tiles, planes, scale)
     whole = lax.all_to_all(copies, PLANE, 0, 0, tiled=True).reshape(ROWS, 128)
     weight_grads = whole[:LIVE_ROWS].astype(F32).reshape(LIVE_ROWS * 128)
 
-    grad_node = call(
-        finish_kernel, "finish", shape(512, 128, BF16), (local_grad, near_back, far_back, lists), vmem=SMALL
-    )
+    grad_node = call(finish_kernel, shape(512, 128, BF16), (local_grad, near_back, far_back, lists), vmem=SMALL)
     return (
         node_out[None],
         edge_out.reshape(1, 4, 128, 128),
@@ -353,7 +351,7 @@
     finer = Mesh(mesh.devices.reshape(4, 8, 2, mesh.shape["grp"]), ("y", "z", "c", "x"))
     by_row = P("x", DOM)
     return jax.shard_map(
-        shards,
+        layer,
         mesh=finer,
         in_specs=(by_row,) * 8 + (P(),) * 12,
         out_specs=(by_row,) * 4 + (P(),),

time: 65.5 us -> 61.9 us (0.945)
  Pallas kernels: 11.7 us -> 8.14 us
    pallas_call x5, Pallas kernels: 11.7 us -> 8.14 us  [call(): pl.pallas_call(body, out_shape=out_shape, in_specs=in_specs or [VMEM] * l...]
where the time goes in v4:
time: 61.9 us; the launch traced here: 61.6 us
  blocking collectives  30 us (48%)
  starting transfers between devices  14 us (23%)
  Pallas kernels  8.14 us (13%)
  waiting for transfers between devices  7.27 us (12%)
  between operations  1.34 us (2%)
  other arithmetic  0.8 us (1%)
    all_to_all x1, blocking collectives, layer(): lax.all_to_all(send.reshape(planes, rows, 128), PLANE, 0, 0, tiled=True)  17.8 us
    all_to_all x1, blocking collectives, layer(): tiles = lax.all_to_all(copies, COLUMN, 0, 0, tiled=True)  12.2 us
    pallas_call x5, Pallas kernels, call(): pl.pallas_call(body, out_shape=out_shape, in_specs=in_specs or [VMEM] * l...  8.14 us
    all_to_all x1, starting transfers between devices, layer(): whole = lax.all_to_all(copies, PLANE, 0, 0, tiled=True).reshape(ROWS, 128)  6.06 us
    ppermute x1, starting transfers between devices, layer(): near = lax.ppermute(near, DOM, near_pairs)  3.29 us
    ppermute x1, waiting for transfers between devices, layer(): far_back = lax.ppermute(far_grad, DOM, far_pairs)  3.17 us
    ppermute x1, waiting for transfers between devices, layer(): far = lax.ppermute(far, DOM, far_pairs)  2.65 us
    ppermute x1, starting transfers between devices, layer(): far_back = lax.ppermute(far_grad, DOM, far_pairs)  2.46 us
  transfers between devices with their start and end apart: 5, of which 3 were waited for; matrix products, arithmetic and copies ran while one was open for 0% of the time, Pallas kernels for 1%

profile of v4, /device:TPU:1, one launch (start us, length us, event | category | flops | bytes accessed | tf_op | source)
XLA Modules:
  0.0 61.6 jit_solution(2519756107601901081)
XLA Ops:
  0.6 1.2 %shard_map.227 = (bf16[128,128]{1,0:T(8,128)(2,1)S(1)}, bf16[128,128]{1,0:T(8,128)(2,1)S(1)}) custom-call(bf16[512,128]{1,0:T(8,128)(2,1)} %bitcast.31, s32[2,128]{1,0:T(2,128)} %bitcast.27), custom_call_target="tpu_custom_call" | custom-call | flops 1000000 | bytes 1000000 | tf_op jit(solution)/shard_map/pallas_call | solution.py:255
  1.9 3.3 %collective-permute-start = (bf16[128,128]{1,0:T(8,128)(2,1)S(1)}, bf16[128,128]{1,0:T(8,128)(2,1)S(1)}, u32[]{:S(2)}, u32[]{:S(2)}) collective-permute-start(bf16[128,128]{1,0:T(8,128)(2,1)S(1)} %get-tuple-element.14), channel_id=1, source_target_pairs={{0,4},{4,0},{8,12},{12,8},{16,20},{20,16},{24,28},{28,24},{32,36},... | collective-permute-start | bytes 98312 | tf_op jit(solution)/shard_map/ppermute | solution.py:298
  5.1 1.9 %collective-permute-start.1 = (bf16[128,128]{1,0:T(8,128)(2,1)S(1)}, bf16[128,128]{1,0:T(8,128)(2,1)S(1)}, u32[]{:S(2)}, u32[]{:S(2)}) collective-permute-start(bf16[128,128]{1,0:T(8,128)(2,1)S(1)} %get-tuple-element.15), channel_id=1, source_target_pairs={{4,8},{12,16},{20,24},{28,32},{36,40},{44,48},{52,56},{60,64},{68,... | collective-permute-start | bytes 98312 | tf_op jit(solution)/shard_map/ppermute | solution.py:297
  7.7 0.0 collective-permute-done.near
  7.7 2.6 %collective-permute-done.1.far = bf16[128,128]{1,0:T(8,128)(2,1)S(1)} collective-permute-done((bf16[128,128]{1,0:T(8,128)(2,1)S(1)}, bf16[128,128]{1,0:T(8,128)(2,1)S(1)}, u32[]{:S(2)}, u32[]{:S(2)}) %collective-permute-start.1) | collective-permute-done | bytes 32800 | tf_op jit(solution)/shard_map/ppermute | solution.py:297
  10.4 5.3 %shard_map.228 = (bf16[512,128]{1,0:T(8,128)(2,1)}, bf16[512,128]{1,0:T(8,128)(2,1)}, bf16[512,128]{1,0:T(8,128)(2,1)}, f32[512,128]{1,0:T(8,128)S(1)}, bf16[128...) custom-call(s32[1,1]{1,0:T(1,128)S(6)} %copy.25.count, ...), custom_call_target="tpu_custom_call" | custom-call | flops 2000000000 | bytes 1000000 | tf_op jit(solution)/shard_map/pallas_call | solution.py:255
  15.6 17.8 %all_to_all.15.tiles = bf16[32,32,128]{2,1,0:T(8,128)(2,1)S(1)} all-to-all(bf16[32,32,128]{2,1,0:T(8,128)(2,1)S(1)} %bitcast.26), channel_id=1, replica_groups=mesh['y'=4,'z'=8,'c'=2,'x'=4] {'c','y','x'}, dimensions={0} | all-to-all | bytes 524288 | tf_op jit(solution)/shard_map/all_to_all | solution.py:333
  33.4 12.2 %all_to_all.16.tiles = bf16[8,32,128]{2,1,0:T(8,128)(2,1)S(1)} all-to-all(bf16[8,32,128]{2,1,0:T(8,128)(2,1)S(1)} %shard_map.230), channel_id=1, replica_groups=mesh['y'=4,'z'=8,'c'=2,'x'=4] {'z'}, dimensions={0} | all-to-all | bytes 131072 | tf_op jit(solution)/shard_map/all_to_all | solution.py:335
  45.6 0.7 %shard_map.231 = bf16[32,32,128]{2,1,0:T(8,128)(2,1)} custom-call(bf16[8,32,128]{2,1,0:T(8,128)(2,1)S(1)} %all_to_all.16.tiles), custom_call_target="tpu_custom_call" | custom-call | flops 1000000 | bytes 1000000 | tf_op jit(solution)/shard_map/pallas_call | solution.py:255
  46.4 6.1 %all-to-all-start.2 = ((bf16[32,32,128]{2,1,0:T(8,128)(2,1)}), bf16[32,32,128]{2,1,0:T(8,128)(2,1)S(1)}, u32[]{:S(2)}, u32[]{:S(2)}) async-start(bf16[32,32,128]{2,1,0:T(8,128)(2,1)} %shard_map.231), calls=%async_computation.2 | async-start | bytes 524288 | tf_op jit(solution)/shard_map/all_to_all | solution.py:337
  52.4 0.3 collective-permute-start.2
  52.8 0.0 copy-start
  52.8 2.5 %collective-permute-start.3 = (bf16[128,128]{1,0:T(8,128)(2,1)S(1)}, bf16[128,128]{1,0:T(8,128)(2,1)S(1)}, u32[]{:S(2)}, u32[]{:S(2)}) collective-permute-start(bf16[128,128]{1,0:T(8,128)(2,1)S(1)} %get-tuple-element.20), channel_id=1, source_target_pairs={{4,8},{12,16},{20,24},{28,32},{36,40},{44,48},{52,56},{60,64},{68,... | collective-permute-start | bytes 98312 | tf_op jit(solution)/shard_map/ppermute | solution.py:328
  55.2 0.0 collective-permute-done.2.near
  55.3 3.2 %collective-permute-done.3.far = bf16[128,128]{1,0:T(8,128)(2,1)S(1)} collective-permute-done((bf16[128,128]{1,0:T(8,128)(2,1)S(1)}, bf16[128,128]{1,0:T(8,128)(2,1)S(1)}, u32[]{:S(2)}, u32[]{:S(2)}) %collective-permute-start.3) | collective-permute-done | bytes 32800 | tf_op jit(solution)/shard_map/ppermute | solution.py:328
  58.4 0.0 copy-done
  58.4 0.9 %shard_map.229 = bf16[512,128]{1,0:T(8,128)(2,1)} custom-call(f32[512,128]{1,0:T(8,128)S(1)} %get-tuple-element.18.local_grad, bf16[128,128]{1,0:T(8,128)(2,1)S(1)} %collective-permute-done.2.near, bf16[128,128]{1,0:T(8,128)(2,1)S(1)} %collective-permute-done.3.far, s32[2,128]{1,0:T(2,128)S(1)} %bitcast.28), custom_call_target="tpu_custom_call" | custom-call | flops 1000000 | bytes 1000000 | tf_op jit(solution)/shard_map/pallas_call | solution.py:255
  59.3 1.4 %all-to-all-done.2 = bf16[32,32,128]{2,1,0:T(8,128)(2,1)S(1)} async-done(((bf16[32,32,128]{2,1,0:T(8,128)(2,1)}), bf16[32,32,128]{2,1,0:T(8,128)(2,1)S(1)}, u32[]{:S(2)}, u32[]{:S(2)}) %all-to-all-start.2) | async-done | bytes 262176 | tf_op jit(solution)/shard_map/all_to_all | solution.py:337
  60.8 0.8 %fusion = f32[115712]{0:T(1024)} fusion(bf16[1024,128]{1,0:T(8,128)(2,1)S(1)} %bitcast.29), kind=kLoop, calls=%fused_computation.1 | loop fusion | flops 115712 | bytes 694272 | tf_op jit(solution)/shard_map/reshape | solution.py:338
  (1 shorter events, 0.0 us)
Async XLA Ops:
  1.9 5.9 %collective-permute-start = (bf16[128,128]{1,0:T(8,128)(2,1)S(1)}, bf16[128,128]{1,0:T(8,128)(2,1)S(1)}, u32[]{:S(2)}, u32[]{:S(2)}) collective-permute-start(bf16[128,128]{1,0:T(8,128)(2,1)S(1)} %get-tuple-element.14), channel_id=1, source_target_pairs={{0,4},{4,0},{8,12},{12,8},{16,20},{20,16},{24,28},{28,24},{32,36},... | collective-permute-start | bytes 98312 | tf_op jit(solution)/shard_map/ppermute | solution.py:298
  5.1 5.2 %collective-permute-start.1 = (bf16[128,128]{1,0:T(8,128)(2,1)S(1)}, bf16[128,128]{1,0:T(8,128)(2,1)S(1)}, u32[]{:S(2)}, u32[]{:S(2)}) collective-permute-start(bf16[128,128]{1,0:T(8,128)(2,1)S(1)} %get-tuple-element.15), channel_id=1, source_target_pairs={{4,8},{12,16},{20,24},{28,32},{36,40},{44,48},{52,56},{60,64},{68,... | collective-permute-start | bytes 98312 | tf_op jit(solution)/shard_map/ppermute | solution.py:297
  46.4 14.4 %all-to-all-start.2 = ((bf16[32,32,128]{2,1,0:T(8,128)(2,1)}), bf16[32,32,128]{2,1,0:T(8,128)(2,1)S(1)}, u32[]{:S(2)}, u32[]{:S(2)}) async-start(bf16[32,32,128]{2,1,0:T(8,128)(2,1)} %shard_map.231), calls=%async_computation.2 | async-start | bytes 524288 | tf_op jit(solution)/shard_map/all_to_all | solution.py:337
  52.4 2.8 %collective-permute-start.2 = (bf16[128,128]{1,0:T(8,128)(2,1)S(1)}, bf16[128,128]{1,0:T(8,128)(2,1)S(1)}, u32[]{:S(2)}, u32[]{:S(2)}) collective-permute-start(bf16[128,128]{1,0:T(8,128)(2,1)S(1)} %get-tuple-element.19), channel_id=1, source_target_pairs={{0,4},{4,0},{8,12},{12,8},{16,20},{20,16},{24,28},{28,24},{32,36},... | collective-permute-start | bytes 98312 | tf_op jit(solution)/shard_map/ppermute | solution.py:329
  52.8 5.7 %copy-start = (s32[1,1,2,128]{3,2,1,0:T(2,128)S(1)}, s32[1,1,2,128]{3,2,1,0:T(2,128)}, u32[]{:S(2)}) copy-start(s32[1,1,2,128]{3,2,1,0:T(2,128)} %param.25) | copy-start | bytes 3076
  52.8 5.6 %collective-permute-start.3 = (bf16[128,128]{1,0:T(8,128)(2,1)S(1)}, bf16[128,128]{1,0:T(8,128)(2,1)S(1)}, u32[]{:S(2)}, u32[]{:S(2)}) collective-permute-start(bf16[128,128]{1,0:T(8,128)(2,1)S(1)} %get-tuple-element.20), channel_id=1, source_target_pairs={{4,8},{12,16},{20,24},{28,32},{36,40},{44,48},{52,56},{60,64},{68,... | collective-permute-start | bytes 98312 | tf_op jit(solution)/shard_map/ppermute | solution.py:328

commit v5 on v4

--- a/solution.py
+++ b/solution.py
@@ -10,13 +10,14 @@
 from jax.sharding import PartitionSpec as P
 
 DOM = ("y", "z", "c")
-PLANE = ("c", "y", "x")
+PLANE = ("y", "x")
 COLUMN = ("z",)
 EPSILON = 1e-05
 F32 = jnp.float32
 BF16 = jnp.bfloat16
 ROWS = 1024
 LIVE_ROWS = 904
+HALF = 512
 SMALL = 8 << 20
 VMEM = pl.BlockSpec(memory_space=pltpu.VMEM)
 SMEM = pl.BlockSpec(memory_space=pltpu.SMEM)
@@ -59,11 +60,6 @@
 
 def joined(value):
     return value[:, :128] + value[:, 128:]
-
-
-def is_live(blocks):
-    line = lax.broadcasted_iota(jnp.int32, (512, 128), 0)
-    return jnp.where(line < blocks * 128, 1.0, 0.0).astype(F32)
 
 
 def pack_kernel(nodes_in, lists_in, near, far, nodes, lists, arrive):
@@ -105,50 +101,61 @@
     return jnp.sum(value, axis=0, keepdims=True)
 
 
-def main_kernel(count, near, far, *refs):
-    sources, refs = refs[:18], refs[18:]
-    (node_out, edge_out, grad_edge, local_grad, near_grad, far_grad, send), refs = refs[:7], refs[7:]
-    landed, refs = refs[:18], refs[18:]
-    left, refs = refs[:3], refs[3:]
+def prepare_kernel(*refs):
+    sources, landed, (receiver, partial, live, pick_send, pick_recv, place_recv, place_send), (arrive,) = (
+        refs[:19], refs[19:38], refs[38:45], refs[45:],
+    )
+    loads = [pltpu.make_async_copy(a, b, arrive.at[k]) for k, (a, b) in enumerate(zip(sources, landed))]
+    for load in loads:
+        load.start()
+    count, senders, receivers, nodes, edges, ew1, eb1 = landed[:7]
+    for load in loads[:3]:
+        load.wait()
+    line = lax.broadcasted_iota(jnp.int32, (512, 128), 0)
+    live[...] = jnp.where(line < count[0:1, :] * 128, 1.0, 0.0).astype(F32)
+    for b in range(4):
+        rows = pl.ds(b * 128, 128)
+        send_row, recv_row = senders[pl.ds(b, 1), :], receivers[pl.ds(b, 1), :]
+        pick_send[rows, :] = pick_rows(send_row, 768)
+        pick_recv[rows, :] = pick_rows(recv_row, 512)
+        place_recv[:, rows] = place_rows(recv_row, 512)
+        place_send[:, rows] = place_rows(send_row, 768)
+    for load in loads[3:]:
+        load.wait()
+    low = dot(pick_recv[...], nodes[...]).astype(BF16)
+    receiver[...] = low
+    partial[...] = dot(jnp.concatenate([edges[...], low], axis=1), around(ew1)) + eb1[...]
+
+
+def around(weight):
+    return jnp.concatenate([weight[0:128, :], weight[256:384, :]], axis=0)
+
+
+def main_kernel(near, far, *refs):
     (
-        table, pick_recv, place_recv, place_send, messages, inputs, hidden, slope, normed, inverse,
-        spread, dxs, dxr, first_low, second_low, node_inputs, node_hidden, node_first, node_second, grads,
-        arrive, leave,
-    ) = refs
-    loads = [pltpu.make_async_copy(a, b, arrive.at[k]) for k, (a, b) in enumerate(zip(sources, landed))]
+        (_, _, _, nodes, edges, ew1, _, ew2, eb2, egain, eshift, nw1, nb1, nw2, nb2, ngain, nshift, node_cot, edge_cot),
+        (receiver, partial, live, pick_send, pick_recv, place_recv, place_send),
+        (node_out, edge_out, grad_edge, local_grad, far_grad, keep, send),
+        left,
+        (
+            table, messages, hidden, slope, normed, inverse, spread, dxs, dxr, sender, first_low, second_low,
+            node_inputs, node_hidden, node_first, node_second, grads, leave,
+        ),
+    ) = refs[:19], refs[19:26], refs[26:33], refs[33:36], refs[36:]
     stores = [
         pltpu.make_async_copy(a, b, leave.at[k])
         for k, (a, b) in enumerate(zip(left, (edge_out, node_out, grad_edge)))
     ]
-    for load in loads:
-        load.start()
-    (
-        senders, receivers, nodes, edges, ew1, eb1, ew2, eb2, egain, eshift,
-        nw1, nb1, nw2, nb2, ngain, nshift, node_cot, edge_cot,
-    ) = landed
     edge_left, node_left, grad_left = left
     core = lax.axis_index("c")
-    live_blocks = count[0, 0]
+    table[pl.ds(0, 512), :] = nodes[...]
     table[pl.ds(pl.multiple_of(640 - 128 * core, 128), 128), :] = near[...]
     table[pl.ds(pl.multiple_of(512 + 128 * core, 128), 128), :] = far[...]
-    for load in loads[:10]:
-        load.wait()
-    for b in range(4):
-        rows = pl.ds(b * 128, 128)
-        send_row, recv_row = senders[pl.ds(b, 1), :], receivers[pl.ds(b, 1), :]
-        pick_recv[rows, :] = pick_rows(recv_row, 512)
-        place_recv[:, rows] = place_rows(recv_row, 512)
-        place_send[:, rows] = place_rows(send_row, 768)
-
-    table[pl.ds(0, 512), :] = nodes[...]
-    live = is_live(live_blocks)
+
     own = edges[...]
-    picks = jnp.concatenate([pick_rows(senders[pl.ds(k, 1), :], 768) for k in range(4)], axis=0)
-    sender = dot(picks, table[...]).astype(BF16)
-    receiver = dot(pick_recv[...], nodes[...]).astype(BF16)
-    gathered = jnp.concatenate([own, sender, receiver], axis=1)
-    inputs[...] = gathered
-    first = dot(gathered, ew1[...]) + eb1[...]
+    low = dot(pick_send[...], table[...]).astype(BF16)
+    sender[...] = low
+    first = partial[...] + dot(low, ew1[128:256, :])
     sigmoid = jax.nn.sigmoid(first)
     low = (first * sigmoid).astype(BF16)
     hidden[...] = low
@@ -156,13 +163,11 @@
     n, inv = norm_forward(dot(low, ew2[...]) + eb2[...])
     normed[...] = n
     inverse[...] = inv
-    message = (n * egain[...] + eshift[...]) * live
+    message = (n * egain[...] + eshift[...]) * live[...]
     edge_left[...] = (own.astype(F32) + message).astype(BF16)
     messages[...] = split(message)
 
     stores[0].start()
-    for load in loads[10:]:
-        load.wait()
     sums = [jnp.zeros((8, 128), F32) for _ in range(8)]
     aggregate = joined(dot(place_recv[...], messages[...])).astype(BF16)
     own = nodes[...]
@@ -188,9 +193,8 @@
         sums[4 + k] += partial_sum(piece)
     stores[1].start()
 
-    live = is_live(live_blocks)
     edge_grad = edge_cot[...].astype(F32)
-    cot = live * (edge_grad + joined(dot(pick_recv[...], spread[...])))
+    cot = live[...] * (edge_grad + joined(dot(pick_recv[...], spread[...])))
     n = normed[...]
     g2 = norm_backward(cot, n, inverse[...], egain[...])
     g2_low = g2.astype(BF16)
@@ -209,10 +213,12 @@
     lower = joined(dot(place_send[512:640, :], dxs[...])).astype(BF16)
     upper = joined(dot(place_send[640:768, :], dxs[...])).astype(BF16)
     is_first = core == 0
-    near_grad[...] = jnp.where(is_first, upper, lower)
+    send[HALF:, :] = jnp.where(is_first, upper, lower)
     far_grad[...] = jnp.where(is_first, lower, upper)
 
-    grads[0:384, :] = dot_tn(inputs[...], first_low[...])
+    grads[0:128, :] = dot_tn(edges[...], first_low[...])
+    grads[128:256, :] = dot_tn(sender[...], first_low[...])
+    grads[256:384, :] = dot_tn(receiver[...], first_low[...])
     grads[384:385, :] = total(sums[0])
     grads[385:513, :] = dot_tn(hidden[...], second_low[...])
     grads[513:514, :] = total(sums[1])
@@ -225,7 +231,8 @@
     grads[902:903, :] = total(sums[6])
     grads[903:904, :] = total(sums[7])
     grads[904:1024, :] = jnp.zeros((120, 128), F32)
-    send[...] = grads[...].astype(BF16)
+    keep[...] = grads[pl.ds(pl.multiple_of(core * HALF, HALF), HALF), :]
+    send[0:HALF, :] = grads[pl.ds(pl.multiple_of((1 - core) * HALF, HALF), HALF), :].astype(BF16)
 
     for b in range(4):
         rows = pl.ds(b * 128, 128)
@@ -276,6 +283,38 @@
     return jax.ShapeDtypeStruct((rows, width), kind)
 
 
+def prepare(sources):
+    outs = tuple(jax.ShapeDtypeStruct(source.shape, source.dtype) for source in sources) + (
+        shape(512, 128, BF16), shape(512, 128, F32), shape(512, 128, F32), shape(512, 768, BF16),
+        shape(512, 512, BF16), shape(512, 512, BF16), shape(768, 512, BF16),
+    )
+    return call(
+        prepare_kernel, outs, (sources[0], *(in_hbm(source) for source in sources[1:])), [VMEM] + [HBM] * 18,
+        scratch=[pltpu.SemaphoreType.DMA((19,))], flops=400000000, vmem=16 << 20,
+    )
+
+
+def compute(near, far, prepared):
+    outs = (
+        shape(512, 128, BF16), shape(512, 128, BF16), shape(512, 128, BF16), shape(512, 128, F32),
+        shape(128, 128, BF16), shape(HALF, 128, F32), shape(HALF + 128, 128, BF16),
+    )
+    scratch = [
+        pltpu.VMEM(dims, kind)
+        for dims, kind in (
+            ((512, 128), BF16), ((512, 128), BF16), ((512, 128), BF16),
+            ((768, 128), BF16), ((512, 256), BF16), ((512, 128), BF16), ((512, 128), F32),
+            ((512, 128), F32), ((512, 1), F32), ((512, 256), BF16), ((512, 256), BF16), ((512, 256), BF16),
+            ((512, 128), BF16), ((512, 128), BF16), ((512, 128), BF16), ((512, 256), BF16), ((512, 128), BF16),
+            ((512, 128), BF16), ((512, 128), BF16), ((ROWS, 128), F32),
+        )
+    ] + [pltpu.SemaphoreType.DMA((3,))]
+    return call(
+        main_kernel, outs, (near, far, *prepared), [VMEM] * 28,
+        (HBM,) * 3 + (VMEM,) * 4, scratch, 2000000000, 24 << 20,
+    )
+
+
 def layer(
     nodes, edges, senders, receivers, block_count, send_rows, node_cot, edge_cot,
     edge_w1, edge_b1, edge_w2, edge_b2, edge_gain, edge_shift,
@@ -298,43 +337,27 @@
     near = lax.ppermute(near, DOM, near_pairs)
 
     sources = (
-        senders[0], receivers[0], own_nodes, edges[0].reshape(512, 128),
+        jnp.broadcast_to(block_count, (8, 128)), senders[0], receivers[0], own_nodes, edges[0].reshape(512, 128),
         edge_w1, line(edge_b1), edge_w2, line(edge_b2), line(edge_gain), line(edge_shift),
         node_w1, line(node_b1), node_w2, line(node_b2), line(node_gain), line(node_shift),
         node_cot[0], edge_cot[0].reshape(512, 128),
     )
-    outs = (
-        shape(512, 128, BF16), shape(512, 128, BF16), shape(512, 128, BF16), shape(512, 128, F32),
-        shape(128, 128, BF16), shape(128, 128, BF16), shape(ROWS, 128, BF16),
-    )
-    scratch = [pltpu.VMEM(source.shape, source.dtype) for source in sources]
-    scratch += [
-        pltpu.VMEM(dims, kind)
-        for dims, kind in (
-            ((512, 128), BF16), ((512, 128), BF16), ((512, 128), BF16),
-            ((768, 128), BF16), ((512, 512), BF16), ((512, 512), BF16), ((768, 512), BF16),
-            ((512, 256), BF16), ((512, 384), BF16), ((512, 128), BF16), ((512, 128), F32),
-            ((512, 128), F32), ((512, 1), F32), ((512, 256), BF16), ((512, 256), BF16), ((512, 256), BF16),
-            ((512, 128), BF16), ((512, 128), BF16), ((512, 256), BF16), ((512, 128), BF16),
-            ((512, 128), BF16), ((512, 128), BF16), ((ROWS, 128), F32),
-        )
-    ] + [pltpu.SemaphoreType.DMA((18,)), pltpu.SemaphoreType.DMA((3,))]
-    node_out, edge_out, grad_edge, local_grad, near_grad, far_grad, send = call(
-        main_kernel, outs, (block_count, near, far)
-        + tuple(in_hbm(source) for source in sources),
-        [SMEM, VMEM, VMEM] + [HBM] * 18, (HBM,) * 3 + (VMEM,) * 4, scratch, 2000000000, 24 << 20,
-    )
-
+    prepared = prepare(sources)
+    node_out, edge_out, grad_edge, local_grad, far_grad, keep, send = compute(near, far, prepared)
+
+    arrived = lax.ppermute(send, "c", [(0, 1), (1, 0)])
     far_back = lax.ppermute(far_grad, DOM, far_pairs)
-    near_back = lax.ppermute(near_grad, DOM, near_pairs)
+    near_back = arrived[HALF:]
     scale = 1.0 / math.sqrt(lax.axis_size(DOM) * lax.axis_size("x") * 512)
     planes, columns = lax.axis_size(PLANE), lax.axis_size(COLUMN)
-    rows = ROWS // planes
-    tiles = lax.all_to_all(send.reshape(planes, rows, 128), PLANE, 0, 0, tiled=True)
+    rows = HALF // planes
+    pair = (keep + arrived[:HALF].astype(F32)).astype(BF16)
+    tiles = lax.all_to_all(pair.reshape(planes, rows, 128), PLANE, 0, 0, tiled=True)
     copies = fold(tiles, columns, 1.0)
     tiles = lax.all_to_all(copies, COLUMN, 0, 0, tiled=True)
     copies = fold(tiles, planes, scale)
-    whole = lax.all_to_all(copies, PLANE, 0, 0, tiled=True).reshape(ROWS, 128)
+    half = lax.all_to_all(copies, PLANE, 0, 0, tiled=True).reshape(HALF, 128)
+    whole = lax.all_gather(half, "c", axis=0, tiled=True)
     weight_grads = whole[:LIVE_ROWS].astype(F32).reshape(LIVE_ROWS * 128)
 
     grad_node = call(finish_kernel, shape(512, 128, BF16), (local_grad, near_back, far_back, lists), vmem=SMALL)

time: 61.9 us -> 62.1 us (level)
  waiting for transfers between devices: 7.27 us -> 3.5 us
  blocking collectives: 30 us -> 32.5 us
  Pallas kernels: 8.14 us -> 9.46 us
    all_gather x0 -> x1, blocking collectives: none -> 4.71 us  [layer(): whole = lax.all_gather(half, 'c', axis=0, tiled=True)]
    ppermute x1, starting transfers between devices: 2.46 us -> 5.3 us  [layer(): far_back = lax.ppermute(far_grad, DOM, far_pairs)]
    all_to_all x1, starting transfers between devices: 6.06 us -> 3.51 us  [layer(): half = lax.all_to_all(copies, PLANE, 0, 0, tiled=True).reshape(HALF, 128)]
    ppermute x1, waiting for transfers between devices: 2.65 us -> 0.26 us  [layer(): far = lax.ppermute(far, DOM, far_pairs)]
    all_to_all x1, blocking collectives: 12.2 us -> 10.7 us  [layer(): tiles = lax.all_to_all(copies, COLUMN, 0, 0, tiled=True)]
    all_to_all x1, waiting for transfers between devices: 1.45 us -> 0.01 us  [layer(): half = lax.all_to_all(copies, PLANE, 0, 0, tiled=True).reshape(HALF, 128)]
    ppermute x1, waiting for transfers between devices: 0.01 us -> 1.38 us  [layer(): arrived = lax.ppermute(send, 'c', [(0, 1), (1, 0)])]
    pallas_call x5 -> x6, Pallas kernels: 8.14 us -> 9.46 us  [call(): pl.pallas_call(body, out_shape=out_shape, in_specs=in_specs or [VMEM] * l...]
  transfers between devices with their start and end apart: 5 -> 5, of which waited for: 3 -> 3; matrix products, arithmetic and copies ran while one was open for 0% -> 0% of each run, Pallas kernels for 1% -> 5%
where the time goes in v5:
time: 62.1 us; the launch traced here: 61.8 us
  blocking collectives  32.5 us (52%)
  starting transfers between devices  14.1 us (23%)
  Pallas kernels  9.46 us (15%)
  waiting for transfers between devices  3.5 us (6%)
  between operations  1.38 us (2%)
  other arithmetic  0.83 us (1%)
    all_to_all x1, blocking collectives, layer(): lax.all_to_all(pair.reshape(planes, rows, 128), PLANE, 0, 0, tiled=True)  17.1 us
    all_to_all x1, blocking collectives, layer(): tiles = lax.all_to_all(copies, COLUMN, 0, 0, tiled=True)  10.7 us
    pallas_call x6, Pallas kernels, call(): pl.pallas_call(body, out_shape=out_shape, in_specs=in_specs or [VMEM] * l...  9.46 us
    ppermute x1, starting transfers between devices, layer(): far_back = lax.ppermute(far_grad, DOM, far_pairs)  5.3 us
    all_gather x1, blocking collectives, layer(): whole = lax.all_gather(half, 'c', axis=0, tiled=True)  4.71 us
    all_to_all x1, starting transfers between devices, layer(): half = lax.all_to_all(copies, PLANE, 0, 0, tiled=True).reshape(HALF, 128)  3.51 us
    ppermute x1, starting transfers between devices, layer(): near = lax.ppermute(near, DOM, near_pairs)  3.29 us
    ppermute x1, starting transfers between devices, layer(): far = lax.ppermute(far, DOM, far_pairs)  1.91 us
  transfers between devices with their start and end apart: 5, of which 3 were waited for; matrix products, arithmetic and copies ran while one was open for 0% of the time, Pallas kernels for 5%

profile of v5, /device:TPU:1, one launch (start us, length us, event | category | flops | bytes accessed | tf_op | source)
XLA Modules:
  0.0 61.8 jit_solution(12698217863447394415)
XLA Ops:
  0.6 1.2 %shard_map.227 = (bf16[128,128]{1,0:T(8,128)(2,1)S(1)}, bf16[128,128]{1,0:T(8,128)(2,1)S(1)}) custom-call(bf16[512,128]{1,0:T(8,128)(2,1)} %bitcast.33, s32[2,128]{1,0:T(2,128)} %bitcast.28), custom_call_target="tpu_custom_call" | custom-call | flops 1000000 | bytes 1000000 | tf_op jit(solution)/shard_map/pallas_call | solution.py:262
  1.9 3.3 %collective-permute-start = (bf16[128,128]{1,0:T(8,128)(2,1)S(1)}, bf16[128,128]{1,0:T(8,128)(2,1)S(1)}, u32[]{:S(2)}, u32[]{:S(2)}) collective-permute-start(bf16[128,128]{1,0:T(8,128)(2,1)S(1)} %get-tuple-element.40), channel_id=1, source_target_pairs={{0,4},{4,0},{8,12},{12,8},{16,20},{20,16},{24,28},{28,24},{32,36},... | collective-permute-start | bytes 98312 | tf_op jit(solution)/shard_map/ppermute | solution.py:337
  5.1 1.9 %collective-permute-start.1 = (bf16[128,128]{1,0:T(8,128)(2,1)S(1)}, bf16[128,128]{1,0:T(8,128)(2,1)S(1)}, u32[]{:S(2)}, u32[]{:S(2)}) collective-permute-start(bf16[128,128]{1,0:T(8,128)(2,1)S(1)} %get-tuple-element.41), channel_id=1, source_target_pairs={{4,8},{12,16},{20,24},{28,32},{36,40},{44,48},{52,56},{60,64},{68,... | collective-permute-start | bytes 98312 | tf_op jit(solution)/shard_map/ppermute | solution.py:336
  7.7 2.4 %shard_map.228 = (s32[8,128]{1,0:T(8,128)S(1)}, s32[4,128]{1,0:T(4,128)S(1)}, s32[4,128]{1,0:T(4,128)S(1)}, bf16[512,128]{1,0:T(8,128)(2,1)S(1)}, bf16[512,128]{...) custom-call(s32[8,128]{1,0:T(8,128)S(1)} %broadcast_in_dim.14.refs_0, ...), custom_call_target="tpu_custom_call" | custom-call | flops 400000000 | bytes 1000000 | tf_op jit(solution)/shard_map/pallas_call | solution.py:262
  10.1 0.0 collective-permute-done.near
  10.1 0.3 collective-permute-done.1.far
  10.4 4.3 %shard_map.229 = (bf16[512,128]{1,0:T(8,128)(2,1)}, bf16[512,128]{1,0:T(8,128)(2,1)}, bf16[512,128]{1,0:T(8,128)(2,1)}, f32[512,128]{1,0:T(8,128)S(1)}, bf16[128...) custom-call(bf16[128,128]{1,0:T(8,128)(2,1)S(1)} %collective-permute-done.near, ...), custom_call_target="tpu_custom_call" | custom-call | flops 2000000000 | bytes 1000000 | tf_op jit(solution)/shard_map/pallas_call | solution.py:262
  14.7 0.1 collective-permute-start.2
  14.8 1.4 %collective-permute-done.2 = bf16[640,128]{1,0:T(8,128)(2,1)S(1)} collective-permute-done((bf16[640,128]{1,0:T(8,128)(2,1)S(1)}, bf16[640,128]{1,0:T(8,128)(2,1)S(1)}, u32[]{:S(2)}, u32[]{:S(2)}) %collective-permute-start.2) | collective-permute-done | bytes 163872 | tf_op jit(solution)/shard_map/ppermute | solution.py:348
  16.2 17.1 %all_to_all.15.tiles = bf16[16,32,128]{2,1,0:T(8,128)(2,1)S(1)} all-to-all(bf16[16,32,128]{2,1,0:T(8,128)(2,1)S(1)} %bitcast.31), channel_id=1, replica_groups=mesh['y'=4,'z'=8,'c'=2,'x'=4] {'y','x'}, dimensions={0} | all-to-all | bytes 262144 | tf_op jit(solution)/shard_map/all_to_all | solution.py:355
  33.3 10.7 %all_to_all.16.tiles = bf16[8,32,128]{2,1,0:T(8,128)(2,1)S(1)} all-to-all(bf16[8,32,128]{2,1,0:T(8,128)(2,1)S(1)} %shard_map.231), channel_id=1, replica_groups=mesh['y'=4,'z'=8,'c'=2,'x'=4] {'z'}, dimensions={0} | all-to-all | bytes 131072 | tf_op jit(solution)/shard_map/all_to_all | solution.py:357
  44.0 0.7 %shard_map.232 = bf16[16,32,128]{2,1,0:T(8,128)(2,1)} custom-call(bf16[8,32,128]{2,1,0:T(8,128)(2,1)S(1)} %all_to_all.16.tiles), custom_call_target="tpu_custom_call" | custom-call | flops 1000000 | bytes 1000000 | tf_op jit(solution)/shard_map/pallas_call | solution.py:262
  44.6 3.5 %all-to-all-start.2 = ((bf16[16,32,128]{2,1,0:T(8,128)(2,1)}), bf16[16,32,128]{2,1,0:T(8,128)(2,1)S(1)}, u32[]{:S(2)}, u32[]{:S(2)}) async-start(bf16[16,32,128]{2,1,0:T(8,128)(2,1)} %shard_map.232), calls=%async_computation.2 | async-start | bytes 262144 | tf_op jit(solution)/shard_map/all_to_all | solution.py:359
  48.2 5.3 %collective-permute-start.3 = (bf16[128,128]{1,0:T(8,128)(2,1)S(1)}, bf16[128,128]{1,0:T(8,128)(2,1)S(1)}, u32[]{:S(2)}, u32[]{:S(2)}) collective-permute-start(bf16[128,128]{1,0:T(8,128)(2,1)S(1)} %get-tuple-element.72), channel_id=1, source_target_pairs={{4,8},{12,16},{20,24},{28,32},{36,40},{44,48},{52,56},{60,64},{68,... | collective-permute-start | bytes 98312 | tf_op jit(solution)/shard_map/ppermute | solution.py:349
  53.5 0.0 copy-start
  53.5 1.9 %collective-permute-done.3.far = bf16[128,128]{1,0:T(8,128)(2,1)S(1)} collective-permute-done((bf16[128,128]{1,0:T(8,128)(2,1)S(1)}, bf16[128,128]{1,0:T(8,128)(2,1)S(1)}, u32[]{:S(2)}, u32[]{:S(2)}) %collective-permute-start.3) | collective-permute-done | bytes 32800 | tf_op jit(solution)/shard_map/ppermute | solution.py:349
  55.4 0.0 copy-done
  55.4 0.9 %shard_map.230 = bf16[512,128]{1,0:T(8,128)(2,1)} custom-call(f32[512,128]{1,0:T(8,128)S(1)} %get-tuple-element.70.local_grad, bf16[128,128]{1,0:T(8,128)(2,1)S(1)} %slice.12.near, bf16[128,128]{1,0:T(8,128)(2,1)S(1)} %collective-permute-done.3.far, s32[2,128]{1,0:T(2,128)S(1)} %bitcast.29), custom_call_target="tpu_custom_call" | custom-call | flops 1000000 | bytes 1000000 | tf_op jit(solution)/shard_map/pallas_call | solution.py:262
  56.2 0.0 all-to-all-done.2
  56.3 4.7 %all_gather.3 = bf16[1024,128]{1,0:T(8,128)(2,1)S(1)} all-gather(bf16[512,128]{1,0:T(8,128)(2,1)S(1)} %bitcast.30), channel_id=1, replica_groups=mesh['y'=4,'z'=8,'c'=2,'x'=4] {'c'}, dimensions={0}, use_global_device_ids=true | all-gather | bytes 393216 | tf_op jit(solution)/shard_map/all_gather | solution.py:360
  61.0 0.8 %fusion = f32[115712]{0:T(1024)} fusion(bf16[1024,128]{1,0:T(8,128)(2,1)S(1)} %all_gather.3), kind=kLoop, calls=%fused_computation.2 | loop fusion | flops 115712 | bytes 694272 | tf_op jit(solution)/shard_map/reshape | solution.py:361
  (4 shorter events, 0.1 us)
Async XLA Ops:
  1.9 8.2 %collective-permute-start = (bf16[128,128]{1,0:T(8,128)(2,1)S(1)}, bf16[128,128]{1,0:T(8,128)(2,1)S(1)}, u32[]{:S(2)}, u32[]{:S(2)}) collective-permute-start(bf16[128,128]{1,0:T(8,128)(2,1)S(1)} %get-tuple-element.40), channel_id=1, source_target_pairs={{0,4},{4,0},{8,12},{12,8},{16,20},{20,16},{24,28},{28,24},{32,36},... | collective-permute-start | bytes 98312 | tf_op jit(solution)/shard_map/ppermute | solution.py:337
  5.1 5.2 %collective-permute-start.1 = (bf16[128,128]{1,0:T(8,128)(2,1)S(1)}, bf16[128,128]{1,0:T(8,128)(2,1)S(1)}, u32[]{:S(2)}, u32[]{:S(2)}) collective-permute-start(bf16[128,128]{1,0:T(8,128)(2,1)S(1)} %get-tuple-element.41), channel_id=1, source_target_pairs={{4,8},{12,16},{20,24},{28,32},{36,40},{44,48},{52,56},{60,64},{68,... | collective-permute-start | bytes 98312 | tf_op jit(solution)/shard_map/ppermute | solution.py:336
  14.7 1.5 %collective-permute-start.2 = (bf16[640,128]{1,0:T(8,128)(2,1)S(1)}, bf16[640,128]{1,0:T(8,128)(2,1)S(1)}, u32[]{:S(2)}, u32[]{:S(2)}) collective-permute-start(bf16[640,128]{1,0:T(8,128)(2,1)S(1)} %get-tuple-element.71), channel_id=1, source_target_pairs={{0,4},{4,0},{1,5},{5,1},{2,6},{6,2},{3,7},{7,3},{8,12},{12,8},{9,1... | collective-permute-start | bytes 491528 | tf_op jit(solution)/shard_map/ppermute | solution.py:348
  44.6 11.6 %all-to-all-start.2 = ((bf16[16,32,128]{2,1,0:T(8,128)(2,1)}), bf16[16,32,128]{2,1,0:T(8,128)(2,1)S(1)}, u32[]{:S(2)}, u32[]{:S(2)}) async-start(bf16[16,32,128]{2,1,0:T(8,128)(2,1)} %shard_map.232), calls=%async_computation.2 | async-start | bytes 262144 | tf_op jit(solution)/shard_map/all_to_all | solution.py:359
  48.2 7.2 %collective-permute-start.3 = (bf16[128,128]{1,0:T(8,128)(2,1)S(1)}, bf16[128,128]{1,0:T(8,128)(2,1)S(1)}, u32[]{:S(2)}, u32[]{:S(2)}) collective-permute-start(bf16[128,128]{1,0:T(8,128)(2,1)S(1)} %get-tuple-element.72), channel_id=1, source_target_pairs={{4,8},{12,16},{20,24},{28,32},{36,40},{44,48},{52,56},{60,64},{68,... | collective-permute-start | bytes 98312 | tf_op jit(solution)/shard_map/ppermute | solution.py:349
  53.5 1.9 %copy-start = (s32[1,1,2,128]{3,2,1,0:T(2,128)S(1)}, s32[1,1,2,128]{3,2,1,0:T(2,128)}, u32[]{:S(2)}) copy-start(s32[1,1,2,128]{3,2,1,0:T(2,128)} %param.25) | copy-start | bytes 3076

commit v6 on v5

--- a/solution.py
+++ b/solution.py
@@ -1,4 +1,3 @@
-import functools
 import math
 
 import jax
@@ -17,7 +16,6 @@
 BF16 = jnp.bfloat16
 ROWS = 1024
 LIVE_ROWS = 904
-HALF = 512
 SMALL = 8 << 20
 VMEM = pl.BlockSpec(memory_space=pltpu.VMEM)
 SMEM = pl.BlockSpec(memory_space=pltpu.SMEM)
@@ -135,13 +133,13 @@
     (
         (_, _, _, nodes, edges, ew1, _, ew2, eb2, egain, eshift, nw1, nb1, nw2, nb2, ngain, nshift, node_cot, edge_cot),
         (receiver, partial, live, pick_send, pick_recv, place_recv, place_send),
-        (node_out, edge_out, grad_edge, local_grad, far_grad, keep, send),
+        (node_out, edge_out, grad_edge, local_grad, keep, send),
         left,
         (
             table, messages, hidden, slope, normed, inverse, spread, dxs, dxr, sender, first_low, second_low,
-            node_inputs, node_hidden, node_first, node_second, grads, leave,
+            node_inputs, node_hidden, node_first, node_second, leave,
         ),
-    ) = refs[:19], refs[19:26], refs[26:33], refs[33:36], refs[36:]
+    ) = refs[:19], refs[19:26], refs[26:32], refs[32:35], refs[35:]
     stores = [
         pltpu.make_async_copy(a, b, leave.at[k])
         for k, (a, b) in enumerate(zip(left, (edge_out, node_out, grad_edge)))
@@ -150,7 +148,10 @@
     core = lax.axis_index("c")
     table[pl.ds(0, 512), :] = nodes[...]
     table[pl.ds(pl.multiple_of(640 - 128 * core, 128), 128), :] = near[...]
-    table[pl.ds(pl.multiple_of(512 + 128 * core, 128), 128), :] = far[...]
+    place = lax.axis_index("y") * lax.axis_size("z") + lax.axis_index("z")
+    last = lax.axis_size("y") * lax.axis_size("z") - 1
+    alone = place == core * last
+    table[pl.ds(pl.multiple_of(512 + 128 * core, 128), 128), :] = jnp.where(alone, 0.0, far[...].astype(F32)).astype(BF16)
 
     own = edges[...]
     low = dot(pick_send[...], table[...]).astype(BF16)
@@ -213,26 +214,25 @@
     lower = joined(dot(place_send[512:640, :], dxs[...])).astype(BF16)
     upper = joined(dot(place_send[640:768, :], dxs[...])).astype(BF16)
     is_first = core == 0
-    send[HALF:, :] = jnp.where(is_first, upper, lower)
-    far_grad[...] = jnp.where(is_first, lower, upper)
-
-    grads[0:128, :] = dot_tn(edges[...], first_low[...])
-    grads[128:256, :] = dot_tn(sender[...], first_low[...])
-    grads[256:384, :] = dot_tn(receiver[...], first_low[...])
-    grads[384:385, :] = total(sums[0])
-    grads[385:513, :] = dot_tn(hidden[...], second_low[...])
-    grads[513:514, :] = total(sums[1])
-    grads[514:515, :] = total(sums[2])
-    grads[515:516, :] = total(sums[3])
-    grads[516:772, :] = dot_tn(node_inputs[...], node_first[...])
-    grads[772:773, :] = total(sums[4])
-    grads[773:901, :] = dot_tn(node_hidden[...], node_second[...])
-    grads[901:902, :] = total(sums[5])
-    grads[902:903, :] = total(sums[6])
-    grads[903:904, :] = total(sums[7])
-    grads[904:1024, :] = jnp.zeros((120, 128), F32)
-    keep[...] = grads[pl.ds(pl.multiple_of(core * HALF, HALF), HALF), :]
-    send[0:HALF, :] = grads[pl.ds(pl.multiple_of((1 - core) * HALF, HALF), HALF), :].astype(BF16)
+    send[ROWS : ROWS + 128, :] = jnp.where(is_first, upper, lower)
+    send[ROWS + 128 :, :] = jnp.where(is_first, lower, upper)
+
+    keep[0:128, :] = dot_tn(edges[...], first_low[...])
+    keep[128:256, :] = dot_tn(sender[...], first_low[...])
+    keep[256:384, :] = dot_tn(receiver[...], first_low[...])
+    keep[384:385, :] = total(sums[0])
+    keep[385:513, :] = dot_tn(hidden[...], second_low[...])
+    keep[513:514, :] = total(sums[1])
+    keep[514:515, :] = total(sums[2])
+    keep[515:516, :] = total(sums[3])
+    keep[516:772, :] = dot_tn(node_inputs[...], node_first[...])
+    keep[772:773, :] = total(sums[4])
+    keep[773:901, :] = dot_tn(node_hidden[...], node_second[...])
+    keep[901:902, :] = total(sums[5])
+    keep[902:903, :] = total(sums[6])
+    keep[903:904, :] = total(sums[7])
+    keep[904:1024, :] = jnp.zeros((120, 128), F32)
+    send[0:ROWS, :] = keep[...].astype(BF16)
 
     for b in range(4):
         rows = pl.ds(b * 128, 128)
@@ -242,20 +242,25 @@
         store.wait()
 
 
-def fold_kernel(scale, tiles, copies):
-    summed = tiles[0].astype(F32)
-    for k in range(1, tiles.shape[0]):
-        summed += tiles[k].astype(F32)
-    low = (summed * scale).astype(BF16)
-    for k in range(copies.shape[0]):
-        copies[k] = low
-
-
-def finish_kernel(local_grad, near, far, lists, out):
+def finish_kernel(
+    local_grad, near, turned, downward, result, received, lists, grad_node, weight_grads, node_left, weight_left, leave
+):
     core = lax.axis_index("c")
+    is_first = core == 0
+    stores = [
+        pltpu.make_async_copy(weight_left, weight_grads, leave.at[0]),
+        pltpu.make_async_copy(node_left, grad_node, leave.at[1]),
+    ]
+    whole = jnp.where(is_first, received[0:LIVE_ROWS, :].astype(F32), result[0:LIVE_ROWS, :].astype(F32))
+    weight_left[...] = whole
+    stores[0].start()
+    far = jnp.where(is_first, turned[0:128, :].astype(F32), downward[...].astype(F32)).astype(BF16)
     added = dot(place_rows(lists[pl.ds(1 - core, 1), :], 512), near[...])
-    added += dot(place_rows(lists[pl.ds(core, 1), :], 512), far[...])
-    out[...] = (local_grad[...] + added).astype(BF16)
+    added += dot(place_rows(lists[pl.ds(core, 1), :], 512), far)
+    node_left[...] = (local_grad[...] + added).astype(BF16)
+    stores[1].start()
+    for store in stores:
+        store.wait()
 
 
 def call(body, out_shape, operands, in_specs=None, out_specs=None, scratch=(), flops=1000000, vmem=None):
@@ -270,11 +275,6 @@
     )(*operands)
 
 
-def fold(tiles, count, scale):
-    out = jax.ShapeDtypeStruct((count, *tiles.shape[1:]), BF16)
-    return call(functools.partial(fold_kernel, scale), out, (tiles,), vmem=SMALL)
-
-
 def in_hbm(value):
     return pltpu.with_memory_space_constraint(value, pltpu.HBM)
 
@@ -297,7 +297,7 @@
 def compute(near, far, prepared):
     outs = (
         shape(512, 128, BF16), shape(512, 128, BF16), shape(512, 128, BF16), shape(512, 128, F32),
-        shape(128, 128, BF16), shape(HALF, 128, F32), shape(HALF + 128, 128, BF16),
+        shape(ROWS, 128, F32), shape(ROWS + 256, 128, BF16),
     )
     scratch = [
         pltpu.VMEM(dims, kind)
@@ -306,12 +306,12 @@
             ((768, 128), BF16), ((512, 256), BF16), ((512, 128), BF16), ((512, 128), F32),
             ((512, 128), F32), ((512, 1), F32), ((512, 256), BF16), ((512, 256), BF16), ((512, 256), BF16),
             ((512, 128), BF16), ((512, 128), BF16), ((512, 128), BF16), ((512, 256), BF16), ((512, 128), BF16),
-            ((512, 128), BF16), ((512, 128), BF16), ((ROWS, 128), F32),
+            ((512, 128), BF16), ((512, 128), BF16),
         )
     ] + [pltpu.SemaphoreType.DMA((3,))]
     return call(
         main_kernel, outs, (near, far, *prepared), [VMEM] * 28,
-        (HBM,) * 3 + (VMEM,) * 4, scratch, 2000000000, 24 << 20,
+        (HBM,) * 3 + (VMEM,) * 3, scratch, 2000000000, 24 << 20,
     )
 
 
@@ -324,7 +324,9 @@
     lists = send_rows[0, 0]
     line = lambda vector: vector.reshape(1, 128)
     near_pairs = [(j, j ^ 1) for j in range(64)]
-    far_pairs = [(j, j + 1) for j in range(1, 63, 2)] + [(j + 1, j) for j in range(1, 63, 2)]
+    far_pairs = [(j, (j + 1) % 64) for j in range(1, 64, 2)] + [((j + 1) % 64, j) for j in range(1, 64, 2)]
+    down = [(j, j - 2) for j in range(2, 64, 2)]
+    up = [(j - 2, j) for j in range(2, 64, 2)]
 
     near, far = call(
         pack_kernel, (shape(128, 128, BF16),) * 2, (in_hbm(own_nodes), in_hbm(lists)), [HBM] * 2,
@@ -343,30 +345,48 @@
         node_cot[0], edge_cot[0].reshape(512, 128),
     )
     prepared = prepare(sources)
-    node_out, edge_out, grad_edge, local_grad, far_grad, keep, send = compute(near, far, prepared)
-
-    arrived = lax.ppermute(send, "c", [(0, 1), (1, 0)])
-    far_back = lax.ppermute(far_grad, DOM, far_pairs)
-    near_back = arrived[HALF:]
+    node_out, edge_out, grad_edge, local_grad, keep, send = compute(near, far, prepared)
+
     scale = 1.0 / math.sqrt(lax.axis_size(DOM) * lax.axis_size("x") * 512)
     planes, columns = lax.axis_size(PLANE), lax.axis_size(COLUMN)
-    rows = HALF // planes
-    pair = (keep + arrived[:HALF].astype(F32)).astype(BF16)
-    tiles = lax.all_to_all(pair.reshape(planes, rows, 128), PLANE, 0, 0, tiled=True)
-    copies = fold(tiles, columns, 1.0)
-    tiles = lax.all_to_all(copies, COLUMN, 0, 0, tiled=True)
-    copies = fold(tiles, planes, scale)
-    half = lax.all_to_all(copies, PLANE, 0, 0, tiled=True).reshape(HALF, 128)
-    whole = lax.all_gather(half, "c", axis=0, tiled=True)
-    weight_grads = whole[:LIVE_ROWS].astype(F32).reshape(LIVE_ROWS * 128)
-
-    grad_node = call(finish_kernel, shape(512, 128, BF16), (local_grad, near_back, far_back, lists), vmem=SMALL)
+    arrived = lax.ppermute(send, "c", [(0, 1), (1, 0)])
+    pair = (keep + arrived[:ROWS].astype(F32)).astype(BF16)
+    near_back = arrived[ROWS : ROWS + 128]
+
+    def carry(pair, mine, other):
+        upward, downward = lax.ppermute(other, DOM, up), lax.ppermute(mine, DOM, down)
+        return pair, jnp.concatenate([upward, downward], axis=0)
+
+    def reduce(pair, mine, other):
+        tiles = lax.all_to_all(pair.reshape(planes, -1, 128), PLANE, 0, 0, tiled=True)
+        piece = jnp.sum(tiles.astype(F32), axis=0).astype(BF16)
+        copies = jnp.broadcast_to(piece, (columns, *piece.shape))
+        tiles = lax.all_to_all(copies, COLUMN, 0, 0, tiled=True)
+        piece = (jnp.sum(tiles.astype(F32), axis=0) * scale).astype(BF16)
+        copies = jnp.broadcast_to(piece, (planes, *piece.shape))
+        tiles = lax.all_to_all(copies, PLANE, 0, 0, tiled=True)
+        whole = tiles.reshape(ROWS, 128)
+        return whole, whole[0:256]
+
+    result, turned = lax.cond(
+        lax.axis_index("c") == 0, carry, reduce, pair, send[ROWS + 128 :], arrived[ROWS + 128 :]
+    )
+    received = lax.ppermute(result, "c", [(0, 1), (1, 0)])
+    downward = lax.ppermute(turned[128:], "c", [(0, 1), (1, 0)])
+    grad_node, weight_grads = call(
+        finish_kernel, (shape(512, 128, BF16), shape(LIVE_ROWS, 128, F32)),
+        (local_grad, near_back, turned, downward, result, received, lists), [VMEM] * 7, (HBM,) * 2,
+        [
+            pltpu.VMEM((512, 128), BF16), pltpu.VMEM((LIVE_ROWS, 128), F32), pltpu.SemaphoreType.DMA((2,))
+        ],
+        vmem=SMALL,
+    )
     return (
         node_out[None],
         edge_out.reshape(1, 4, 128, 128),
         grad_node[None],
         grad_edge.reshape(1, 4, 128, 128),
-        weight_grads,
+        weight_grads.reshape(LIVE_ROWS * 128),
     )
 
 

time: 62.1 us -> 58.1 us (0.936)
  starting transfers between devices: 14.1 us -> 10.3 us
  blocking collectives: 32.5 us -> 34.4 us
  waiting for transfers between devices: 3.5 us -> 2.61 us
  other arithmetic: 0.83 us -> 0.13 us
    all_to_all x2 -> x3, blocking collectives: 27.8 us -> 34.4 us  [the longest x1 12.4 us: reduce(): tiles = lax.all_to_all(copies, COLUMN, 0, 0, tiled=True)]
    ppermute x1, starting transfers between devices: 0.09 us -> 6.55 us  [layer(): arrived = lax.ppermute(send, 'c', [(0, 1), (1, 0)])]
    ppermute x1 -> x2, starting transfers between devices: 5.3 us -> 0.5 us  [the longest x1 0.49 us: layer(): downward = lax.ppermute(turned[128:], 'c', [(0, 1), (1, 0)])]
    all_gather x1 -> x0, blocking collectives: 4.71 us -> none  [layer(): whole = lax.all_gather(half, 'c', axis=0, tiled=True)]
    all_to_all x1 -> x0, starting transfers between devices: 3.51 us -> none  [layer(): half = lax.all_to_all(copies, PLANE, 0, 0, tiled=True).reshape(HALF, 128)]
    ppermute x1, starting transfers between devices: 1.91 us -> 0.01 us  [layer(): far = lax.ppermute(far, DOM, far_pairs)]
    reshape x1 -> x0, other arithmetic: 0.8 us -> none  [layer(): weight_grads = whole[:LIVE_ROWS].astype(F32).reshape(LIVE_ROWS * 128)]
    ppermute x1 -> x2, waiting for transfers between devices: 1.85 us -> 1.06 us  [the longest x1 1.06 us: layer(): downward = lax.ppermute(turned[128:], 'c', [(0, 1), (1, 0)])]
  transfers between devices with their start and end apart: 5 -> 5, of which waited for: 3 -> 3; matrix products, arithmetic and copies ran while one was open for 0% -> 0% of each run, Pallas kernels for 5% -> 4%
where the time goes in v6:
time: 58.1 us; the launch traced here: 57.9 us
  blocking collectives  34.4 us (59%)
  starting transfers between devices  10.3 us (18%)
  Pallas kernels  8.89 us (15%)
  waiting for transfers between devices  2.61 us (4%)
  between operations  1.35 us (2%)
    all_to_all x1, blocking collectives, reduce(): tiles = lax.all_to_all(copies, COLUMN, 0, 0, tiled=True)  12.4 us
    all_to_all x1, blocking collectives, reduce(): lax.all_to_all(pair.reshape(planes, -1, 128), PLANE, 0, 0, tiled=True)  11.6 us
    all_to_all x1, blocking collectives, reduce(): tiles = lax.all_to_all(copies, PLANE, 0, 0, tiled=True)  10.4 us
    pallas_call x4, Pallas kernels, call(): pl.pallas_call(body, out_shape=out_shape, in_specs=in_specs or [VMEM] * l...  8.89 us
    ppermute x1, starting transfers between devices, layer(): arrived = lax.ppermute(send, 'c', [(0, 1), (1, 0)])  6.55 us
    ppermute x1, starting transfers between devices, layer(): near = lax.ppermute(near, DOM, near_pairs)  3.29 us
    ppermute x1, waiting for transfers between devices, layer(): arrived = lax.ppermute(send, 'c', [(0, 1), (1, 0)])  1.26 us
  transfers between devices with their start and end apart: 5, of which 3 were waited for; matrix products, arithmetic and copies ran while one was open for 0% of the time, Pallas kernels for 4%

profile of v6, /device:TPU:1, one launch (start us, length us, event | category | flops | bytes accessed | tf_op | source)
XLA Modules:
  0.0 57.9 jit_solution(6134213681107594486)
XLA Ops:
  0.6 1.2 %shard_map.227 = (bf16[128,128]{1,0:T(8,128)(2,1)S(1)}, bf16[128,128]{1,0:T(8,128)(2,1)S(1)}) custom-call(bf16[512,128]{1,0:T(8,128)(2,1)} %bitcast.30, s32[2,128]{1,0:T(2,128)} %bitcast.25), custom_call_target="tpu_custom_call" | custom-call | flops 1000000 | bytes 1000000 | tf_op jit(solution)/shard_map/pallas_call | solution.py:267
  1.9 3.3 %collective-permute-start.2 = (bf16[128,128]{1,0:T(8,128)(2,1)S(1)}, bf16[128,128]{1,0:T(8,128)(2,1)S(1)}, u32[]{:S(2)}, u32[]{:S(2)}) collective-permute-start(bf16[128,128]{1,0:T(8,128)(2,1)S(1)} %get-tuple-element.55), channel_id=1, source_target_pairs={{0,4},{4,0},{8,12},{12,8},{16,20},{20,16},{24,28},{28,24},{32,36},... | collective-permute-start | bytes 98312 | tf_op jit(solution)/shard_map/ppermute | solution.py:339
  5.1 0.0 collective-permute-start.3
  5.8 2.4 %shard_map.228 = (s32[8,128]{1,0:T(8,128)S(1)}, s32[4,128]{1,0:T(4,128)S(1)}, s32[4,128]{1,0:T(4,128)S(1)}, bf16[512,128]{1,0:T(8,128)(2,1)S(1)}, bf16[512,128]{...) custom-call(s32[8,128]{1,0:T(8,128)S(1)} %broadcast_in_dim.20.refs_0, ...), custom_call_target="tpu_custom_call" | custom-call | flops 400000000 | bytes 1000000 | tf_op jit(solution)/shard_map/pallas_call | solution.py:267
  8.2 0.0 collective-permute-done.2.near
  8.2 0.3 collective-permute-done.3.far
  8.5 4.2 %shard_map.229 = (bf16[512,128]{1,0:T(8,128)(2,1)}, bf16[512,128]{1,0:T(8,128)(2,1)}, bf16[512,128]{1,0:T(8,128)(2,1)}, f32[512,128]{1,0:T(8,128)S(1)}, f32[1024...) custom-call(bf16[128,128]{1,0:T(8,128)(2,1)S(1)} %collective-permute-done.2.near, ...), custom_call_target="tpu_custom_call" | custom-call | flops 2000000000 | bytes 1000000 | tf_op jit(solution)/shard_map/pallas_call | solution.py:267
  12.7 6.6 %collective-permute-start.4 = (bf16[1280,128]{1,0:T(8,128)(2,1)S(1)}, bf16[1280,128]{1,0:T(8,128)(2,1)S(1)}, u32[]{:S(2)}, u32[]{:S(2)}) collective-permute-start(bf16[1280,128]{1,0:T(8,128)(2,1)S(1)} %get-tuple-element.86), channel_id=1, source_target_pairs={{0,4},{4,0},{1,5},{5,1},{2,6},{6,2},{3,7},{7,3},{8,12},{12,8},{9,1... | collective-permute-start | bytes 983048 | tf_op jit(solution)/shard_map/ppermute | solution.py:352
  19.2 1.3 %collective-permute-done.4 = bf16[1280,128]{1,0:T(8,128)(2,1)S(1)} collective-permute-done((bf16[1280,128]{1,0:T(8,128)(2,1)S(1)}, bf16[1280,128]{1,0:T(8,128)(2,1)S(1)}, u32[]{:S(2)}, u32[]{:S(2)}) %collective-permute-start.4) | collective-permute-done | bytes 327712 | tf_op jit(solution)/shard_map/ppermute | solution.py:352
  20.5 0.1 add_convert_fusion
  20.6 34.6 %conditional.1 = (bf16[1024,128]{1,0:T(8,128)(2,1)S(1)}, bf16[256,128]{1,0:T(8,128)(2,1)S(1)}) conditional(s32[]{:T(128)} %convert_element_type.20, bf16[1024,128]{1,0:T(8,128)(2,1)S(1)} %add_convert_fusion, (bf16[1280,128]{1,0:T(8,128)(2,1)S(1)}, bf16[1280,128]{1,0:T(8,128)(2,1)S(1)}, bf16[1024,128]{1,0:T(8,128)(2,1)S(1)}) %tuple.16), branch_computations={%region_0.0_spmd, %region_3.0_spmd} | conditional | flops 262144 | bytes 2359314 | solution.py:371
  20.6 11.6 %all_to_all.12 = bf16[16,64,128]{2,1,0:T(8,128)(2,1)S(1)} all-to-all(bf16[16,64,128]{2,1,0:T(8,128)(2,1)S(1)} %bitcast.27), channel_id=1, replica_groups=mesh['y'=4,'z'=8,'c'=2,'x'=4] {'y','x'}, dimensions={0} | all-to-all | bytes 524288 | tf_op jit(solution)/shard_map/cond/branch_0_fun/all_to_all | solution.py:361
  32.3 12.4 %all_to_all.13 = bf16[8,64,128]{2,1,0:T(8,128)(2,1)S(1)} all-to-all(bf16[8,64,128]{2,1,0:T(8,128)(2,1)S(1)} %broadcast_in_dim.7), channel_id=1, replica_groups=mesh['y'=4,'z'=8,'c'=2,'x'=4] {'z'}, dimensions={0} | all-to-all | bytes 262144 | tf_op jit(solution)/shard_map/cond/branch_0_fun/all_to_all | solution.py:364
  44.7 10.4 %all_to_all.14 = bf16[16,64,128]{2,1,0:T(8,128)(2,1)S(1)} all-to-all(bf16[16,64,128]{2,1,0:T(8,128)(2,1)S(1)} %broadcast_in_dim.14), channel_id=1, replica_groups=mesh['y'=4,'z'=8,'c'=2,'x'=4] {'y','x'}, dimensions={0} | all-to-all | bytes 524288 | tf_op jit(solution)/shard_map/cond/branch_0_fun/all_to_all | solution.py:367
  55.2 0.0 collective-permute-start.6
  55.2 0.5 collective-permute-start.5
  55.7 0.0 copy-start
  55.7 1.1 %collective-permute-done.5.downward = bf16[128,128]{1,0:T(8,128)(2,1)S(1)} collective-permute-done((bf16[128,128]{1,0:T(8,128)(2,1)S(1)}, bf16[128,128]{1,0:T(8,128)(2,1)S(1)}, u32[]{:S(2)}, u32[]{:S(2)}) %collective-permute-start.5) | collective-permute-done | bytes 32800 | tf_op jit(solution)/shard_map/ppermute | solution.py:375
  56.8 0.0 collective-permute-done.6.received
  56.8 0.0 copy-done
  56.8 1.1 %shard_map.230 = (bf16[512,128]{1,0:T(8,128)(2,1)}, f32[904,128]{1,0:T(8,128)}) custom-call(f32[512,128]{1,0:T(8,128)S(1)} %get-tuple-element.85.local_grad, bf16[128,128]{1,0:T(8,128)(2,1)S(1)} %slice.27.near, bf16[256,128]{1,0:T(8,128)(2,1)S(1)} %get-tuple-element.88.turned, bf16[128,128]{1,0:T(8,128)(2,1)S(1)} %collective-permute-done.5.downward, ...), custom_call_target="tpu_custom_call" | custom-call | flops 1000000 | bytes 1000000 | tf_op jit(solution)/shard_map/pallas_call | solution.py:267
  (9 shorter events, 0.2 us)
Async XLA Ops:
  1.9 6.3 %collective-permute-start.2 = (bf16[128,128]{1,0:T(8,128)(2,1)S(1)}, bf16[128,128]{1,0:T(8,128)(2,1)S(1)}, u32[]{:S(2)}, u32[]{:S(2)}) collective-permute-start(bf16[128,128]{1,0:T(8,128)(2,1)S(1)} %get-tuple-element.55), channel_id=1, source_target_pairs={{0,4},{4,0},{8,12},{12,8},{16,20},{20,16},{24,28},{28,24},{32,36},... | collective-permute-start | bytes 98312 | tf_op jit(solution)/shard_map/ppermute | solution.py:339
  5.1 3.3 %collective-permute-start.3 = (bf16[128,128]{1,0:T(8,128)(2,1)S(1)}, bf16[128,128]{1,0:T(8,128)(2,1)S(1)}, u32[]{:S(2)}, u32[]{:S(2)}) collective-permute-start(bf16[128,128]{1,0:T(8,128)(2,1)S(1)} %get-tuple-element.56), channel_id=1, source_target_pairs={{4,8},{12,16},{20,24},{28,32},{36,40},{44,48},{52,56},{60,64},{68,... | collective-permute-start | bytes 98312 | tf_op jit(solution)/shard_map/ppermute | solution.py:338
  12.7 7.8 %collective-permute-start.4 = (bf16[1280,128]{1,0:T(8,128)(2,1)S(1)}, bf16[1280,128]{1,0:T(8,128)(2,1)S(1)}, u32[]{:S(2)}, u32[]{:S(2)}) collective-permute-start(bf16[1280,128]{1,0:T(8,128)(2,1)S(1)} %get-tuple-element.86), channel_id=1, source_target_pairs={{0,4},{4,0},{1,5},{5,1},{2,6},{6,2},{3,7},{7,3},{8,12},{12,8},{9,1... | collective-permute-start | bytes 983048 | tf_op jit(solution)/shard_map/ppermute | solution.py:352
  55.2 1.6 %collective-permute-start.6 = (bf16[1024,128]{1,0:T(8,128)(2,1)S(1)}, bf16[1024,128]{1,0:T(8,128)(2,1)S(1)}, u32[]{:S(2)}, u32[]{:S(2)}) collective-permute-start(bf16[1024,128]{1,0:T(8,128)(2,1)S(1)} %get-tuple-element.89.result), channel_id=1, source_target_pairs={{0,4},{4,0},{1,5},{5,1},{2,6},{6,2},{3,7},{7,3},{8,12},{12,8},{9,1... | collective-permute-start | bytes 786440 | tf_op jit(solution)/shard_map/ppermute | solution.py:374
  55.2 1.6 %collective-permute-start.5 = (bf16[128,128]{1,0:T(8,128)(2,1)S(1)}, bf16[128,128]{1,0:T(8,128)(2,1)S(1)}, u32[]{:S(2)}, u32[]{:S(2)}) collective-permute-start(bf16[128,128]{1,0:T(8,128)(2,1)S(1)} %slice.25), channel_id=1, source_target_pairs={{0,4},{4,0},{1,5},{5,1},{2,6},{6,2},{3,7},{7,3},{8,12},{12,8},{9,1... | collective-permute-start | bytes 98312 | tf_op jit(solution)/shard_map/ppermute | solution.py:375
  55.7 1.1 %copy-start = (s32[1,1,2,128]{3,2,1,0:T(2,128)S(1)}, s32[1,1,2,128]{3,2,1,0:T(2,128)}, u32[]{:S(2)}) copy-start(s32[1,1,2,128]{3,2,1,0:T(2,128)} %param.27) | copy-start | bytes 3076

commit v7 on v6

--- a/solution.py
+++ b/solution.py
@@ -35,19 +35,21 @@
 
 
 def as_bf16(mask):
-    return jnp.where(mask, 1.0, 0.0).astype(BF16)
+    return jnp.where(mask, jnp.ones((), BF16), jnp.zeros((), BF16))
 
 
 def pick_rows(row, count):
-    column = jnp.transpose(jnp.broadcast_to(row, (128, 128)))
-    lanes = lax.broadcasted_iota(jnp.int32, (128, 128), 1)
-    tiles = [as_bf16(column == lanes + 128 * j) for j in range(count // 128)]
+    column = jnp.transpose(jnp.broadcast_to(row, (128, 128))).astype(jnp.int16)
+    lanes = lax.broadcasted_iota(jnp.int16, (128, 128), 1)
+    tiles = [as_bf16(column - jnp.int16(128 * j) == lanes) for j in range(count // 128)]
     return jnp.concatenate(tiles, axis=1)
 
 
 def place_rows(row, count):
-    lines = lax.broadcasted_iota(jnp.int32, (count, 128), 0)
-    return as_bf16(lines == row)
+    lines = lax.broadcasted_iota(jnp.int16, (128, 128), 0)
+    wide = jnp.broadcast_to(row, (128, 128)).astype(jnp.int16)
+    tiles = [as_bf16(wide - jnp.int16(128 * j) == lines) for j in range(count // 128)]
+    return jnp.concatenate(tiles, axis=0)
 
 
 def split(value):
@@ -60,18 +62,22 @@
     return value[:, :128] + value[:, 128:]
 
 
-def pack_kernel(nodes_in, lists_in, near, far, nodes, lists, arrive):
+def pack_kernel(*refs):
+    sources, (near, far), landed, (lists, arrive) = refs[:4], refs[4:6], refs[6:9], refs[9:]
     loads = [
-        pltpu.make_async_copy(nodes_in, nodes, arrive.at[0]),
-        pltpu.make_async_copy(lists_in, lists, arrive.at[1]),
+        pltpu.make_async_copy(a, b, arrive.at[k])
+        for k, (a, b) in enumerate(zip(sources, (lists, *landed)))
     ]
     for load in loads:
         load.start()
-    for load in loads[::-1]:
+    nodes = landed[0]
+    for load in loads[:2]:
         load.wait()
     core = lax.axis_index("c")
     near[...] = dot(pick_rows(lists[pl.ds(1 - core, 1), :], 512), nodes[...]).astype(BF16)
     far[...] = dot(pick_rows(lists[pl.ds(core, 1), :], 512), nodes[...]).astype(BF16)
+    for load in loads[2:]:
+        load.wait()
 
 
 def norm_forward(second):
@@ -99,18 +105,16 @@
     return jnp.sum(value, axis=0, keepdims=True)
 
 
-def prepare_kernel(*refs):
+def prepare_kernel(nodes, senders, receivers, count, *refs):
     sources, landed, (receiver, partial, live, pick_send, pick_recv, place_recv, place_send), (arrive,) = (
-        refs[:19], refs[19:38], refs[38:45], refs[45:],
+        refs[:15], refs[15:30], refs[30:37], refs[37:],
     )
     loads = [pltpu.make_async_copy(a, b, arrive.at[k]) for k, (a, b) in enumerate(zip(sources, landed))]
     for load in loads:
         load.start()
-    count, senders, receivers, nodes, edges, ew1, eb1 = landed[:7]
-    for load in loads[:3]:
-        load.wait()
+    edges, ew1, eb1 = landed[:3]
     line = lax.broadcasted_iota(jnp.int32, (512, 128), 0)
-    live[...] = jnp.where(line < count[0:1, :] * 128, 1.0, 0.0).astype(F32)
+    live[...] = jnp.where(line < count[0:1, 0:1] * 128, 1.0, 0.0).astype(F32)
     for b in range(4):
         rows = pl.ds(b * 128, 128)
         send_row, recv_row = senders[pl.ds(b, 1), :], receivers[pl.ds(b, 1), :]
@@ -118,7 +122,7 @@
         pick_recv[rows, :] = pick_rows(recv_row, 512)
         place_recv[:, rows] = place_rows(recv_row, 512)
         place_send[:, rows] = place_rows(send_row, 768)
-    for load in loads[3:]:
+    for load in loads:
         load.wait()
     low = dot(pick_recv[...], nodes[...]).astype(BF16)
     receiver[...] = low
@@ -129,9 +133,9 @@
     return jnp.concatenate([weight[0:128, :], weight[256:384, :]], axis=0)
 
 
-def main_kernel(near, far, *refs):
+def main_kernel(near, far, nodes, *refs):
     (
-        (_, _, _, nodes, edges, ew1, _, ew2, eb2, egain, eshift, nw1, nb1, nw2, nb2, ngain, nshift, node_cot, edge_cot),
+        (edges, ew1, _, ew2, eb2, egain, eshift, nw1, nb1, nw2, nb2, ngain, nshift, node_cot, edge_cot),
         (receiver, partial, live, pick_send, pick_recv, place_recv, place_send),
         (node_out, edge_out, grad_edge, local_grad, keep, send),
         left,
@@ -139,7 +143,7 @@
             table, messages, hidden, slope, normed, inverse, spread, dxs, dxr, sender, first_low, second_low,
             node_inputs, node_hidden, node_first, node_second, leave,
         ),
-    ) = refs[:19], refs[19:26], refs[26:32], refs[32:35], refs[35:]
+    ) = refs[:15], refs[15:22], refs[22:28], refs[28:31], refs[31:]
     stores = [
         pltpu.make_async_copy(a, b, leave.at[k])
         for k, (a, b) in enumerate(zip(left, (edge_out, node_out, grad_edge)))
@@ -283,18 +287,18 @@
     return jax.ShapeDtypeStruct((rows, width), kind)
 
 
-def prepare(sources):
+def prepare(early, sources):
     outs = tuple(jax.ShapeDtypeStruct(source.shape, source.dtype) for source in sources) + (
         shape(512, 128, BF16), shape(512, 128, F32), shape(512, 128, F32), shape(512, 768, BF16),
         shape(512, 512, BF16), shape(512, 512, BF16), shape(768, 512, BF16),
     )
     return call(
-        prepare_kernel, outs, (sources[0], *(in_hbm(source) for source in sources[1:])), [VMEM] + [HBM] * 18,
-        scratch=[pltpu.SemaphoreType.DMA((19,))], flops=400000000, vmem=16 << 20,
-    )
-
-
-def compute(near, far, prepared):
+        prepare_kernel, outs, (*early, *(in_hbm(source) for source in sources)),
+        [VMEM] * 4 + [HBM] * 15, scratch=[pltpu.SemaphoreType.DMA((15,))], flops=400000000, vmem=16 << 20,
+    )
+
+
+def compute(near, far, nodes, prepared):
     outs = (
         shape(512, 128, BF16), shape(512, 128, BF16), shape(512, 128, BF16), shape(512, 128, F32),
         shape(ROWS, 128, F32), shape(ROWS + 256, 128, BF16),
@@ -310,7 +314,7 @@
         )
     ] + [pltpu.SemaphoreType.DMA((3,))]
     return call(
-        main_kernel, outs, (near, far, *prepared), [VMEM] * 28,
+        main_kernel, outs, (near, far, nodes, *prepared), [VMEM] * 25,
         (HBM,) * 3 + (VMEM,) * 3, scratch, 2000000000, 24 << 20,
     )
 
@@ -328,24 +332,29 @@
     down = [(j, j - 2) for j in range(2, 64, 2)]
     up = [(j - 2, j) for j in range(2, 64, 2)]
 
-    near, far = call(
-        pack_kernel, (shape(128, 128, BF16),) * 2, (in_hbm(own_nodes), in_hbm(lists)), [HBM] * 2,
-        scratch=[
-            pltpu.VMEM((512, 128), BF16), pltpu.VMEM((2, 128), jnp.int32), pltpu.SemaphoreType.DMA((2,))
-        ],
+    outs = (
+        shape(128, 128, BF16), shape(128, 128, BF16), shape(512, 128, BF16), shape(4, 128, jnp.int32),
+        shape(4, 128, jnp.int32),
+    )
+    near, far, *early = call(
+        pack_kernel, outs,
+        (in_hbm(lists), in_hbm(own_nodes), in_hbm(senders[0]), in_hbm(receivers[0])), [HBM] * 4,
+        scratch=[pltpu.VMEM((2, 128), jnp.int32), pltpu.SemaphoreType.DMA((4,))],
         vmem=SMALL,
     )
+    block_count, far = lax.optimization_barrier((block_count, far))
+    early.append(jnp.pad(block_count, ((0, 7), (0, 127))))
     far = lax.ppermute(far, DOM, far_pairs)
     near = lax.ppermute(near, DOM, near_pairs)
 
     sources = (
-        jnp.broadcast_to(block_count, (8, 128)), senders[0], receivers[0], own_nodes, edges[0].reshape(512, 128),
+        edges[0].reshape(512, 128),
         edge_w1, line(edge_b1), edge_w2, line(edge_b2), line(edge_gain), line(edge_shift),
         node_w1, line(node_b1), node_w2, line(node_b2), line(node_gain), line(node_shift),
         node_cot[0], edge_cot[0].reshape(512, 128),
     )
-    prepared = prepare(sources)
-    node_out, edge_out, grad_edge, local_grad, keep, send = compute(near, far, prepared)
+    prepared = prepare(early, sources)
+    node_out, edge_out, grad_edge, local_grad, keep, send = compute(near, far, early[0], prepared)
 
     scale = 1.0 / math.sqrt(lax.axis_size(DOM) * lax.axis_size("x") * 512)
     planes, columns = lax.axis_size(PLANE), lax.axis_size(COLUMN)

time: 58.1 us -> 57.4 us (0.988)
    ppermute x1, starting transfers between devices: 6.55 us -> 0.09 us  [layer(): arrived = lax.ppermute(send, 'c', [(0, 1), (1, 0)])]
    ppermute x1, starting transfers between devices: 0.01 us -> 3.1 us  [layer(): far = lax.ppermute(far, DOM, far_pairs)]
    ppermute x1, starting transfers between devices: 3.29 us -> 6.23 us  [layer(): near = lax.ppermute(near, DOM, near_pairs)]
  transfers between devices with their start and end apart: 5 -> 5, of which waited for: 3 -> 2; matrix products, arithmetic and copies ran while one was open for 0% -> 0% of each run, Pallas kernels for 4% -> 4%
where the time goes in v7:
time: 57.4 us; the launch traced here: 57.2 us
  blocking collectives  34.4 us (60%)
  starting transfers between devices  9.91 us (17%)
  Pallas kernels  8.58 us (15%)
  waiting for transfers between devices  2.68 us (5%)
  between operations  1.37 us (2%)
    all_to_all x1, blocking collectives, reduce(): tiles = lax.all_to_all(copies, COLUMN, 0, 0, tiled=True)  12.3 us
    all_to_all x1, blocking collectives, reduce(): lax.all_to_all(pair.reshape(planes, -1, 128), PLANE, 0, 0, tiled=True)  11.6 us
    all_to_all x1, blocking collectives, reduce(): tiles = lax.all_to_all(copies, PLANE, 0, 0, tiled=True)  10.4 us
    pallas_call x4, Pallas kernels, call(): pl.pallas_call(body, out_shape=out_shape, in_specs=in_specs or [VMEM] * l...  8.58 us
    ppermute x1, starting transfers between devices, layer(): near = lax.ppermute(near, DOM, near_pairs)  6.23 us
    ppermute x1, starting transfers between devices, layer(): far = lax.ppermute(far, DOM, far_pairs)  3.1 us
    ppermute x1, waiting for transfers between devices, layer(): arrived = lax.ppermute(send, 'c', [(0, 1), (1, 0)])  1.61 us
  transfers between devices with their start and end apart: 5, of which 2 were waited for; matrix products, arithmetic and copies ran while one was open for 0% of the time, Pallas kernels for 4%

profile of v7, /device:TPU:1, one launch (start us, length us, event | category | flops | bytes accessed | tf_op | source)
XLA Modules:
  0.0 57.2 jit_solution(15958871711766707697)
XLA Ops:
  0.6 1.2 %shard_map.227 = (bf16[128,128]{1,0:T(8,128)(2,1)S(1)}, bf16[128,128]{1,0:T(8,128)(2,1)S(1)}, bf16[512,128]{1,0:T(8,128)(2,1)S(1)}, s32[4,128]{1,0:T(4,128)S(1)}, s32[4,128]{1,0:T(4,128)S(1)}) custom-call(s32[2,128]{1,0:T(2,128)} %bitcast.23, bf16[512,128]{1,0:T(8,128)(2,1)} %bitcast.28, s32[4,128]{1,0:T(4,128)} %bitcast.29, s32[4,128]{1,0:T(4,128)} %bitcast.30), custom_call_target="tpu_custom_call" | custom-call | flops 1000000 | bytes 1000000 | tf_op jit(solution)/shard_map/pallas_call | solution.py:271
  1.9 3.1 %collective-permute-start.3 = (bf16[128,128]{1,0:T(8,128)(2,1)S(1)}, bf16[128,128]{1,0:T(8,128)(2,1)S(1)}, u32[]{:S(2)}, u32[]{:S(2)}) collective-permute-start(bf16[128,128]{1,0:T(8,128)(2,1)S(1)} %get-tuple-element.58), channel_id=1, source_target_pairs={{4,8},{12,16},{20,24},{28,32},{36,40},{44,48},{52,56},{60,64},{68,... | collective-permute-start | bytes 98312 | tf_op jit(solution)/shard_map/ppermute | solution.py:347
  5.0 6.2 %collective-permute-start.2 = (bf16[128,128]{1,0:T(8,128)(2,1)S(1)}, bf16[128,128]{1,0:T(8,128)(2,1)S(1)}, u32[]{:S(2)}, u32[]{:S(2)}) collective-permute-start(bf16[128,128]{1,0:T(8,128)(2,1)S(1)} %get-tuple-element.56), channel_id=1, source_target_pairs={{0,4},{4,0},{8,12},{12,8},{16,20},{20,16},{24,28},{28,24},{32,36},... | collective-permute-start | bytes 98312 | tf_op jit(solution)/shard_map/ppermute | solution.py:348
  11.9 2.1 %shard_map.228 = (bf16[512,128]{1,0:T(8,128)(2,1)S(1)}, bf16[384,128]{1,0:T(8,128)(2,1)S(1)}, f32[1,128]{1,0:T(1,128)S(1)}, bf16[128,128]{1,0:T(8,128)(2,1)S(1)}...) custom-call(bf16[512,128]{1,0:T(8,128)(2,1)S(1)} %get-tuple-element., ...), custom_call_target="tpu_custom_call" | custom-call | flops 400000000 | bytes 1000000 | tf_op jit(solution)/shard_map/pallas_call | solution.py:271
  14.0 0.0 collective-permute-done.3.far
  14.0 0.0 collective-permute-done.2.near
  14.0 4.2 %shard_map.229 = (bf16[512,128]{1,0:T(8,128)(2,1)}, bf16[512,128]{1,0:T(8,128)(2,1)}, bf16[512,128]{1,0:T(8,128)(2,1)}, f32[512,128]{1,0:T(8,128)S(1)}, f32[1024...) custom-call(bf16[128,128]{1,0:T(8,128)(2,1)S(1)} %collective-permute-done.2.near, ...), custom_call_target="tpu_custom_call" | custom-call | flops 2000000000 | bytes 1000000 | tf_op jit(solution)/shard_map/pallas_call | solution.py:271
  18.2 0.1 collective-permute-start.4
  18.3 1.6 %collective-permute-done.4 = bf16[1280,128]{1,0:T(8,128)(2,1)S(1)} collective-permute-done((bf16[1280,128]{1,0:T(8,128)(2,1)S(1)}, bf16[1280,128]{1,0:T(8,128)(2,1)S(1)}, u32[]{:S(2)}, u32[]{:S(2)}) %collective-permute-start.4) | collective-permute-done | bytes 327712 | tf_op jit(solution)/shard_map/ppermute | solution.py:361
  19.9 0.1 add_convert_fusion
  19.9 34.6 %conditional.1 = (bf16[1024,128]{1,0:T(8,128)(2,1)S(1)}, bf16[256,128]{1,0:T(8,128)(2,1)S(1)}) conditional(s32[]{:T(128)} %convert_element_type.20, bf16[1024,128]{1,0:T(8,128)(2,1)S(1)} %add_convert_fusion, (bf16[1280,128]{1,0:T(8,128)(2,1)S(1)}, bf16[1280,128]{1,0:T(8,128)(2,1)S(1)}, bf16[1024,128]{1,0:T(8,128)(2,1)S(1)}) %tuple.18), branch_computations={%region_0.3_spmd, %region_3.4_spmd} | conditional | flops 262144 | bytes 2359314 | solution.py:380
  20.0 11.6 %all_to_all.12 = bf16[16,64,128]{2,1,0:T(8,128)(2,1)S(1)} all-to-all(bf16[16,64,128]{2,1,0:T(8,128)(2,1)S(1)} %bitcast.25), channel_id=1, replica_groups=mesh['y'=4,'z'=8,'c'=2,'x'=4] {'y','x'}, dimensions={0} | all-to-all | bytes 524288 | tf_op jit(solution)/shard_map/cond/branch_0_fun/all_to_all | solution.py:370
  31.7 12.3 %all_to_all.13 = bf16[8,64,128]{2,1,0:T(8,128)(2,1)S(1)} all-to-all(bf16[8,64,128]{2,1,0:T(8,128)(2,1)S(1)} %broadcast_in_dim.8), channel_id=1, replica_groups=mesh['y'=4,'z'=8,'c'=2,'x'=4] {'z'}, dimensions={0} | all-to-all | bytes 262144 | tf_op jit(solution)/shard_map/cond/branch_0_fun/all_to_all | solution.py:373
  44.1 10.4 %all_to_all.14 = bf16[16,64,128]{2,1,0:T(8,128)(2,1)S(1)} all-to-all(bf16[16,64,128]{2,1,0:T(8,128)(2,1)S(1)} %broadcast_in_dim.9), channel_id=1, replica_groups=mesh['y'=4,'z'=8,'c'=2,'x'=4] {'y','x'}, dimensions={0} | all-to-all | bytes 524288 | tf_op jit(solution)/shard_map/cond/branch_0_fun/all_to_all | solution.py:376
  54.5 0.0 collective-permute-start.6
  54.5 0.5 collective-permute-start.5
  55.0 0.0 copy-start
  55.0 1.1 %collective-permute-done.5.downward = bf16[128,128]{1,0:T(8,128)(2,1)S(1)} collective-permute-done((bf16[128,128]{1,0:T(8,128)(2,1)S(1)}, bf16[128,128]{1,0:T(8,128)(2,1)S(1)}, u32[]{:S(2)}, u32[]{:S(2)}) %collective-permute-start.5) | collective-permute-done | bytes 32800 | tf_op jit(solution)/shard_map/ppermute | solution.py:384
  56.1 0.0 collective-permute-done.6.received
  56.1 0.0 copy-done
  56.1 1.1 %shard_map.230 = (bf16[512,128]{1,0:T(8,128)(2,1)}, f32[904,128]{1,0:T(8,128)}) custom-call(f32[512,128]{1,0:T(8,128)S(1)} %get-tuple-element.87.local_grad, bf16[128,128]{1,0:T(8,128)(2,1)S(1)} %slice.27.near, bf16[256,128]{1,0:T(8,128)(2,1)S(1)} %get-tuple-element.90.turned, bf16[128,128]{1,0:T(8,128)(2,1)S(1)} %collective-permute-done.5.downward, ...), custom_call_target="tpu_custom_call" | custom-call | flops 1000000 | bytes 1000000 | tf_op jit(solution)/shard_map/pallas_call | solution.py:271
  (9 shorter events, 0.2 us)
Async XLA Ops:
  1.9 12.1 %collective-permute-start.3 = (bf16[128,128]{1,0:T(8,128)(2,1)S(1)}, bf16[128,128]{1,0:T(8,128)(2,1)S(1)}, u32[]{:S(2)}, u32[]{:S(2)}) collective-permute-start(bf16[128,128]{1,0:T(8,128)(2,1)S(1)} %get-tuple-element.58), channel_id=1, source_target_pairs={{4,8},{12,16},{20,24},{28,32},{36,40},{44,48},{52,56},{60,64},{68,... | collective-permute-start | bytes 98312 | tf_op jit(solution)/shard_map/ppermute | solution.py:347
  5.0 9.0 %collective-permute-start.2 = (bf16[128,128]{1,0:T(8,128)(2,1)S(1)}, bf16[128,128]{1,0:T(8,128)(2,1)S(1)}, u32[]{:S(2)}, u32[]{:S(2)}) collective-permute-start(bf16[128,128]{1,0:T(8,128)(2,1)S(1)} %get-tuple-element.56), channel_id=1, source_target_pairs={{0,4},{4,0},{8,12},{12,8},{16,20},{20,16},{24,28},{28,24},{32,36},... | collective-permute-start | bytes 98312 | tf_op jit(solution)/shard_map/ppermute | solution.py:348
  18.2 1.7 %collective-permute-start.4 = (bf16[1280,128]{1,0:T(8,128)(2,1)S(1)}, bf16[1280,128]{1,0:T(8,128)(2,1)S(1)}, u32[]{:S(2)}, u32[]{:S(2)}) collective-permute-start(bf16[1280,128]{1,0:T(8,128)(2,1)S(1)} %get-tuple-element.88), channel_id=1, source_target_pairs={{0,4},{4,0},{1,5},{5,1},{2,6},{6,2},{3,7},{7,3},{8,12},{12,8},{9,1... | collective-permute-start | bytes 983048 | tf_op jit(solution)/shard_map/ppermute | solution.py:361
  54.5 1.6 %collective-permute-start.6 = (bf16[1024,128]{1,0:T(8,128)(2,1)S(1)}, bf16[1024,128]{1,0:T(8,128)(2,1)S(1)}, u32[]{:S(2)}, u32[]{:S(2)}) collective-permute-start(bf16[1024,128]{1,0:T(8,128)(2,1)S(1)} %get-tuple-element.91.result), channel_id=1, source_target_pairs={{0,4},{4,0},{1,5},{5,1},{2,6},{6,2},{3,7},{7,3},{8,12},{12,8},{9,1... | collective-permute-start | bytes 786440 | tf_op jit(solution)/shard_map/ppermute | solution.py:383
  54.5 1.6 %collective-permute-start.5 = (bf16[128,128]{1,0:T(8,128)(2,1)S(1)}, bf16[128,128]{1,0:T(8,128)(2,1)S(1)}, u32[]{:S(2)}, u32[]{:S(2)}) collective-permute-start(bf16[128,128]{1,0:T(8,128)(2,1)S(1)} %slice.25), channel_id=1, source_target_pairs={{0,4},{4,0},{1,5},{5,1},{2,6},{6,2},{3,7},{7,3},{8,12},{12,8},{9,1... | collective-permute-start | bytes 98312 | tf_op jit(solution)/shard_map/ppermute | solution.py:384
  55.0 1.1 %copy-start = (s32[1,1,2,128]{3,2,1,0:T(2,128)S(1)}, s32[1,1,2,128]{3,2,1,0:T(2,128)}, u32[]{:S(2)}) copy-start(s32[1,1,2,128]{3,2,1,0:T(2,128)} %param.27) | copy-start | bytes 3076

commit v8 on v7

--- a/solution.py
+++ b/solution.py
@@ -247,7 +247,7 @@
 
 
 def finish_kernel(
-    local_grad, near, turned, downward, result, received, lists, grad_node, weight_grads, node_left, weight_left, leave
+    local_grad, near, result, received, lists, grad_node, weight_grads, node_left, weight_left, leave
 ):
     core = lax.axis_index("c")
     is_first = core == 0
@@ -258,7 +258,8 @@
     whole = jnp.where(is_first, received[0:LIVE_ROWS, :].astype(F32), result[0:LIVE_ROWS, :].astype(F32))
     weight_left[...] = whole
     stores[0].start()
-    far = jnp.where(is_first, turned[0:128, :].astype(F32), downward[...].astype(F32)).astype(BF16)
+    upward, downward = result[ROWS + 128 :, :], received[ROWS : ROWS + 128, :]
+    far = jnp.where(is_first, upward.astype(F32), downward.astype(F32)).astype(BF16)
     added = dot(place_rows(lists[pl.ds(1 - core, 1), :], 512), near[...])
     added += dot(place_rows(lists[pl.ds(core, 1), :], 512), far)
     node_left[...] = (local_grad[...] + added).astype(BF16)
@@ -328,7 +329,7 @@
     lists = send_rows[0, 0]
     line = lambda vector: vector.reshape(1, 128)
     near_pairs = [(j, j ^ 1) for j in range(64)]
-    far_pairs = [(j, (j + 1) % 64) for j in range(1, 64, 2)] + [((j + 1) % 64, j) for j in range(1, 64, 2)]
+    far_pairs = [(0, 0), (63, 63)] + [(j, j + 1) for j in range(1, 63, 2)] + [(j + 1, j) for j in range(1, 63, 2)]
     down = [(j, j - 2) for j in range(2, 64, 2)]
     up = [(j - 2, j) for j in range(2, 64, 2)]
 
@@ -364,27 +365,26 @@
 
     def carry(pair, mine, other):
         upward, downward = lax.ppermute(other, DOM, up), lax.ppermute(mine, DOM, down)
-        return pair, jnp.concatenate([upward, downward], axis=0)
+        return jnp.concatenate([pair, downward, upward], axis=0)
 
     def reduce(pair, mine, other):
         tiles = lax.all_to_all(pair.reshape(planes, -1, 128), PLANE, 0, 0, tiled=True)
-        piece = jnp.sum(tiles.astype(F32), axis=0).astype(BF16)
+        piece = (jnp.sum(tiles.astype(F32), axis=0) * 0.0625).astype(BF16)
         copies = jnp.broadcast_to(piece, (columns, *piece.shape))
         tiles = lax.all_to_all(copies, COLUMN, 0, 0, tiled=True)
-        piece = (jnp.sum(tiles.astype(F32), axis=0) * scale).astype(BF16)
+        piece = (jnp.sum(tiles.astype(F32), axis=0) * (16.0 * scale)).astype(BF16)
         copies = jnp.broadcast_to(piece, (planes, *piece.shape))
         tiles = lax.all_to_all(copies, PLANE, 0, 0, tiled=True)
         whole = tiles.reshape(ROWS, 128)
-        return whole, whole[0:256]
-
-    result, turned = lax.cond(
+        return jnp.concatenate([whole, whole[0:256]], axis=0)
+
+    result = lax.cond(
         lax.axis_index("c") == 0, carry, reduce, pair, send[ROWS + 128 :], arrived[ROWS + 128 :]
     )
     received = lax.ppermute(result, "c", [(0, 1), (1, 0)])
-    downward = lax.ppermute(turned[128:], "c", [(0, 1), (1, 0)])
     grad_node, weight_grads = call(
         finish_kernel, (shape(512, 128, BF16), shape(LIVE_ROWS, 128, F32)),
-        (local_grad, near_back, turned, downward, result, received, lists), [VMEM] * 7, (HBM,) * 2,
+        (local_grad, near_back, result, received, lists), [VMEM] * 5, (HBM,) * 2,
         [
             pltpu.VMEM((512, 128), BF16), pltpu.VMEM((LIVE_ROWS, 128), F32), pltpu.SemaphoreType.DMA((2,))
         ],

time: 57.4 us -> 59.2 us (1.031)
  blocking collectives: 34.4 us -> 40.1 us
  starting transfers between devices: 9.91 us -> 5.69 us
    ppermute x1, starting transfers between devices: 6.23 us -> 0.09 us  [layer(): near = lax.ppermute(near, DOM, near_pairs)]
    all_to_all x1, blocking collectives: 11.6 us -> 17.7 us  [reduce(): lax.all_to_all(pair.reshape(planes, -1, 128), PLANE, 0, 0, tiled=True)]
    ppermute x1, starting transfers between devices: 3.1 us -> 4.92 us  [layer(): far = lax.ppermute(far, DOM, far_pairs)]
    ppermute x1, waiting for transfers between devices: 0.01 us -> 1.59 us  [layer(): received = lax.ppermute(result, 'c', [(0, 1), (1, 0)])]
    ppermute x1 -> x0, waiting for transfers between devices: 1.06 us -> none  [layer(): downward = lax.ppermute(turned[128:], 'c', [(0, 1), (1, 0)])]
  transfers between devices with their start and end apart: 5 -> 4, of which waited for: 2 -> 2; matrix products, arithmetic and copies ran while one was open for 0% -> 0% of each run, Pallas kernels for 4% -> 4%
where the time goes in v8:
time: 59.2 us; the launch traced here: 58.9 us
  blocking collectives  40.1 us (68%)
  Pallas kernels  8.58 us (14%)
  starting transfers between devices  5.69 us (10%)
  waiting for transfers between devices  2.85 us (5%)
  between operations  1.38 us (2%)
    all_to_all x1, blocking collectives, reduce(): lax.all_to_all(pair.reshape(planes, -1, 128), PLANE, 0, 0, tiled=True)  17.7 us
    all_to_all x1, blocking collectives, reduce(): tiles = lax.all_to_all(copies, COLUMN, 0, 0, tiled=True)  11.9 us
    all_to_all x1, blocking collectives, reduce(): tiles = lax.all_to_all(copies, PLANE, 0, 0, tiled=True)  10.5 us
    pallas_call x4, Pallas kernels, call(): pl.pallas_call(body, out_shape=out_shape, in_specs=in_specs or [VMEM] * l...  8.58 us
    ppermute x1, starting transfers between devices, layer(): far = lax.ppermute(far, DOM, far_pairs)  4.92 us
    ppermute x1, waiting for transfers between devices, layer(): received = lax.ppermute(result, 'c', [(0, 1), (1, 0)])  1.59 us
    ppermute x1, waiting for transfers between devices, layer(): arrived = lax.ppermute(send, 'c', [(0, 1), (1, 0)])  1.26 us
  transfers between devices with their start and end apart: 4, of which 2 were waited for; matrix products, arithmetic and copies ran while one was open for 0% of the time, Pallas kernels for 4%

profile of v8, /device:TPU:1, one launch (start us, length us, event | category | flops | bytes accessed | tf_op | source)
XLA Modules:
  0.0 58.9 jit_solution(16523560547240528348)
XLA Ops:
  0.6 1.2 %shard_map.227 = (bf16[128,128]{1,0:T(8,128)(2,1)S(1)}, bf16[128,128]{1,0:T(8,128)(2,1)S(1)}, bf16[512,128]{1,0:T(8,128)(2,1)S(1)}, s32[4,128]{1,0:T(4,128)S(1)}, s32[4,128]{1,0:T(4,128)S(1)}) custom-call(s32[2,128]{1,0:T(2,128)} %bitcast.23, bf16[512,128]{1,0:T(8,128)(2,1)} %bitcast.28, s32[4,128]{1,0:T(4,128)} %bitcast.29, s32[4,128]{1,0:T(4,128)} %bitcast.30), custom_call_target="tpu_custom_call" | custom-call | flops 1000000 | bytes 1000000 | tf_op jit(solution)/shard_map/pallas_call | solution.py:272
  1.9 4.9 %collective-permute-start.3 = (bf16[128,128]{1,0:T(8,128)(2,1)S(1)}, bf16[128,128]{1,0:T(8,128)(2,1)S(1)}, u32[]{:S(2)}, u32[]{:S(2)}) collective-permute-start(bf16[128,128]{1,0:T(8,128)(2,1)S(1)} %get-tuple-element.59), channel_id=1, source_target_pairs={{0,0},{252,252},{4,8},{12,16},{20,24},{28,32},{36,40},{44,48},{52,... | collective-permute-start | bytes 98312 | tf_op jit(solution)/shard_map/ppermute | solution.py:348
  6.8 0.1 collective-permute-start.2
  7.6 2.1 %shard_map.228 = (bf16[512,128]{1,0:T(8,128)(2,1)S(1)}, bf16[384,128]{1,0:T(8,128)(2,1)S(1)}, f32[1,128]{1,0:T(1,128)S(1)}, bf16[128,128]{1,0:T(8,128)(2,1)S(1)}...) custom-call(bf16[512,128]{1,0:T(8,128)(2,1)S(1)} %get-tuple-element., ...), custom_call_target="tpu_custom_call" | custom-call | flops 400000000 | bytes 1000000 | tf_op jit(solution)/shard_map/pallas_call | solution.py:272
  9.7 0.0 collective-permute-done.3.far
  9.7 0.0 collective-permute-done.2.near
  9.7 4.2 %shard_map.229 = (bf16[512,128]{1,0:T(8,128)(2,1)}, bf16[512,128]{1,0:T(8,128)(2,1)}, bf16[512,128]{1,0:T(8,128)(2,1)}, f32[512,128]{1,0:T(8,128)S(1)}, f32[1024...) custom-call(bf16[128,128]{1,0:T(8,128)(2,1)S(1)} %collective-permute-done.2.near, ...), custom_call_target="tpu_custom_call" | custom-call | flops 2000000000 | bytes 1000000 | tf_op jit(solution)/shard_map/pallas_call | solution.py:272
  13.9 0.6 %collective-permute-start.4 = (bf16[1280,128]{1,0:T(8,128)(2,1)S(1)}, bf16[1280,128]{1,0:T(8,128)(2,1)S(1)}, u32[]{:S(2)}, u32[]{:S(2)}) collective-permute-start(bf16[1280,128]{1,0:T(8,128)(2,1)S(1)} %get-tuple-element.89), channel_id=1, source_target_pairs={{0,4},{4,0},{1,5},{5,1},{2,6},{6,2},{3,7},{7,3},{8,12},{12,8},{9,1... | collective-permute-start | bytes 983048 | tf_op jit(solution)/shard_map/ppermute | solution.py:362
  14.5 1.3 %collective-permute-done.4 = bf16[1280,128]{1,0:T(8,128)(2,1)S(1)} collective-permute-done((bf16[1280,128]{1,0:T(8,128)(2,1)S(1)}, bf16[1280,128]{1,0:T(8,128)(2,1)S(1)}, u32[]{:S(2)}, u32[]{:S(2)}) %collective-permute-start.4) | collective-permute-done | bytes 327712 | tf_op jit(solution)/shard_map/ppermute | solution.py:362
  15.7 0.1 add_convert_fusion
  15.8 40.3 %conditional.1 = (bf16[1280,128]{1,0:T(8,128)(2,1)S(1)}) conditional(s32[]{:T(128)} %convert_element_type.24, bf16[1024,128]{1,0:T(8,128)(2,1)S(1)} %add_convert_fusion, (bf16[1280,128]{1,0:T(8,128)(2,1)S(1)}, bf16[1280,128]{1,0:T(8,128)(2,1)S(1)}, bf16[1024,128]{1,0:T(8,128)(2,1)S(1)}) %tuple.16), branch_computations={%region_0.3_spmd, %region_3.4_spmd} | conditional | flops 1064960 | bytes 3080200 | solution.py:381
  15.8 17.7 %all_to_all.12 = bf16[16,64,128]{2,1,0:T(8,128)(2,1)S(1)} all-to-all(bf16[16,64,128]{2,1,0:T(8,128)(2,1)S(1)} %bitcast.25), channel_id=1, replica_groups=mesh['y'=4,'z'=8,'c'=2,'x'=4] {'y','x'}, dimensions={0} | all-to-all | bytes 524288 | tf_op jit(solution)/shard_map/cond/branch_0_fun/all_to_all | solution.py:371
  33.6 11.9 %all_to_all.13 = bf16[8,64,128]{2,1,0:T(8,128)(2,1)S(1)} all-to-all(bf16[8,64,128]{2,1,0:T(8,128)(2,1)S(1)} %broadcast_in_dim.8), channel_id=1, replica_groups=mesh['y'=4,'z'=8,'c'=2,'x'=4] {'z'}, dimensions={0} | all-to-all | bytes 262144 | tf_op jit(solution)/shard_map/cond/branch_0_fun/all_to_all | solution.py:374
  45.6 10.5 %all_to_all.14 = bf16[16,64,128]{2,1,0:T(8,128)(2,1)S(1)} all-to-all(bf16[16,64,128]{2,1,0:T(8,128)(2,1)S(1)} %broadcast_in_dim.9), channel_id=1, replica_groups=mesh['y'=4,'z'=8,'c'=2,'x'=4] {'y','x'}, dimensions={0} | all-to-all | bytes 524288 | tf_op jit(solution)/shard_map/cond/branch_0_fun/all_to_all | solution.py:377
  56.1 0.1 collective-permute-start.5
  56.2 0.0 copy-start
  56.2 1.6 %collective-permute-done.5.received = bf16[1280,128]{1,0:T(8,128)(2,1)S(1)} collective-permute-done((bf16[1280,128]{1,0:T(8,128)(2,1)S(1)}, bf16[1280,128]{1,0:T(8,128)(2,1)S(1)}, u32[]{:S(2)}, u32[]{:S(2)}) %collective-permute-start.5) | collective-permute-done | bytes 327712 | tf_op jit(solution)/shard_map/ppermute | solution.py:384
  57.8 0.0 copy-done
  57.8 1.1 %shard_map.230 = (bf16[512,128]{1,0:T(8,128)(2,1)}, f32[904,128]{1,0:T(8,128)}) custom-call(f32[512,128]{1,0:T(8,128)S(1)} %get-tuple-element.88.local_grad, bf16[128,128]{1,0:T(8,128)(2,1)S(1)} %slice.23.near, bf16[1280,128]{1,0:T(8,128)(2,1)S(1)} %get-tuple-element.94.result, bf16[1280,128]{1,0:T(8,128)(2,1)S(1)} %collective-permute-done.5.received, ...), custom_call_target="tpu_custom_call" | custom-call | flops 1000000 | bytes 1000000 | tf_op jit(solution)/shard_map/pallas_call | solution.py:272
  (10 shorter events, 0.2 us)
Async XLA Ops:
  1.9 7.8 %collective-permute-start.3 = (bf16[128,128]{1,0:T(8,128)(2,1)S(1)}, bf16[128,128]{1,0:T(8,128)(2,1)S(1)}, u32[]{:S(2)}, u32[]{:S(2)}) collective-permute-start(bf16[128,128]{1,0:T(8,128)(2,1)S(1)} %get-tuple-element.59), channel_id=1, source_target_pairs={{0,0},{252,252},{4,8},{12,16},{20,24},{28,32},{36,40},{44,48},{52,... | collective-permute-start | bytes 98312 | tf_op jit(solution)/shard_map/ppermute | solution.py:348
  6.8 2.9 %collective-permute-start.2 = (bf16[128,128]{1,0:T(8,128)(2,1)S(1)}, bf16[128,128]{1,0:T(8,128)(2,1)S(1)}, u32[]{:S(2)}, u32[]{:S(2)}) collective-permute-start(bf16[128,128]{1,0:T(8,128)(2,1)S(1)} %get-tuple-element.57), channel_id=1, source_target_pairs={{0,4},{4,0},{8,12},{12,8},{16,20},{20,16},{24,28},{28,24},{32,36},... | collective-permute-start | bytes 98312 | tf_op jit(solution)/shard_map/ppermute | solution.py:349
  13.9 1.8 %collective-permute-start.4 = (bf16[1280,128]{1,0:T(8,128)(2,1)S(1)}, bf16[1280,128]{1,0:T(8,128)(2,1)S(1)}, u32[]{:S(2)}, u32[]{:S(2)}) collective-permute-start(bf16[1280,128]{1,0:T(8,128)(2,1)S(1)} %get-tuple-element.89), channel_id=1, source_target_pairs={{0,4},{4,0},{1,5},{5,1},{2,6},{6,2},{3,7},{7,3},{8,12},{12,8},{9,1... | collective-permute-start | bytes 983048 | tf_op jit(solution)/shard_map/ppermute | solution.py:362
  56.1 1.7 %collective-permute-start.5 = (bf16[1280,128]{1,0:T(8,128)(2,1)S(1)}, bf16[1280,128]{1,0:T(8,128)(2,1)S(1)}, u32[]{:S(2)}, u32[]{:S(2)}) collective-permute-start(bf16[1280,128]{1,0:T(8,128)(2,1)S(1)} %get-tuple-element.94.result), channel_id=1, source_target_pairs={{0,4},{4,0},{1,5},{5,1},{2,6},{6,2},{3,7},{7,3},{8,12},{12,8},{9,1... | collective-permute-start | bytes 983048 | tf_op jit(solution)/shard_map/ppermute | solution.py:384
  56.2 1.6 %copy-start = (s32[1,1,2,128]{3,2,1,0:T(2,128)S(1)}, s32[1,1,2,128]{3,2,1,0:T(2,128)}, u32[]{:S(2)}) copy-start(s32[1,1,2,128]{3,2,1,0:T(2,128)} %param.27) | copy-start | bytes 3076

commit v9 on v7

--- a/solution.py
+++ b/solution.py
@@ -328,7 +328,10 @@
     lists = send_rows[0, 0]
     line = lambda vector: vector.reshape(1, 128)
     near_pairs = [(j, j ^ 1) for j in range(64)]
-    far_pairs = [(j, (j + 1) % 64) for j in range(1, 64, 2)] + [((j + 1) % 64, j) for j in range(1, 64, 2)]
+    beside = {0: 0, 63: 63} | {j: j + 1 for j in range(1, 63, 2)} | {j + 1: j for j in range(1, 63, 2)}
+    far_pairs = [
+        (4 * j + x, 4 * k + (x ^ 1 if j == k else x)) for j, k in beside.items() for x in range(4)
+    ]
     down = [(j, j - 2) for j in range(2, 64, 2)]
     up = [(j - 2, j) for j in range(2, 64, 2)]
 
@@ -344,7 +347,7 @@
     )
     block_count, far = lax.optimization_barrier((block_count, far))
     early.append(jnp.pad(block_count, ((0, 7), (0, 127))))
-    far = lax.ppermute(far, DOM, far_pairs)
+    far = lax.ppermute(far, (*DOM, "x"), far_pairs)
     near = lax.ppermute(near, DOM, near_pairs)
 
     sources = (
@@ -368,10 +371,10 @@
 
     def reduce(pair, mine, other):
         tiles = lax.all_to_all(pair.reshape(planes, -1, 128), PLANE, 0, 0, tiled=True)
-        piece = jnp.sum(tiles.astype(F32), axis=0).astype(BF16)
+        piece = (jnp.sum(tiles.astype(F32), axis=0) * 0.0625).astype(BF16)
         copies = jnp.broadcast_to(piece, (columns, *piece.shape))
         tiles = lax.all_to_all(copies, COLUMN, 0, 0, tiled=True)
-        piece = (jnp.sum(tiles.astype(F32), axis=0) * scale).astype(BF16)
+        piece = (jnp.sum(tiles.astype(F32), axis=0) * (16.0 * scale)).astype(BF16)
         copies = jnp.broadcast_to(piece, (planes, *piece.shape))
         tiles = lax.all_to_all(copies, PLANE, 0, 0, tiled=True)
         whole = tiles.reshape(ROWS, 128)

time: 57.4 us -> 56.9 us (level)
  starting transfers between devices: 9.91 us -> 5 us
  blocking collectives: 34.4 us -> 39.1 us
    ppermute x1, starting transfers between devices: 6.23 us -> 0.29 us  [layer(): near = lax.ppermute(near, DOM, near_pairs)]
    all_to_all x1, blocking collectives: 11.6 us -> 16.9 us  [reduce(): lax.all_to_all(pair.reshape(planes, -1, 128), PLANE, 0, 0, tiled=True)]
    ppermute x1, starting transfers between devices: 0.09 us -> 1.12 us  [layer(): arrived = lax.ppermute(send, 'c', [(0, 1), (1, 0)])]
where the time goes in v9:
time: 56.9 us; the launch traced here: 56.6 us
  blocking collectives  39.1 us (69%)
  Pallas kernels  8.58 us (15%)
  starting transfers between devices  5 us (9%)
  waiting for transfers between devices  2.33 us (4%)
  between operations  1.35 us (2%)
    all_to_all x1, blocking collectives, reduce(): lax.all_to_all(pair.reshape(planes, -1, 128), PLANE, 0, 0, tiled=True)  16.9 us
    all_to_all x1, blocking collectives, reduce(): tiles = lax.all_to_all(copies, COLUMN, 0, 0, tiled=True)  12 us
    all_to_all x1, blocking collectives, reduce(): tiles = lax.all_to_all(copies, PLANE, 0, 0, tiled=True)  10.2 us
    pallas_call x4, Pallas kernels, call(): pl.pallas_call(body, out_shape=out_shape, in_specs=in_specs or [VMEM] * l...  8.58 us
    ppermute x1, starting transfers between devices, layer(): far = lax.ppermute(far, (*DOM, 'x'), far_pairs)  3.1 us
    ppermute x1, waiting for transfers between devices, layer(): arrived = lax.ppermute(send, 'c', [(0, 1), (1, 0)])  1.26 us
  transfers between devices with their start and end apart: 5, of which 2 were waited for; matrix products, arithmetic and copies ran while one was open for 0% of the time, Pallas kernels for 4%

profile of v9, /device:TPU:1, one launch (start us, length us, event | category | flops | bytes accessed | tf_op | source)
XLA Modules:
  0.0 56.6 jit_solution(17472259696630107841)
XLA Ops:
  0.6 1.2 %shard_map.227 = (bf16[128,128]{1,0:T(8,128)(2,1)S(1)}, bf16[128,128]{1,0:T(8,128)(2,1)S(1)}, bf16[512,128]{1,0:T(8,128)(2,1)S(1)}, s32[4,128]{1,0:T(4,128)S(1)}, s32[4,128]{1,0:T(4,128)S(1)}) custom-call(s32[2,128]{1,0:T(2,128)} %bitcast.23, bf16[512,128]{1,0:T(8,128)(2,1)} %bitcast.28, s32[4,128]{1,0:T(4,128)} %bitcast.29, s32[4,128]{1,0:T(4,128)} %bitcast.30), custom_call_target="tpu_custom_call" | custom-call | flops 1000000 | bytes 1000000 | tf_op jit(solution)/shard_map/pallas_call | solution.py:271
  1.9 3.1 %collective-permute-start.3 = (bf16[128,128]{1,0:T(8,128)(2,1)S(1)}, bf16[128,128]{1,0:T(8,128)(2,1)S(1)}, u32[]{:S(2)}, u32[]{:S(2)}) collective-permute-start(bf16[128,128]{1,0:T(8,128)(2,1)S(1)} %get-tuple-element.58), channel_id=1, source_target_pairs={{0,1},{1,0},{2,3},{3,2},{252,253},{253,252},{254,255},{255,254},{4... | collective-permute-start | bytes 98312 | tf_op jit(solution)/shard_map/ppermute | solution.py:350
  5.0 0.3 collective-permute-start.2
  5.9 2.1 %shard_map.228 = (bf16[512,128]{1,0:T(8,128)(2,1)S(1)}, bf16[384,128]{1,0:T(8,128)(2,1)S(1)}, f32[1,128]{1,0:T(1,128)S(1)}, bf16[128,128]{1,0:T(8,128)(2,1)S(1)}...) custom-call(bf16[512,128]{1,0:T(8,128)(2,1)S(1)} %get-tuple-element., ...), custom_call_target="tpu_custom_call" | custom-call | flops 400000000 | bytes 1000000 | tf_op jit(solution)/shard_map/pallas_call | solution.py:271
  8.0 0.0 collective-permute-done.3.far
  8.0 0.0 collective-permute-done.2.near
  8.0 4.2 %shard_map.229 = (bf16[512,128]{1,0:T(8,128)(2,1)}, bf16[512,128]{1,0:T(8,128)(2,1)}, bf16[512,128]{1,0:T(8,128)(2,1)}, f32[512,128]{1,0:T(8,128)S(1)}, f32[1024...) custom-call(bf16[128,128]{1,0:T(8,128)(2,1)S(1)} %collective-permute-done.2.near, ...), custom_call_target="tpu_custom_call" | custom-call | flops 2000000000 | bytes 1000000 | tf_op jit(solution)/shard_map/pallas_call | solution.py:271
  12.2 1.1 %collective-permute-start.4 = (bf16[1280,128]{1,0:T(8,128)(2,1)S(1)}, bf16[1280,128]{1,0:T(8,128)(2,1)S(1)}, u32[]{:S(2)}, u32[]{:S(2)}) collective-permute-start(bf16[1280,128]{1,0:T(8,128)(2,1)S(1)} %get-tuple-element.88), channel_id=1, source_target_pairs={{0,4},{4,0},{1,5},{5,1},{2,6},{6,2},{3,7},{7,3},{8,12},{12,8},{9,1... | collective-permute-start | bytes 983048 | tf_op jit(solution)/shard_map/ppermute | solution.py:364
  13.4 1.3 %collective-permute-done.4 = bf16[1280,128]{1,0:T(8,128)(2,1)S(1)} collective-permute-done((bf16[1280,128]{1,0:T(8,128)(2,1)S(1)}, bf16[1280,128]{1,0:T(8,128)(2,1)S(1)}, u32[]{:S(2)}, u32[]{:S(2)}) %collective-permute-start.4) | collective-permute-done | bytes 327712 | tf_op jit(solution)/shard_map/ppermute | solution.py:364
  14.6 0.1 add_convert_fusion
  14.7 39.3 %conditional.1 = (bf16[1024,128]{1,0:T(8,128)(2,1)S(1)}, bf16[256,128]{1,0:T(8,128)(2,1)S(1)}) conditional(s32[]{:T(128)} %convert_element_type.24, bf16[1024,128]{1,0:T(8,128)(2,1)S(1)} %add_convert_fusion, (bf16[1280,128]{1,0:T(8,128)(2,1)S(1)}, bf16[1280,128]{1,0:T(8,128)(2,1)S(1)}, bf16[1024,128]{1,0:T(8,128)(2,1)S(1)}) %tuple.18), branch_computations={%region_0.3_spmd, %region_3.4_spmd} | conditional | flops 409600 | bytes 2424848 | solution.py:383
  14.7 16.9 %all_to_all.12 = bf16[16,64,128]{2,1,0:T(8,128)(2,1)S(1)} all-to-all(bf16[16,64,128]{2,1,0:T(8,128)(2,1)S(1)} %bitcast.25), channel_id=1, replica_groups=mesh['y'=4,'z'=8,'c'=2,'x'=4] {'y','x'}, dimensions={0} | all-to-all | bytes 524288 | tf_op jit(solution)/shard_map/cond/branch_0_fun/all_to_all | solution.py:373
  31.7 12.0 %all_to_all.13 = bf16[8,64,128]{2,1,0:T(8,128)(2,1)S(1)} all-to-all(bf16[8,64,128]{2,1,0:T(8,128)(2,1)S(1)} %broadcast_in_dim.8), channel_id=1, replica_groups=mesh['y'=4,'z'=8,'c'=2,'x'=4] {'z'}, dimensions={0} | all-to-all | bytes 262144 | tf_op jit(solution)/shard_map/cond/branch_0_fun/all_to_all | solution.py:376
  43.8 10.2 %all_to_all.14 = bf16[16,64,128]{2,1,0:T(8,128)(2,1)S(1)} all-to-all(bf16[16,64,128]{2,1,0:T(8,128)(2,1)S(1)} %broadcast_in_dim.9), channel_id=1, replica_groups=mesh['y'=4,'z'=8,'c'=2,'x'=4] {'y','x'}, dimensions={0} | all-to-all | bytes 524288 | tf_op jit(solution)/shard_map/cond/branch_0_fun/all_to_all | solution.py:379
  54.0 0.0 collective-permute-start.6
  54.0 0.5 collective-permute-start.5
  54.5 0.0 copy-start
  54.5 1.1 %collective-permute-done.5.downward = bf16[128,128]{1,0:T(8,128)(2,1)S(1)} collective-permute-done((bf16[128,128]{1,0:T(8,128)(2,1)S(1)}, bf16[128,128]{1,0:T(8,128)(2,1)S(1)}, u32[]{:S(2)}, u32[]{:S(2)}) %collective-permute-start.5) | collective-permute-done | bytes 32800 | tf_op jit(solution)/shard_map/ppermute | solution.py:387
  55.6 0.0 collective-permute-done.6.received
  55.6 0.0 copy-done
  55.6 1.1 %shard_map.230 = (bf16[512,128]{1,0:T(8,128)(2,1)}, f32[904,128]{1,0:T(8,128)}) custom-call(f32[512,128]{1,0:T(8,128)S(1)} %get-tuple-element.87.local_grad, bf16[128,128]{1,0:T(8,128)(2,1)S(1)} %slice.27.near, bf16[256,128]{1,0:T(8,128)(2,1)S(1)} %get-tuple-element.90.turned, bf16[128,128]{1,0:T(8,128)(2,1)S(1)} %collective-permute-done.5.downward, ...), custom_call_target="tpu_custom_call" | custom-call | flops 1000000 | bytes 1000000 | tf_op jit(solution)/shard_map/pallas_call | solution.py:271
  (10 shorter events, 0.2 us)
Async XLA Ops:
  1.9 6.1 %collective-permute-start.3 = (bf16[128,128]{1,0:T(8,128)(2,1)S(1)}, bf16[128,128]{1,0:T(8,128)(2,1)S(1)}, u32[]{:S(2)}, u32[]{:S(2)}) collective-permute-start(bf16[128,128]{1,0:T(8,128)(2,1)S(1)} %get-tuple-element.58), channel_id=1, source_target_pairs={{0,1},{1,0},{2,3},{3,2},{252,253},{253,252},{254,255},{255,254},{4... | collective-permute-start | bytes 98312 | tf_op jit(solution)/shard_map/ppermute | solution.py:350
  5.0 3.0 %collective-permute-start.2 = (bf16[128,128]{1,0:T(8,128)(2,1)S(1)}, bf16[128,128]{1,0:T(8,128)(2,1)S(1)}, u32[]{:S(2)}, u32[]{:S(2)}) collective-permute-start(bf16[128,128]{1,0:T(8,128)(2,1)S(1)} %get-tuple-element.56), channel_id=1, source_target_pairs={{0,4},{4,0},{8,12},{12,8},{16,20},{20,16},{24,28},{28,24},{32,36},... | collective-permute-start | bytes 98312 | tf_op jit(solution)/shard_map/ppermute | solution.py:351
  12.2 2.4 %collective-permute-start.4 = (bf16[1280,128]{1,0:T(8,128)(2,1)S(1)}, bf16[1280,128]{1,0:T(8,128)(2,1)S(1)}, u32[]{:S(2)}, u32[]{:S(2)}) collective-permute-start(bf16[1280,128]{1,0:T(8,128)(2,1)S(1)} %get-tuple-element.88), channel_id=1, source_target_pairs={{0,4},{4,0},{1,5},{5,1},{2,6},{6,2},{3,7},{7,3},{8,12},{12,8},{9,1... | collective-permute-start | bytes 983048 | tf_op jit(solution)/shard_map/ppermute | solution.py:364
  54.0 1.6 %collective-permute-start.6 = (bf16[1024,128]{1,0:T(8,128)(2,1)S(1)}, bf16[1024,128]{1,0:T(8,128)(2,1)S(1)}, u32[]{:S(2)}, u32[]{:S(2)}) collective-permute-start(bf16[1024,128]{1,0:T(8,128)(2,1)S(1)} %get-tuple-element.91.result), channel_id=1, source_target_pairs={{0,4},{4,0},{1,5},{5,1},{2,6},{6,2},{3,7},{7,3},{8,12},{12,8},{9,1... | collective-permute-start | bytes 786440 | tf_op jit(solution)/shard_map/ppermute | solution.py:386
  54.0 1.6 %collective-permute-start.5 = (bf16[128,128]{1,0:T(8,128)(2,1)S(1)}, bf16[128,128]{1,0:T(8,128)(2,1)S(1)}, u32[]{:S(2)}, u32[]{:S(2)}) collective-permute-start(bf16[128,128]{1,0:T(8,128)(2,1)S(1)} %slice.25), channel_id=1, source_target_pairs={{0,4},{4,0},{1,5},{5,1},{2,6},{6,2},{3,7},{7,3},{8,12},{12,8},{9,1... | collective-permute-start | bytes 98312 | tf_op jit(solution)/shard_map/ppermute | solution.py:387
  54.5 1.1 %copy-start = (s32[1,1,2,128]{3,2,1,0:T(2,128)S(1)}, s32[1,1,2,128]{3,2,1,0:T(2,128)}, u32[]{:S(2)}) copy-start(s32[1,1,2,128]{3,2,1,0:T(2,128)} %param.27) | copy-start | bytes 3076

commit v10 on v9

--- a/solution.py
+++ b/solution.py
@@ -106,60 +106,62 @@
 
 
 def prepare_kernel(nodes, senders, receivers, count, *refs):
-    sources, landed, (receiver, partial, live, pick_send, pick_recv, place_recv, place_send), (arrive,) = (
-        refs[:15], refs[15:30], refs[30:37], refs[37:],
-    )
+    (
+        sources, landed,
+        (sender, receiver, partial, node_partial, live, pick_halo, pick_recv, place_recv, place_send),
+        (pick_own, arrive),
+    ) = refs[:15], refs[15:30], refs[30:39], refs[39:]
     loads = [pltpu.make_async_copy(a, b, arrive.at[k]) for k, (a, b) in enumerate(zip(sources, landed))]
     for load in loads:
         load.start()
-    edges, ew1, eb1 = landed[:3]
+    edges, ew1, eb1, _, _, _, _, nw1, nb1 = landed[:9]
     line = lax.broadcasted_iota(jnp.int32, (512, 128), 0)
     live[...] = jnp.where(line < count[0:1, 0:1] * 128, 1.0, 0.0).astype(F32)
     for b in range(4):
         rows = pl.ds(b * 128, 128)
         send_row, recv_row = senders[pl.ds(b, 1), :], receivers[pl.ds(b, 1), :]
-        pick_send[rows, :] = pick_rows(send_row, 768)
+        picked = pick_rows(send_row, 768)
+        pick_own[rows, :] = picked[:, 0:512]
+        pick_halo[rows, :] = picked[:, 512:768]
         pick_recv[rows, :] = pick_rows(recv_row, 512)
         place_recv[:, rows] = place_rows(recv_row, 512)
         place_send[:, rows] = place_rows(send_row, 768)
+    sent = dot(pick_own[...], nodes[...]).astype(BF16)
+    sender[...] = sent
+    low = dot(pick_recv[...], nodes[...]).astype(BF16)
+    receiver[...] = low
     for load in loads:
         load.wait()
-    low = dot(pick_recv[...], nodes[...]).astype(BF16)
-    receiver[...] = low
-    partial[...] = dot(jnp.concatenate([edges[...], low], axis=1), around(ew1)) + eb1[...]
-
-
-def around(weight):
-    return jnp.concatenate([weight[0:128, :], weight[256:384, :]], axis=0)
+    partial[...] = dot(jnp.concatenate([edges[...], sent, low], axis=1), ew1[...]) + eb1[...]
+    node_partial[...] = dot(nodes[...], nw1[0:128, :]) + nb1[...]
 
 
 def main_kernel(near, far, nodes, *refs):
     (
         (edges, ew1, _, ew2, eb2, egain, eshift, nw1, nb1, nw2, nb2, ngain, nshift, node_cot, edge_cot),
-        (receiver, partial, live, pick_send, pick_recv, place_recv, place_send),
+        (own_sender, receiver, partial, node_partial, live, pick_halo, pick_recv, place_recv, place_send),
         (node_out, edge_out, grad_edge, local_grad, keep, send),
         left,
         (
-            table, messages, hidden, slope, normed, inverse, spread, dxs, dxr, sender, first_low, second_low,
-            node_inputs, node_hidden, node_first, node_second, leave,
+            halo, messages, hidden, slope, normed, inverse, spread, dxs, dxr, sender, first_low, second_low,
+            aggregated, node_hidden, node_first, node_second, leave,
         ),
-    ) = refs[:15], refs[15:22], refs[22:28], refs[28:31], refs[31:]
+    ) = refs[:15], refs[15:24], refs[24:30], refs[30:33], refs[33:]
     stores = [
         pltpu.make_async_copy(a, b, leave.at[k])
         for k, (a, b) in enumerate(zip(left, (edge_out, node_out, grad_edge)))
     ]
     edge_left, node_left, grad_left = left
     core = lax.axis_index("c")
-    table[pl.ds(0, 512), :] = nodes[...]
-    table[pl.ds(pl.multiple_of(640 - 128 * core, 128), 128), :] = near[...]
+    halo[pl.ds(pl.multiple_of(128 - 128 * core, 128), 128), :] = near[...]
     place = lax.axis_index("y") * lax.axis_size("z") + lax.axis_index("z")
     last = lax.axis_size("y") * lax.axis_size("z") - 1
     alone = place == core * last
-    table[pl.ds(pl.multiple_of(512 + 128 * core, 128), 128), :] = jnp.where(alone, 0.0, far[...].astype(F32)).astype(BF16)
+    halo[pl.ds(pl.multiple_of(128 * core, 128), 128), :] = jnp.where(alone, 0.0, far[...].astype(F32)).astype(BF16)
 
     own = edges[...]
-    low = dot(pick_send[...], table[...]).astype(BF16)
-    sender[...] = low
+    low = dot(pick_halo[...], halo[...]).astype(BF16)
+    sender[...] = own_sender[...] + low
     first = partial[...] + dot(low, ew1[128:256, :])
     sigmoid = jax.nn.sigmoid(first)
     low = (first * sigmoid).astype(BF16)
@@ -176,9 +178,8 @@
     sums = [jnp.zeros((8, 128), F32) for _ in range(8)]
     aggregate = joined(dot(place_recv[...], messages[...])).astype(BF16)
     own = nodes[...]
-    gathered = jnp.concatenate([own, aggregate], axis=1)
-    node_inputs[...] = gathered
-    first = dot(gathered, nw1[...]) + nb1[...]
+    aggregated[...] = aggregate
+    first = node_partial[...] + dot(aggregate, nw1[128:256, :])
     sigmoid = jax.nn.sigmoid(first)
     low = (first * sigmoid).astype(BF16)
     node_hidden[...] = low
@@ -229,7 +230,8 @@
     keep[513:514, :] = total(sums[1])
     keep[514:515, :] = total(sums[2])
     keep[515:516, :] = total(sums[3])
-    keep[516:772, :] = dot_tn(node_inputs[...], node_first[...])
+    keep[516:644, :] = dot_tn(nodes[...], node_first[...])
+    keep[644:772, :] = dot_tn(aggregated[...], node_first[...])
     keep[772:773, :] = total(sums[4])
     keep[773:901, :] = dot_tn(node_hidden[...], node_second[...])
     keep[901:902, :] = total(sums[5])
@@ -289,12 +291,13 @@
 
 def prepare(early, sources):
     outs = tuple(jax.ShapeDtypeStruct(source.shape, source.dtype) for source in sources) + (
-        shape(512, 128, BF16), shape(512, 128, F32), shape(512, 128, F32), shape(512, 768, BF16),
-        shape(512, 512, BF16), shape(512, 512, BF16), shape(768, 512, BF16),
+        shape(512, 128, BF16), shape(512, 128, BF16), shape(512, 128, F32), shape(512, 128, F32),
+        shape(512, 128, F32), shape(512, 256, BF16), shape(512, 512, BF16), shape(512, 512, BF16),
+        shape(768, 512, BF16),
     )
     return call(
         prepare_kernel, outs, (*early, *(in_hbm(source) for source in sources)),
-        [VMEM] * 4 + [HBM] * 15, scratch=[pltpu.SemaphoreType.DMA((15,))], flops=400000000, vmem=16 << 20,
+        [VMEM] * 4 + [HBM] * 15, scratch=[pltpu.VMEM((512, 512), BF16), pltpu.SemaphoreType.DMA((15,))], flops=400000000, vmem=16 << 20,
     )
 
 
@@ -307,14 +310,14 @@
         pltpu.VMEM(dims, kind)
         for dims, kind in (
             ((512, 128), BF16), ((512, 128), BF16), ((512, 128), BF16),
-            ((768, 128), BF16), ((512, 256), BF16), ((512, 128), BF16), ((512, 128), F32),
+            ((256, 128), BF16), ((512, 256), BF16), ((512, 128), BF16), ((512, 128), F32),
             ((512, 128), F32), ((512, 1), F32), ((512, 256), BF16), ((512, 256), BF16), ((512, 256), BF16),
-            ((512, 128), BF16), ((512, 128), BF16), ((512, 128), BF16), ((512, 256), BF16), ((512, 128), BF16),
+            ((512, 128), BF16), ((512, 128), BF16), ((512, 128), BF16), ((512, 128), BF16), ((512, 128), BF16),
             ((512, 128), BF16), ((512, 128), BF16),
         )
     ] + [pltpu.SemaphoreType.DMA((3,))]
     return call(
-        main_kernel, outs, (near, far, nodes, *prepared), [VMEM] * 25,
+        main_kernel, outs, (near, far, nodes, *prepared), [VMEM] * 27,
         (HBM,) * 3 + (VMEM,) * 3, scratch, 2000000000, 24 << 20,
     )
 

time: 56.9 us -> 56.5 us (level)
  no operation moved by 1% of the time
where the time goes in v10:
time: 56.5 us; the launch traced here: 56.3 us
  blocking collectives  39.1 us (69%)
  Pallas kernels  8.28 us (15%)
  starting transfers between devices  4.96 us (9%)
  waiting for transfers between devices  2.33 us (4%)
  between operations  1.35 us (2%)
    all_to_all x1, blocking collectives, reduce(): lax.all_to_all(pair.reshape(planes, -1, 128), PLANE, 0, 0, tiled=True)  17 us
    all_to_all x1, blocking collectives, reduce(): tiles = lax.all_to_all(copies, COLUMN, 0, 0, tiled=True)  12 us
    all_to_all x1, blocking collectives, reduce(): tiles = lax.all_to_all(copies, PLANE, 0, 0, tiled=True)  10.2 us
    pallas_call x4, Pallas kernels, call(): pl.pallas_call(body, out_shape=out_shape, in_specs=in_specs or [VMEM] * l...  8.28 us
    ppermute x1, starting transfers between devices, layer(): far = lax.ppermute(far, (*DOM, 'x'), far_pairs)  3.1 us
    ppermute x1, waiting for transfers between devices, layer(): arrived = lax.ppermute(send, 'c', [(0, 1), (1, 0)])  1.26 us
  transfers between devices with their start and end apart: 5, of which 2 were waited for; matrix products, arithmetic and copies ran while one was open for 0% of the time, Pallas kernels for 4%

profile of v10, /device:TPU:1, one launch (start us, length us, event | category | flops | bytes accessed | tf_op | source)
XLA Modules:
  0.0 56.3 jit_solution(15150296225845148379)
XLA Ops:
  0.6 1.2 %shard_map.227 = (bf16[128,128]{1,0:T(8,128)(2,1)S(1)}, bf16[128,128]{1,0:T(8,128)(2,1)S(1)}, bf16[512,128]{1,0:T(8,128)(2,1)S(1)}, s32[4,128]{1,0:T(4,128)S(1)}, s32[4,128]{1,0:T(4,128)S(1)}) custom-call(s32[2,128]{1,0:T(2,128)} %bitcast.23, bf16[512,128]{1,0:T(8,128)(2,1)} %bitcast.28, s32[4,128]{1,0:T(4,128)} %bitcast.29, s32[4,128]{1,0:T(4,128)} %bitcast.30), custom_call_target="tpu_custom_call" | custom-call | flops 1000000 | bytes 1000000 | tf_op jit(solution)/shard_map/pallas_call | solution.py:273
  1.9 3.1 %collective-permute-start.3 = (bf16[128,128]{1,0:T(8,128)(2,1)S(1)}, bf16[128,128]{1,0:T(8,128)(2,1)S(1)}, u32[]{:S(2)}, u32[]{:S(2)}) collective-permute-start(bf16[128,128]{1,0:T(8,128)(2,1)S(1)} %get-tuple-element.60), channel_id=1, source_target_pairs={{0,1},{1,0},{2,3},{3,2},{252,253},{253,252},{254,255},{255,254},{4... | collective-permute-start | bytes 98312 | tf_op jit(solution)/shard_map/ppermute | solution.py:353
  5.0 0.3 collective-permute-start.2
  5.9 2.1 %shard_map.228 = (bf16[512,128]{1,0:T(8,128)(2,1)S(1)}, bf16[384,128]{1,0:T(8,128)(2,1)S(1)}, f32[1,128]{1,0:T(1,128)S(1)}, bf16[128,128]{1,0:T(8,128)(2,1)S(1)}...) custom-call(bf16[512,128]{1,0:T(8,128)(2,1)S(1)} %get-tuple-element., ...), custom_call_target="tpu_custom_call" | custom-call | flops 400000000 | bytes 1000000 | tf_op jit(solution)/shard_map/pallas_call | solution.py:273
  8.1 0.0 collective-permute-done.3.far
  8.1 0.0 collective-permute-done.2.near
  8.1 3.8 %shard_map.229 = (bf16[512,128]{1,0:T(8,128)(2,1)}, bf16[512,128]{1,0:T(8,128)(2,1)}, bf16[512,128]{1,0:T(8,128)(2,1)}, f32[512,128]{1,0:T(8,128)S(1)}, f32[1024...) custom-call(bf16[128,128]{1,0:T(8,128)(2,1)S(1)} %collective-permute-done.2.near, ...), custom_call_target="tpu_custom_call" | custom-call | flops 2000000000 | bytes 1000000 | tf_op jit(solution)/shard_map/pallas_call | solution.py:273
  11.9 1.1 %collective-permute-start.4 = (bf16[1280,128]{1,0:T(8,128)(2,1)S(1)}, bf16[1280,128]{1,0:T(8,128)(2,1)S(1)}, u32[]{:S(2)}, u32[]{:S(2)}) collective-permute-start(bf16[1280,128]{1,0:T(8,128)(2,1)S(1)} %get-tuple-element.92), channel_id=1, source_target_pairs={{0,4},{4,0},{1,5},{5,1},{2,6},{6,2},{3,7},{7,3},{8,12},{12,8},{9,1... | collective-permute-start | bytes 983048 | tf_op jit(solution)/shard_map/ppermute | solution.py:367
  13.0 1.3 %collective-permute-done.4 = bf16[1280,128]{1,0:T(8,128)(2,1)S(1)} collective-permute-done((bf16[1280,128]{1,0:T(8,128)(2,1)S(1)}, bf16[1280,128]{1,0:T(8,128)(2,1)S(1)}, u32[]{:S(2)}, u32[]{:S(2)}) %collective-permute-start.4) | collective-permute-done | bytes 327712 | tf_op jit(solution)/shard_map/ppermute | solution.py:367
  14.3 0.1 add_convert_fusion
  14.3 39.3 %conditional.1 = (bf16[1024,128]{1,0:T(8,128)(2,1)S(1)}, bf16[256,128]{1,0:T(8,128)(2,1)S(1)}) conditional(s32[]{:T(128)} %convert_element_type.24, bf16[1024,128]{1,0:T(8,128)(2,1)S(1)} %add_convert_fusion, (bf16[1280,128]{1,0:T(8,128)(2,1)S(1)}, bf16[1280,128]{1,0:T(8,128)(2,1)S(1)}, bf16[1024,128]{1,0:T(8,128)(2,1)S(1)}) %tuple.18), branch_computations={%region_0.3_spmd, %region_3.4_spmd} | conditional | flops 409600 | bytes 2424848 | solution.py:386
  14.3 17.0 %all_to_all.12 = bf16[16,64,128]{2,1,0:T(8,128)(2,1)S(1)} all-to-all(bf16[16,64,128]{2,1,0:T(8,128)(2,1)S(1)} %bitcast.25), channel_id=1, replica_groups=mesh['y'=4,'z'=8,'c'=2,'x'=4] {'y','x'}, dimensions={0} | all-to-all | bytes 524288 | tf_op jit(solution)/shard_map/cond/branch_0_fun/all_to_all | solution.py:376
  31.4 12.0 %all_to_all.13 = bf16[8,64,128]{2,1,0:T(8,128)(2,1)S(1)} all-to-all(bf16[8,64,128]{2,1,0:T(8,128)(2,1)S(1)} %broadcast_in_dim.8), channel_id=1, replica_groups=mesh['y'=4,'z'=8,'c'=2,'x'=4] {'z'}, dimensions={0} | all-to-all | bytes 262144 | tf_op jit(solution)/shard_map/cond/branch_0_fun/all_to_all | solution.py:379
  43.4 10.2 %all_to_all.14 = bf16[16,64,128]{2,1,0:T(8,128)(2,1)S(1)} all-to-all(bf16[16,64,128]{2,1,0:T(8,128)(2,1)S(1)} %broadcast_in_dim.9), channel_id=1, replica_groups=mesh['y'=4,'z'=8,'c'=2,'x'=4] {'y','x'}, dimensions={0} | all-to-all | bytes 524288 | tf_op jit(solution)/shard_map/cond/branch_0_fun/all_to_all | solution.py:382
  53.6 0.0 collective-permute-start.6
  53.6 0.5 collective-permute-start.5
  54.1 0.0 copy-start
  54.1 1.1 %collective-permute-done.5.downward = bf16[128,128]{1,0:T(8,128)(2,1)S(1)} collective-permute-done((bf16[128,128]{1,0:T(8,128)(2,1)S(1)}, bf16[128,128]{1,0:T(8,128)(2,1)S(1)}, u32[]{:S(2)}, u32[]{:S(2)}) %collective-permute-start.5) | collective-permute-done | bytes 32800 | tf_op jit(solution)/shard_map/ppermute | solution.py:390
  55.2 0.0 collective-permute-done.6.received
  55.2 0.0 copy-done
  55.2 1.1 %shard_map.230 = (bf16[512,128]{1,0:T(8,128)(2,1)}, f32[904,128]{1,0:T(8,128)}) custom-call(f32[512,128]{1,0:T(8,128)S(1)} %get-tuple-element.91.local_grad, bf16[128,128]{1,0:T(8,128)(2,1)S(1)} %slice.27.near, bf16[256,128]{1,0:T(8,128)(2,1)S(1)} %get-tuple-element.94.turned, bf16[128,128]{1,0:T(8,128)(2,1)S(1)} %collective-permute-done.5.downward, ...), custom_call_target="tpu_custom_call" | custom-call | flops 1000000 | bytes 1000000 | tf_op jit(solution)/shard_map/pallas_call | solution.py:273
  (10 shorter events, 0.2 us)
Async XLA Ops:
  1.9 6.2 %collective-permute-start.3 = (bf16[128,128]{1,0:T(8,128)(2,1)S(1)}, bf16[128,128]{1,0:T(8,128)(2,1)S(1)}, u32[]{:S(2)}, u32[]{:S(2)}) collective-permute-start(bf16[128,128]{1,0:T(8,128)(2,1)S(1)} %get-tuple-element.60), channel_id=1, source_target_pairs={{0,1},{1,0},{2,3},{3,2},{252,253},{253,252},{254,255},{255,254},{4... | collective-permute-start | bytes 98312 | tf_op jit(solution)/shard_map/ppermute | solution.py:353
  5.0 3.1 %collective-permute-start.2 = (bf16[128,128]{1,0:T(8,128)(2,1)S(1)}, bf16[128,128]{1,0:T(8,128)(2,1)S(1)}, u32[]{:S(2)}, u32[]{:S(2)}) collective-permute-start(bf16[128,128]{1,0:T(8,128)(2,1)S(1)} %get-tuple-element.58), channel_id=1, source_target_pairs={{0,4},{4,0},{8,12},{12,8},{16,20},{20,16},{24,28},{28,24},{32,36},... | collective-permute-start | bytes 98312 | tf_op jit(solution)/shard_map/ppermute | solution.py:354
  11.9 2.3 %collective-permute-start.4 = (bf16[1280,128]{1,0:T(8,128)(2,1)S(1)}, bf16[1280,128]{1,0:T(8,128)(2,1)S(1)}, u32[]{:S(2)}, u32[]{:S(2)}) collective-permute-start(bf16[1280,128]{1,0:T(8,128)(2,1)S(1)} %get-tuple-element.92), channel_id=1, source_target_pairs={{0,4},{4,0},{1,5},{5,1},{2,6},{6,2},{3,7},{7,3},{8,12},{12,8},{9,1... | collective-permute-start | bytes 983048 | tf_op jit(solution)/shard_map/ppermute | solution.py:367
  53.6 1.6 %collective-permute-start.6 = (bf16[1024,128]{1,0:T(8,128)(2,1)S(1)}, bf16[1024,128]{1,0:T(8,128)(2,1)S(1)}, u32[]{:S(2)}, u32[]{:S(2)}) collective-permute-start(bf16[1024,128]{1,0:T(8,128)(2,1)S(1)} %get-tuple-element.95.result), channel_id=1, source_target_pairs={{0,4},{4,0},{1,5},{5,1},{2,6},{6,2},{3,7},{7,3},{8,12},{12,8},{9,1... | collective-permute-start | bytes 786440 | tf_op jit(solution)/shard_map/ppermute | solution.py:389
  53.6 1.6 %collective-permute-start.5 = (bf16[128,128]{1,0:T(8,128)(2,1)S(1)}, bf16[128,128]{1,0:T(8,128)(2,1)S(1)}, u32[]{:S(2)}, u32[]{:S(2)}) collective-permute-start(bf16[128,128]{1,0:T(8,128)(2,1)S(1)} %slice.25), channel_id=1, source_target_pairs={{0,4},{4,0},{1,5},{5,1},{2,6},{6,2},{3,7},{7,3},{8,12},{12,8},{9,1... | collective-permute-start | bytes 98312 | tf_op jit(solution)/shard_map/ppermute | solution.py:390
  54.1 1.1 %copy-start = (s32[1,1,2,128]{3,2,1,0:T(2,128)S(1)}, s32[1,1,2,128]{3,2,1,0:T(2,128)}, u32[]{:S(2)}) copy-start(s32[1,1,2,128]{3,2,1,0:T(2,128)} %param.27) | copy-start | bytes 3076

commit v11 on v10

--- a/solution.py
+++ b/solution.py
@@ -146,12 +146,12 @@
             halo, messages, hidden, slope, normed, inverse, spread, dxs, dxr, sender, first_low, second_low,
             aggregated, node_hidden, node_first, node_second, leave,
         ),
-    ) = refs[:15], refs[15:24], refs[24:30], refs[30:33], refs[33:]
+    ) = refs[:15], refs[15:24], refs[24:30], refs[30:32], refs[32:]
     stores = [
         pltpu.make_async_copy(a, b, leave.at[k])
-        for k, (a, b) in enumerate(zip(left, (edge_out, node_out, grad_edge)))
+        for k, (a, b) in enumerate(zip(left, (edge_out, node_out)))
     ]
-    edge_left, node_left, grad_left = left
+    edge_left, node_left = left
     core = lax.axis_index("c")
     halo[pl.ds(pl.multiple_of(128 - 128 * core, 128), 128), :] = near[...]
     place = lax.axis_index("y") * lax.axis_size("z") + lax.axis_index("z")
@@ -209,12 +209,11 @@
     first_low[...] = g1_low
     second_low[...] = g2_low
     back = dot_nt(g1_low, ew1[...])
-    grad_left[...] = (edge_grad + back[:, :128]).astype(BF16)
+    grad_edge[...] = (edge_grad + back[:, :128]).astype(BF16)
     dxs[...] = split(back[:, 128:256])
     dxr[...] = split(back[:, 256:])
     for k, piece in enumerate((g1, g2, cot * n, cot)):
         sums[k] += partial_sum(piece)
-    stores[2].start()
 
     lower = joined(dot(place_send[512:640, :], dxs[...])).astype(BF16)
     upper = joined(dot(place_send[640:768, :], dxs[...])).astype(BF16)
@@ -249,17 +248,20 @@
 
 
 def finish_kernel(
-    local_grad, near, turned, downward, result, received, lists, grad_node, weight_grads, node_left, weight_left, leave
+    local_grad, near, turned, downward, result, received, lists, edge_left,
+    grad_node, weight_grads, grad_edge, node_left, weight_left, leave,
 ):
     core = lax.axis_index("c")
     is_first = core == 0
     stores = [
         pltpu.make_async_copy(weight_left, weight_grads, leave.at[0]),
         pltpu.make_async_copy(node_left, grad_node, leave.at[1]),
+        pltpu.make_async_copy(edge_left, grad_edge, leave.at[2]),
     ]
     whole = jnp.where(is_first, received[0:LIVE_ROWS, :].astype(F32), result[0:LIVE_ROWS, :].astype(F32))
     weight_left[...] = whole
     stores[0].start()
+    stores[2].start()
     far = jnp.where(is_first, turned[0:128, :].astype(F32), downward[...].astype(F32)).astype(BF16)
     added = dot(place_rows(lists[pl.ds(1 - core, 1), :], 512), near[...])
     added += dot(place_rows(lists[pl.ds(core, 1), :], 512), far)
@@ -309,16 +311,16 @@
     scratch = [
         pltpu.VMEM(dims, kind)
         for dims, kind in (
-            ((512, 128), BF16), ((512, 128), BF16), ((512, 128), BF16),
+            ((512, 128), BF16), ((512, 128), BF16),
             ((256, 128), BF16), ((512, 256), BF16), ((512, 128), BF16), ((512, 128), F32),
             ((512, 128), F32), ((512, 1), F32), ((512, 256), BF16), ((512, 256), BF16), ((512, 256), BF16),
             ((512, 128), BF16), ((512, 128), BF16), ((512, 128), BF16), ((512, 128), BF16), ((512, 128), BF16),
             ((512, 128), BF16), ((512, 128), BF16),
         )
-    ] + [pltpu.SemaphoreType.DMA((3,))]
+    ] + [pltpu.SemaphoreType.DMA((2,))]
     return call(
         main_kernel, outs, (near, far, nodes, *prepared), [VMEM] * 27,
-        (HBM,) * 3 + (VMEM,) * 3, scratch, 2000000000, 24 << 20,
+        (HBM,) * 2 + (VMEM,) * 4, scratch, 2000000000, 24 << 20,
     )
 
 
@@ -388,11 +390,11 @@
     )
     received = lax.ppermute(result, "c", [(0, 1), (1, 0)])
     downward = lax.ppermute(turned[128:], "c", [(0, 1), (1, 0)])
-    grad_node, weight_grads = call(
-        finish_kernel, (shape(512, 128, BF16), shape(LIVE_ROWS, 128, F32)),
-        (local_grad, near_back, turned, downward, result, received, lists), [VMEM] * 7, (HBM,) * 2,
+    grad_node, weight_grads, grad_edge = call(
+        finish_kernel, (shape(512, 128, BF16), shape(LIVE_ROWS, 128, F32), shape(512, 128, BF16)),
+        (local_grad, near_back, turned, downward, result, received, lists, grad_edge), [VMEM] * 8, (HBM,) * 3,
         [
-            pltpu.VMEM((512, 128), BF16), pltpu.VMEM((LIVE_ROWS, 128), F32), pltpu.SemaphoreType.DMA((2,))
+            pltpu.VMEM((512, 128), BF16), pltpu.VMEM((LIVE_ROWS, 128), F32), pltpu.SemaphoreType.DMA((3,))
         ],
         vmem=SMALL,
     )

time: 56.5 us -> 57.2 us (1.012)
  local copies, waits for them, and re-layouts: 0.08 us -> 0.76 us
    unnamed x2, local copies, waits for them, and re-layouts: 0.01 us -> 0.68 us
where the time goes in v11:
time: 57.2 us; the launch traced here: 57 us
  blocking collectives  39.1 us (68%)
  Pallas kernels  8.28 us (14%)
  starting transfers between devices  4.96 us (9%)
  waiting for transfers between devices  2.33 us (4%)
  between operations  1.35 us (2%)
  local copies, waits for them, and re-layouts  0.76 us (1%)
    all_to_all x1, blocking collectives, reduce(): lax.all_to_all(pair.reshape(planes, -1, 128), PLANE, 0, 0, tiled=True)  17 us
    all_to_all x1, blocking collectives, reduce(): tiles = lax.all_to_all(copies, COLUMN, 0, 0, tiled=True)  12 us
    all_to_all x1, blocking collectives, reduce(): tiles = lax.all_to_all(copies, PLANE, 0, 0, tiled=True)  10.2 us
    pallas_call x4, Pallas kernels, call(): pl.pallas_call(body, out_shape=out_shape, in_specs=in_specs or [VMEM] * l...  8.28 us
    ppermute x1, starting transfers between devices, layer(): far = lax.ppermute(far, (*DOM, 'x'), far_pairs)  3.1 us
    ppermute x1, waiting for transfers between devices, layer(): arrived = lax.ppermute(send, 'c', [(0, 1), (1, 0)])  1.26 us
  transfers between devices with their start and end apart: 5, of which 2 were waited for; matrix products, arithmetic and copies ran while one was open for 0% of the time, Pallas kernels for 4%

profile of v11, /device:TPU:1, one launch (start us, length us, event | category | flops | bytes accessed | tf_op | source)
XLA Modules:
  0.0 57.0 jit_solution(1521980604785934355)
XLA Ops:
  0.6 1.2 %shard_map.227 = (bf16[128,128]{1,0:T(8,128)(2,1)S(1)}, bf16[128,128]{1,0:T(8,128)(2,1)S(1)}, bf16[512,128]{1,0:T(8,128)(2,1)S(1)}, s32[4,128]{1,0:T(4,128)S(1)}, s32[4,128]{1,0:T(4,128)S(1)}) custom-call(s32[2,128]{1,0:T(2,128)} %bitcast.23, bf16[512,128]{1,0:T(8,128)(2,1)} %bitcast.28, s32[4,128]{1,0:T(4,128)} %bitcast.29, s32[4,128]{1,0:T(4,128)} %bitcast.30), custom_call_target="tpu_custom_call" | custom-call | flops 1000000 | bytes 1000000 | tf_op jit(solution)/shard_map/pallas_call | solution.py:275
  1.9 3.1 %collective-permute-start.3 = (bf16[128,128]{1,0:T(8,128)(2,1)S(1)}, bf16[128,128]{1,0:T(8,128)(2,1)S(1)}, u32[]{:S(2)}, u32[]{:S(2)}) collective-permute-start(bf16[128,128]{1,0:T(8,128)(2,1)S(1)} %get-tuple-element.61), channel_id=1, source_target_pairs={{0,1},{1,0},{2,3},{3,2},{252,253},{253,252},{254,255},{255,254},{4... | collective-permute-start | bytes 98312 | tf_op jit(solution)/shard_map/ppermute | solution.py:355
  5.0 0.3 collective-permute-start.2
  5.9 2.1 %shard_map.228 = (bf16[512,128]{1,0:T(8,128)(2,1)S(1)}, bf16[384,128]{1,0:T(8,128)(2,1)S(1)}, f32[1,128]{1,0:T(1,128)S(1)}, bf16[128,128]{1,0:T(8,128)(2,1)S(1)}...) custom-call(bf16[512,128]{1,0:T(8,128)(2,1)S(1)} %get-tuple-element., ...), custom_call_target="tpu_custom_call" | custom-call | flops 400000000 | bytes 1000000 | tf_op jit(solution)/shard_map/pallas_call | solution.py:275
  8.1 0.0 collective-permute-done.3.far
  8.1 0.0 collective-permute-done.2.near
  8.1 3.8 %shard_map.229 = (bf16[512,128]{1,0:T(8,128)(2,1)}, bf16[512,128]{1,0:T(8,128)(2,1)}, bf16[512,128]{1,0:T(8,128)(2,1)S(1)}, f32[512,128]{1,0:T(8,128)S(1)}, f32[...) custom-call(bf16[128,128]{1,0:T(8,128)(2,1)S(1)} %collective-permute-done.2.near, ...), custom_call_target="tpu_custom_call" | custom-call | flops 2000000000 | bytes 1000000 | tf_op jit(solution)/shard_map/pallas_call | solution.py:275
  11.9 1.1 %collective-permute-start.4 = (bf16[1280,128]{1,0:T(8,128)(2,1)S(1)}, bf16[1280,128]{1,0:T(8,128)(2,1)S(1)}, u32[]{:S(2)}, u32[]{:S(2)}) collective-permute-start(bf16[1280,128]{1,0:T(8,128)(2,1)S(1)} %get-tuple-element.93), channel_id=1, source_target_pairs={{0,4},{4,0},{1,5},{5,1},{2,6},{6,2},{3,7},{7,3},{8,12},{12,8},{9,1... | collective-permute-start | bytes 983048 | tf_op jit(solution)/shard_map/ppermute | solution.py:369
  13.0 1.3 %collective-permute-done.4 = bf16[1280,128]{1,0:T(8,128)(2,1)S(1)} collective-permute-done((bf16[1280,128]{1,0:T(8,128)(2,1)S(1)}, bf16[1280,128]{1,0:T(8,128)(2,1)S(1)}, u32[]{:S(2)}, u32[]{:S(2)}) %collective-permute-start.4) | collective-permute-done | bytes 327712 | tf_op jit(solution)/shard_map/ppermute | solution.py:369
  14.2 0.1 add_convert_fusion
  14.3 39.3 %conditional.1 = (bf16[1024,128]{1,0:T(8,128)(2,1)S(1)}, bf16[256,128]{1,0:T(8,128)(2,1)S(1)}) conditional(s32[]{:T(128)} %convert_element_type.24, bf16[1024,128]{1,0:T(8,128)(2,1)S(1)} %add_convert_fusion, (bf16[1280,128]{1,0:T(8,128)(2,1)S(1)}, bf16[1280,128]{1,0:T(8,128)(2,1)S(1)}, bf16[1024,128]{1,0:T(8,128)(2,1)S(1)}) %tuple.18), branch_computations={%region_0.3_spmd, %region_3.4_spmd} | conditional | flops 409600 | bytes 2424848 | solution.py:388
  14.3 17.0 %all_to_all.12 = bf16[16,64,128]{2,1,0:T(8,128)(2,1)S(1)} all-to-all(bf16[16,64,128]{2,1,0:T(8,128)(2,1)S(1)} %bitcast.25), channel_id=1, replica_groups=mesh['y'=4,'z'=8,'c'=2,'x'=4] {'y','x'}, dimensions={0} | all-to-all | bytes 524288 | tf_op jit(solution)/shard_map/cond/branch_0_fun/all_to_all | solution.py:378
  31.3 12.0 %all_to_all.13 = bf16[8,64,128]{2,1,0:T(8,128)(2,1)S(1)} all-to-all(bf16[8,64,128]{2,1,0:T(8,128)(2,1)S(1)} %broadcast_in_dim.8), channel_id=1, replica_groups=mesh['y'=4,'z'=8,'c'=2,'x'=4] {'z'}, dimensions={0} | all-to-all | bytes 262144 | tf_op jit(solution)/shard_map/cond/branch_0_fun/all_to_all | solution.py:381
  43.4 10.2 %all_to_all.14 = bf16[16,64,128]{2,1,0:T(8,128)(2,1)S(1)} all-to-all(bf16[16,64,128]{2,1,0:T(8,128)(2,1)S(1)} %broadcast_in_dim.9), channel_id=1, replica_groups=mesh['y'=4,'z'=8,'c'=2,'x'=4] {'y','x'}, dimensions={0} | all-to-all | bytes 524288 | tf_op jit(solution)/shard_map/cond/branch_0_fun/all_to_all | solution.py:384
  53.6 0.0 collective-permute-start.6
  53.6 0.5 collective-permute-start.5
  54.1 1.1 %collective-permute-done.5.downward = bf16[128,128]{1,0:T(8,128)(2,1)S(1)} collective-permute-done((bf16[128,128]{1,0:T(8,128)(2,1)S(1)}, bf16[128,128]{1,0:T(8,128)(2,1)S(1)}, u32[]{:S(2)}, u32[]{:S(2)}) %collective-permute-start.5) | collective-permute-done | bytes 32800 | tf_op jit(solution)/shard_map/ppermute | solution.py:392
  55.1 0.0 collective-permute-done.6.received
  55.1 0.0 copy-start
  55.1 0.7 %copy-done = s32[1,1,2,128]{3,2,1,0:T(2,128)S(1)} copy-done((s32[1,1,2,128]{3,2,1,0:T(2,128)S(1)}, s32[1,1,2,128]{3,2,1,0:T(2,128)}, u32[]{:S(2)}) %copy-start) | copy-done | bytes 1048
  55.8 1.1 %shard_map.230 = (bf16[512,128]{1,0:T(8,128)(2,1)}, f32[904,128]{1,0:T(8,128)}, bf16[512,128]{1,0:T(8,128)(2,1)}) custom-call(f32[512,128]{1,0:T(8,128)S(1)} %get-tuple-element.92.local_grad, bf16[128,128]{1,0:T(8,128)(2,1)S(1)} %slice.27.near, bf16[256,128]{1,0:T(8,128)(2,1)S(1)} %get-tuple-element.95.turned, ...), custom_call_target="tpu_custom_call" | custom-call | flops 1000000 | bytes 1000000 | tf_op jit(solution)/shard_map/pallas_call | solution.py:275
  (10 shorter events, 0.2 us)
Async XLA Ops:
  1.9 6.2 %collective-permute-start.3 = (bf16[128,128]{1,0:T(8,128)(2,1)S(1)}, bf16[128,128]{1,0:T(8,128)(2,1)S(1)}, u32[]{:S(2)}, u32[]{:S(2)}) collective-permute-start(bf16[128,128]{1,0:T(8,128)(2,1)S(1)} %get-tuple-element.61), channel_id=1, source_target_pairs={{0,1},{1,0},{2,3},{3,2},{252,253},{253,252},{254,255},{255,254},{4... | collective-permute-start | bytes 98312 | tf_op jit(solution)/shard_map/ppermute | solution.py:355
  5.0 3.1 %collective-permute-start.2 = (bf16[128,128]{1,0:T(8,128)(2,1)S(1)}, bf16[128,128]{1,0:T(8,128)(2,1)S(1)}, u32[]{:S(2)}, u32[]{:S(2)}) collective-permute-start(bf16[128,128]{1,0:T(8,128)(2,1)S(1)} %get-tuple-element.59), channel_id=1, source_target_pairs={{0,4},{4,0},{8,12},{12,8},{16,20},{20,16},{24,28},{28,24},{32,36},... | collective-permute-start | bytes 98312 | tf_op jit(solution)/shard_map/ppermute | solution.py:356
  11.9 2.3 %collective-permute-start.4 = (bf16[1280,128]{1,0:T(8,128)(2,1)S(1)}, bf16[1280,128]{1,0:T(8,128)(2,1)S(1)}, u32[]{:S(2)}, u32[]{:S(2)}) collective-permute-start(bf16[1280,128]{1,0:T(8,128)(2,1)S(1)} %get-tuple-element.93), channel_id=1, source_target_pairs={{0,4},{4,0},{1,5},{5,1},{2,6},{6,2},{3,7},{7,3},{8,12},{12,8},{9,1... | collective-permute-start | bytes 983048 | tf_op jit(solution)/shard_map/ppermute | solution.py:369
  53.6 1.6 %collective-permute-start.6 = (bf16[1024,128]{1,0:T(8,128)(2,1)S(1)}, bf16[1024,128]{1,0:T(8,128)(2,1)S(1)}, u32[]{:S(2)}, u32[]{:S(2)}) collective-permute-start(bf16[1024,128]{1,0:T(8,128)(2,1)S(1)} %get-tuple-element.96.result), channel_id=1, source_target_pairs={{0,4},{4,0},{1,5},{5,1},{2,6},{6,2},{3,7},{7,3},{8,12},{12,8},{9,1... | collective-permute-start | bytes 786440 | tf_op jit(solution)/shard_map/ppermute | solution.py:391
  53.6 1.6 %collective-permute-start.5 = (bf16[128,128]{1,0:T(8,128)(2,1)S(1)}, bf16[128,128]{1,0:T(8,128)(2,1)S(1)}, u32[]{:S(2)}, u32[]{:S(2)}) collective-permute-start(bf16[128,128]{1,0:T(8,128)(2,1)S(1)} %slice.25), channel_id=1, source_target_pairs={{0,4},{4,0},{1,5},{5,1},{2,6},{6,2},{3,7},{7,3},{8,12},{12,8},{9,1... | collective-permute-start | bytes 98312 | tf_op jit(solution)/shard_map/ppermute | solution.py:392
  55.1 0.7 %copy-start = (s32[1,1,2,128]{3,2,1,0:T(2,128)S(1)}, s32[1,1,2,128]{3,2,1,0:T(2,128)}, u32[]{:S(2)}) copy-start(s32[1,1,2,128]{3,2,1,0:T(2,128)} %param.27) | copy-start | bytes 3076
